TPU v7x, 256 devices: a whole 4x4x8 slice. The times are simulated.
256 devices in a mesh: gx: 8 (over z), gz: 4 (over x), gy: 8 (over y, core).
Axes of the slice: x: 4, y: 4, z: 8, core: 2. Of those that a mesh axis runs over, the one named last changes fastest.
Arguments:
- row_embed: bfloat16 [131072, 128], P(('gx', 'gz')), may hold values from -24 to 24, as said below
- col_embed: bfloat16 [4096, 128], P('gy'), may hold values from -24 to 24, as said below
- row_mass: float32 [131072], P(('gx', 'gz')), may hold values from 1 to 10
- col_mass: float32 [4096], P('gy'), may hold values from 1 to 10
Outputs:
- row_potential: float32 [131072], P(('gx', 'gz'))
- col_potential: float32 [4096], P('gy')
- errors: float32 [10, 2], replicated
Inputs may be any that keep to these rules, and one draw needn't show every extreme that they name: `row_embed`: entries are real-valued embedding coordinates. `col_embed`: entries are real-valued embedding coordinates.
All inputs are finite; a program needn't handle non-finite values.
Results may differ from a plain program's by a relative error of at most 0.0003.
Values sent between devices are 32-bit elements; how exact they have to be, the bound alone decides.
No kernel may reach another device: no remote copies, remote signals or barrier semaphores. Data moves between devices by JAX's collectives and lax.ppermute only.
A program may use at most 64 MiB of HBM per device.

v0:
```python
import functools
import math

import jax
import jax.numpy as jnp
from jax import lax
from jax.sharding import Mesh
from jax.sharding import PartitionSpec as P

ITERS = 10
GY = ("gy_0", "gy_1")
GX_GZ_GY = ("gx", "gz", "gy_0", "gy_1")


eps = 0.05


def from_everyone(x, axis):
    copies = jnp.broadcast_to(x, (lax.axis_size(axis), *x.shape))
    return lax.all_to_all(copies, axis, split_axis=0, concat_axis=0, tiled=True)


def over_copies(x, axis):
    return from_everyone(x, axis).sum(axis=0)


def folded_in_pairs(pieces, combine):
    while len(jax.tree.leaves(pieces)[0]) > 1:
        pieces = jax.vmap(combine)(
            *(jax.tree.map(lambda part: part[side::2], pieces) for side in (0, 1))
        )
    return jax.tree.map(lambda part: part[0], pieces)


def joined_all(x, axis, combine):
    pieces = jax.tree.map(lambda part: from_everyone(part, axis), x)
    return folded_in_pairs(pieces, combine)


def collected_together(x, axis):
    leaves = jax.tree.leaves(x)
    turns = sorted(range(len(leaves)), key=lambda k: -leaves[k].size)
    width = (1, *leaves[turns[0]].shape)[-1]
    lines = [
        jnp.pad(leaves[k].reshape(-1), (0, -leaves[k].size % width)).reshape(-1, width)
        for k in turns
    ]
    both, at, found = (from_everyone(jnp.concatenate(lines), axis), 0, {})
    for k, line in zip(turns, lines):
        slab = both[:, at : at + len(line)].reshape(len(both), -1)
        found[k] = slab[:, : leaves[k].size].reshape(-1, *leaves[k].shape)
        at += len(line)
    numbers = iter(range(len(leaves)))
    return jax.tree.map(lambda _: found[next(numbers)], x)


def merged(x, axis, combine):
    pieces = collected_together(x, axis)
    return folded_in_pairs(pieces, combine)


def one_axis_at_a_time(x, axes):
    return functools.reduce(lax.psum, axes, x)


def combine(first, second):
    top = jnp.maximum(first[0], second[0])
    total = first[1] * jnp.exp(first[0] - top) + second[1] * jnp.exp(second[0] - top)
    return (top, total)


def cost_block(xb, col_embed, col_sq, width):
    cross = lax.dot_general(
        xb, col_embed, (((1,), (1,)), ((), ())), preferred_element_type=jnp.float32
    )
    xf = xb.astype(jnp.float32)
    row_sq = jnp.sum(xf * xf, axis=1)
    return (row_sq[:, None] + col_sq[None, :] - 2.0 * cross) / width


def on_device(row_embed, col_embed, row_mass, col_mass):
    rows, width = row_embed.shape
    cols = col_embed.shape[0]
    total_rows = over_copies(jnp.sum(row_mass), ("gx", "gz"))
    total_cols = over_copies(jnp.sum(col_mass), GY)
    mass_a = row_mass / total_rows
    mass_b = col_mass / total_cols
    log_a = jnp.log(mass_a)
    log_b = jnp.log(mass_b)
    yf = col_embed.astype(jnp.float32)
    col_sq = jnp.sum(yf * yf, axis=1)
    block = math.gcd(rows, 512)
    count = rows // block
    xblocks = row_embed.reshape(count, block, width)
    row_share = 1.0 / lax.axis_size(GY)
    col_share = 1.0 / (lax.axis_size("gx") * lax.axis_size("gz"))
    f_pot = jnp.zeros((rows,), jnp.float32)
    g_pot = jnp.zeros((cols,), jnp.float32)
    row_terms = []
    col_terms = []
    for index in range(ITERS):

        def one(xb):
            z = (g_pot[None, :] - cost_block(xb, col_embed, col_sq, width)) / eps
            top = jnp.max(z, axis=1)
            return (top, jnp.sum(jnp.exp(z - top[:, None]), axis=1))

        top, total = lax.map(one, xblocks)
        top, total = joined_all((top.reshape(rows), total.reshape(rows)), GY, combine)
        f_new = eps * (log_a - (top + jnp.log(total)))
        row_local = jnp.sum(jnp.abs(jnp.exp(log_a + (f_pot - f_new) / eps) - mass_a))
        f_pot = f_new
        fblocks = f_pot.reshape(count, block)

        def step(carry, item):
            top, total = carry
            xb, fb = item
            z = (fb[:, None] - cost_block(xb, col_embed, col_sq, width)) / eps
            newtop = jnp.maximum(top, jnp.max(z, axis=0))
            total = total * jnp.exp(top - newtop) + jnp.sum(jnp.exp(z - newtop[None, :]), axis=0)
            return ((newtop, total), None)

        start = (jnp.full((cols,), -jnp.inf, jnp.float32), jnp.zeros((cols,), jnp.float32))
        result, unused = lax.scan(step, start, (xblocks, fblocks))
        top, total = merged(result, ("gx", "gz"), combine)
        g_new = eps * (log_b - (top + jnp.log(total)))
        col_local = jnp.sum(jnp.abs(jnp.exp(log_b + (g_pot - g_new) / eps) - mass_b))
        g_pot = g_new
        row_terms.append(row_local * row_share)
        col_terms.append(col_local * col_share)
    row_vec = jnp.stack(row_terms)
    col_vec = jnp.stack(col_terms)
    row_vec, col_vec = (
        one_axis_at_a_time(row_vec, GX_GZ_GY),
        one_axis_at_a_time(col_vec, GX_GZ_GY),
    )
    errors = jnp.stack([row_vec, col_vec], axis=1)
    return (f_pot, g_pot, errors)


def solution(mesh):
    split = Mesh(
        mesh.devices.reshape(mesh.shape["gx"], mesh.shape["gz"], 4, 2), ("gx", "gz", "gy_0", "gy_1")
    )
    return jax.shard_map(
        on_device,
        mesh=split,
        in_specs=(P(("gx", "gz"), None), P(GY, None), P(("gx", "gz")), P(GY)),
        out_specs=(P(("gx", "gz")), P(GY), P()),
        check_vma=False,
    )
```

profile of v0, /device:TPU:1, one launch (start us, length us, event | category | flops | bytes accessed | tf_op | source)
XLA Modules:
  0.0 610.4 jit_solution(3720859963800496676)
XLA Ops:
  3.3 11.9 %all-to-all-start = ((f32[32,1,1]{2,1,0:T(1,128)}), f32[32,1,1]{2,1,0:T(1,128)S(1)}, u32[]{:S(2)}, u32[]{:S(2)}) async-start(f32[32,1,1]{2,1,0:T(1,128)} %broadcast_in_dim.279), calls=%async_computation | async-start | bytes 32768 | tf_op jit(solution)/shard_map/all_to_all | solution.py:20
  16.2 21.8 %while.250 = (s32[]{:T(128)}, f32[8,512]{1,0:T(8,128)S(1)}, f32[8,512]{1,0:T(8,128)S(1)}, bf16[8,512,128]{2,1,0:T(8,128)(2,1)}, f32[512]{0:T(512)S(1)}, /*index=5*/bf16[512,128]{1,0:T(8,128)(2,1)S(1)}, s32[]{:T(128)}, s32[]{:T(128)}) while((s32[]{:T(128)}, f32[8,512]{1,0:T(8,128)S(1)}, f32[8,512]{1,0:T(8,128)S(1)}, ...), condition=%wide.region_9.10_spmd, body=%wide.region_5.9_spmd.sunk | while | flops 69663232 | bytes 2511457 | solution.py:108
  74.5 9.5 %all-to-all-start.4 = ((f32[32,2,512]{2,1,0:T(2,128)}), f32[32,2,512]{2,1,0:T(2,128)S(1)}, u32[]{:S(2)}, u32[]{:S(2)}) async-start(f32[32,2,512]{2,1,0:T(2,128)} %broadcast_in_dim.285), calls=%async_computation.4 | async-start | bytes 262144 | tf_op jit(solution)/shard_map/all_to_all | solution.py:20
  84.6 9.2 %all-to-all-done.4 = f32[32,2,512]{2,1,0:T(2,128)S(1)} async-done(((f32[32,2,512]{2,1,0:T(2,128)}), f32[32,2,512]{2,1,0:T(2,128)S(1)}, u32[]{:S(2)}, u32[]{:S(2)}) %all-to-all-start.4) | async-done | bytes 131104 | tf_op jit(solution)/shard_map/all_to_all | solution.py:20
  95.1 7.4 %while.251 = (s32[]{:T(128)}, f32[8,512]{1,0:T(8,128)S(1)}, f32[8,512]{1,0:T(8,128)S(1)}, f32[512]{0:T(512)S(1)}, bf16[8,512,128]{2,1,0:T(8,128)(2,1)S(1)}, /*in...) while((s32[]{:T(128)}, f32[8,512]{1,0:T(8,128)S(1)}, f32[8,512]{1,0:T(8,128)S(1)}, ...), condition=%wide.region_19.20_spmd, body=%wide.region_15.0_spmd.sunk | while | flops 69663232 | bytes 2513005 | solution.py:108
  137.6 9.4 %all-to-all-done.7 = f32[32,2,512]{2,1,0:T(2,128)S(1)} async-done(((f32[32,2,512]{2,1,0:T(2,128)}), f32[32,2,512]{2,1,0:T(2,128)S(1)}, u32[]{:S(2)}, u32[]{:S(2)}) %all-to-all-start.7) | async-done | bytes 131104 | tf_op jit(solution)/shard_map/all_to_all | solution.py:20
  147.7 7.4 %while.252 = (s32[]{:T(128)}, f32[8,512]{1,0:T(8,128)S(1)}, f32[8,512]{1,0:T(8,128)S(1)}, f32[512]{0:T(512)S(1)}, bf16[8,512,128]{2,1,0:T(8,128)(2,1)S(1)}, /*in...) while((s32[]{:T(128)}, f32[8,512]{1,0:T(8,128)S(1)}, f32[8,512]{1,0:T(8,128)S(1)}, ...), condition=%wide.region_29.30_spmd, body=%wide.region_25.0_spmd.sunk | while | flops 69663232 | bytes 2513005 | solution.py:108
  189.7 9.4 %all-to-all-done.10 = f32[32,2,512]{2,1,0:T(2,128)S(1)} async-done(((f32[32,2,512]{2,1,0:T(2,128)}), f32[32,2,512]{2,1,0:T(2,128)S(1)}, u32[]{:S(2)}, u32[]{:S(2)}) %all-to-all-start.10) | async-done | bytes 131104 | tf_op jit(solution)/shard_map/all_to_all | solution.py:20
  199.7 7.4 %while.253 = (s32[]{:T(128)}, f32[8,512]{1,0:T(8,128)S(1)}, f32[8,512]{1,0:T(8,128)S(1)}, f32[512]{0:T(512)S(1)}, bf16[8,512,128]{2,1,0:T(8,128)(2,1)S(1)}, /*in...) while((s32[]{:T(128)}, f32[8,512]{1,0:T(8,128)S(1)}, f32[8,512]{1,0:T(8,128)S(1)}, ...), condition=%wide.region_39.40_spmd, body=%wide.region_35.39_spmd.sunk | while | flops 69663232 | bytes 2513005 | solution.py:108
  241.6 9.4 %all-to-all-done.13 = f32[32,2,512]{2,1,0:T(2,128)S(1)} async-done(((f32[32,2,512]{2,1,0:T(2,128)}), f32[32,2,512]{2,1,0:T(2,128)S(1)}, u32[]{:S(2)}, u32[]{:S(2)}) %all-to-all-start.13) | async-done | bytes 131104 | tf_op jit(solution)/shard_map/all_to_all | solution.py:20
  251.6 7.4 %while.254 = (s32[]{:T(128)}, f32[8,512]{1,0:T(8,128)S(1)}, f32[8,512]{1,0:T(8,128)S(1)}, f32[512]{0:T(512)S(1)}, bf16[8,512,128]{2,1,0:T(8,128)(2,1)S(1)}, /*in...) while((s32[]{:T(128)}, f32[8,512]{1,0:T(8,128)S(1)}, f32[8,512]{1,0:T(8,128)S(1)}, ...), condition=%wide.region_49.50_spmd, body=%wide.region_45.49_spmd.sunk | while | flops 69663232 | bytes 2513005 | solution.py:108
  293.5 9.4 %all-to-all-done.16 = f32[32,2,512]{2,1,0:T(2,128)S(1)} async-done(((f32[32,2,512]{2,1,0:T(2,128)}), f32[32,2,512]{2,1,0:T(2,128)S(1)}, u32[]{:S(2)}, u32[]{:S(2)}) %all-to-all-start.16) | async-done | bytes 131104 | tf_op jit(solution)/shard_map/all_to_all | solution.py:20
  303.5 7.4 %while.255 = (s32[]{:T(128)}, f32[8,512]{1,0:T(8,128)S(1)}, f32[8,512]{1,0:T(8,128)S(1)}, f32[512]{0:T(512)S(1)}, bf16[8,512,128]{2,1,0:T(8,128)(2,1)S(1)}, /*in...) while((s32[]{:T(128)}, f32[8,512]{1,0:T(8,128)S(1)}, f32[8,512]{1,0:T(8,128)S(1)}, ...), condition=%wide.region_59.60_spmd, body=%wide.region_55.0_spmd.sunk | while | flops 69663232 | bytes 2513005 | solution.py:108
  345.6 9.4 %all-to-all-done.19 = f32[32,2,512]{2,1,0:T(2,128)S(1)} async-done(((f32[32,2,512]{2,1,0:T(2,128)}), f32[32,2,512]{2,1,0:T(2,128)S(1)}, u32[]{:S(2)}, u32[]{:S(2)}) %all-to-all-start.19) | async-done | bytes 131104 | tf_op jit(solution)/shard_map/all_to_all | solution.py:20
  355.6 7.4 %while.256 = (s32[]{:T(128)}, f32[8,512]{1,0:T(8,128)S(1)}, f32[8,512]{1,0:T(8,128)S(1)}, f32[512]{0:T(512)S(1)}, bf16[8,512,128]{2,1,0:T(8,128)(2,1)S(1)}, /*in...) while((s32[]{:T(128)}, f32[8,512]{1,0:T(8,128)S(1)}, f32[8,512]{1,0:T(8,128)S(1)}, ...), condition=%wide.region_69.70_spmd, body=%wide.region_65.69_spmd.sunk | while | flops 69663232 | bytes 2513005 | solution.py:108
  397.4 9.4 %all-to-all-done.22 = f32[32,2,512]{2,1,0:T(2,128)S(1)} async-done(((f32[32,2,512]{2,1,0:T(2,128)}), f32[32,2,512]{2,1,0:T(2,128)S(1)}, u32[]{:S(2)}, u32[]{:S(2)}) %all-to-all-start.22) | async-done | bytes 131104 | tf_op jit(solution)/shard_map/all_to_all | solution.py:20
  407.5 7.4 %while.257 = (s32[]{:T(128)}, f32[8,512]{1,0:T(8,128)S(1)}, f32[8,512]{1,0:T(8,128)S(1)}, f32[512]{0:T(512)S(1)}, bf16[8,512,128]{2,1,0:T(8,128)(2,1)S(1)}, /*in...) while((s32[]{:T(128)}, f32[8,512]{1,0:T(8,128)S(1)}, f32[8,512]{1,0:T(8,128)S(1)}, ...), condition=%wide.region_79.80_spmd, body=%wide.region_75.79_spmd.sunk | while | flops 69663232 | bytes 2513005 | solution.py:108
  449.3 9.4 %all-to-all-done.25 = f32[32,2,512]{2,1,0:T(2,128)S(1)} async-done(((f32[32,2,512]{2,1,0:T(2,128)}), f32[32,2,512]{2,1,0:T(2,128)S(1)}, u32[]{:S(2)}, u32[]{:S(2)}) %all-to-all-start.25) | async-done | bytes 131104 | tf_op jit(solution)/shard_map/all_to_all | solution.py:20
  459.4 7.4 %while.258 = (s32[]{:T(128)}, f32[8,512]{1,0:T(8,128)S(1)}, f32[8,512]{1,0:T(8,128)S(1)}, f32[512]{0:T(512)S(1)}, bf16[8,512,128]{2,1,0:T(8,128)(2,1)S(1)}, /*in...) while((s32[]{:T(128)}, f32[8,512]{1,0:T(8,128)S(1)}, f32[8,512]{1,0:T(8,128)S(1)}, ...), condition=%wide.region_89.90_spmd, body=%wide.region_85.0_spmd.sunk | while | flops 69663232 | bytes 2513005 | solution.py:108
  501.5 9.4 %all-to-all-done.28 = f32[32,2,512]{2,1,0:T(2,128)S(1)} async-done(((f32[32,2,512]{2,1,0:T(2,128)}), f32[32,2,512]{2,1,0:T(2,128)S(1)}, u32[]{:S(2)}, u32[]{:S(2)}) %all-to-all-start.28) | async-done | bytes 131104 | tf_op jit(solution)/shard_map/all_to_all | solution.py:20
  511.5 7.4 %while.259 = (s32[]{:T(128)}, f32[8,512]{1,0:T(8,128)S(1)}, f32[8,512]{1,0:T(8,128)S(1)}, f32[512]{0:T(512)S(1)}, bf16[8,512,128]{2,1,0:T(8,128)(2,1)S(1)}, /*in...) while((s32[]{:T(128)}, f32[8,512]{1,0:T(8,128)S(1)}, f32[8,512]{1,0:T(8,128)S(1)}, ...), condition=%wide.region_99.100_spmd, body=%wide.region_95.99_spmd.sunk | while | flops 69663232 | bytes 2513005 | solution.py:108
  572.4 11.4 %all-reduce = (f32[10]{0:T(128)S(1)}, f32[10]{0:T(128)S(1)}) all-reduce(f32[10]{0:T(128)S(1)} %stack.97, f32[10]{0:T(128)S(1)} %stack.85), channel_id=1, replica_groups=mesh['gx'=8,'gz'=4,'gy_0'=4,'gy_1'=2] {'gx'}, use_global_device_ids=true, to_apply=%region_129.130 | all-reduce | flops 20 | bytes 160 | tf_op jit(solution)/shard_map/psum | solution.py:63
  583.8 7.2 %all-reduce.2 = (f32[10]{0:T(128)S(1)}, f32[10]{0:T(128)S(1)}) all-reduce(f32[10]{0:T(128)S(1)} %get-tuple-element.1336, f32[10]{0:T(128)S(1)} %get-tuple-element.1337), channel_id=1, replica_groups=mesh['gx'=8,'gz'=4,'gy_0'=4,'gy_1'=2] {'gz'}, use_global_device_ids=true, to_apply=%region_130.131 | all-reduce | flops 20 | bytes 160 | tf_op jit(solution)/shard_map/psum | solution.py:63
  598.0 11.4 %all-reduce.3 = (f32[10,1]{0,1:T(1,128)S(1)}, f32[10,1]{0,1:T(1,128)S(1)}) all-reduce(f32[10,1]{0,1:T(1,128)S(1)} %bitcast.776, f32[10,1]{0,1:T(1,128)S(1)} %bitcast.777), channel_id=1, replica_groups=mesh['gx'=8,'gz'=4,'gy_0'=4,'gy_1'=2] {'gy_1'}, use_global_device_ids=true, to_apply=%region_132.133 | all-reduce | flops 20 | bytes 160 | tf_op jit(solution)/shard_map/psum | solution.py:63
  (1543 shorter events, 519.9 us)
Async XLA Ops:
  3.3 34.8 %all-to-all-start = ((f32[32,1,1]{2,1,0:T(1,128)}), f32[32,1,1]{2,1,0:T(1,128)S(1)}, u32[]{:S(2)}, u32[]{:S(2)}) async-start(f32[32,1,1]{2,1,0:T(1,128)} %broadcast_in_dim.279), calls=%async_computation | async-start | bytes 32768 | tf_op jit(solution)/shard_map/all_to_all | solution.py:20
  38.7 10.7 %all-to-all-start.2 = ((f32[8,1,4096]{2,1,0:T(1,128)}), f32[8,1,4096]{2,1,0:T(1,128)S(1)}, u32[]{:S(2)}, u32[]{:S(2)}) async-start(f32[8,1,4096]{2,1,0:T(1,128)} %broadcast_in_dim.282), calls=%async_computation.2 | async-start | bytes 262144 | tf_op jit(solution)/shard_map/all_to_all | solution.py:20
  60.7 13.2 %all-to-all-start.1 = ((f32[8,1,1]{2,1,0:T(1,128)}), f32[8,1,1]{2,1,0:T(1,128)S(1)}, u32[]{:S(2)}, u32[]{:S(2)}) async-start(f32[8,1,1]{2,1,0:T(1,128)} %broadcast_in_dim.280), calls=%async_computation.1 | async-start | bytes 8192 | tf_op jit(solution)/shard_map/all_to_all | solution.py:20
  74.5 19.3 %all-to-all-start.4 = ((f32[32,2,512]{2,1,0:T(2,128)}), f32[32,2,512]{2,1,0:T(2,128)S(1)}, u32[]{:S(2)}, u32[]{:S(2)}) async-start(f32[32,2,512]{2,1,0:T(2,128)} %broadcast_in_dim.285), calls=%async_computation.4 | async-start | bytes 262144 | tf_op jit(solution)/shard_map/all_to_all | solution.py:20
  103.2 11.3 %all-to-all-start.5 = ((f32[8,1,4096]{2,1,0:T(1,128)}), f32[8,1,4096]{2,1,0:T(1,128)S(1)}, u32[]{:S(2)}, u32[]{:S(2)}) async-start(f32[8,1,4096]{2,1,0:T(1,128)} %broadcast_in_dim.287), calls=%async_computation.5 | async-start | bytes 262144 | tf_op jit(solution)/shard_map/all_to_all | solution.py:20
  133.7 13.3 %all-to-all-start.7 = ((f32[32,2,512]{2,1,0:T(2,128)}), f32[32,2,512]{2,1,0:T(2,128)S(1)}, u32[]{:S(2)}, u32[]{:S(2)}) async-start(f32[32,2,512]{2,1,0:T(2,128)} %broadcast_in_dim.290), calls=%async_computation.7 | async-start | bytes 262144 | tf_op jit(solution)/shard_map/all_to_all | solution.py:20
  155.8 10.7 %all-to-all-start.8 = ((f32[8,1,4096]{2,1,0:T(1,128)}), f32[8,1,4096]{2,1,0:T(1,128)S(1)}, u32[]{:S(2)}, u32[]{:S(2)}) async-start(f32[8,1,4096]{2,1,0:T(1,128)} %broadcast_in_dim.292), calls=%async_computation.8 | async-start | bytes 262144 | tf_op jit(solution)/shard_map/all_to_all | solution.py:20
  185.6 13.4 %all-to-all-start.10 = ((f32[32,2,512]{2,1,0:T(2,128)}), f32[32,2,512]{2,1,0:T(2,128)S(1)}, u32[]{:S(2)}, u32[]{:S(2)}) async-start(f32[32,2,512]{2,1,0:T(2,128)} %broadcast_in_dim.295), calls=%async_computation.10 | async-start | bytes 262144 | tf_op jit(solution)/shard_map/all_to_all | solution.py:20
  207.8 10.6 %all-to-all-start.11 = ((f32[8,1,4096]{2,1,0:T(1,128)}), f32[8,1,4096]{2,1,0:T(1,128)S(1)}, u32[]{:S(2)}, u32[]{:S(2)}) async-start(f32[8,1,4096]{2,1,0:T(1,128)} %broadcast_in_dim.297), calls=%async_computation.11 | async-start | bytes 262144 | tf_op jit(solution)/shard_map/all_to_all | solution.py:20
  219.2 9.4 %all-to-all-start.12 = ((f32[8,1,4096]{2,1,0:T(1,128)}), f32[8,1,4096]{2,1,0:T(1,128)S(1)}, u32[]{:S(2)}, u32[]{:S(2)}) async-start(f32[8,1,4096]{2,1,0:T(1,128)} %broadcast_in_dim.299), calls=%async_computation.12 | async-start | bytes 262144 | tf_op jit(solution)/shard_map/all_to_all | solution.py:20
  237.7 13.3 %all-to-all-start.13 = ((f32[32,2,512]{2,1,0:T(2,128)}), f32[32,2,512]{2,1,0:T(2,128)S(1)}, u32[]{:S(2)}, u32[]{:S(2)}) async-start(f32[32,2,512]{2,1,0:T(2,128)} %broadcast_in_dim.300), calls=%async_computation.13 | async-start | bytes 262144 | tf_op jit(solution)/shard_map/all_to_all | solution.py:20
  259.7 10.6 %all-to-all-start.14 = ((f32[8,1,4096]{2,1,0:T(1,128)}), f32[8,1,4096]{2,1,0:T(1,128)S(1)}, u32[]{:S(2)}, u32[]{:S(2)}) async-start(f32[8,1,4096]{2,1,0:T(1,128)} %broadcast_in_dim.302), calls=%async_computation.14 | async-start | bytes 262144 | tf_op jit(solution)/shard_map/all_to_all | solution.py:20
  289.6 13.3 %all-to-all-start.16 = ((f32[32,2,512]{2,1,0:T(2,128)}), f32[32,2,512]{2,1,0:T(2,128)S(1)}, u32[]{:S(2)}, u32[]{:S(2)}) async-start(f32[32,2,512]{2,1,0:T(2,128)} %broadcast_in_dim.305), calls=%async_computation.16 | async-start | bytes 262144 | tf_op jit(solution)/shard_map/all_to_all | solution.py:20
  311.6 10.6 %all-to-all-start.17 = ((f32[8,1,4096]{2,1,0:T(1,128)}), f32[8,1,4096]{2,1,0:T(1,128)S(1)}, u32[]{:S(2)}, u32[]{:S(2)}) async-start(f32[8,1,4096]{2,1,0:T(1,128)} %broadcast_in_dim.307), calls=%async_computation.17 | async-start | bytes 262144 | tf_op jit(solution)/shard_map/all_to_all | solution.py:20
  341.5 13.5 %all-to-all-start.19 = ((f32[32,2,512]{2,1,0:T(2,128)}), f32[32,2,512]{2,1,0:T(2,128)S(1)}, u32[]{:S(2)}, u32[]{:S(2)}) async-start(f32[32,2,512]{2,1,0:T(2,128)} %broadcast_in_dim.310), calls=%async_computation.19 | async-start | bytes 262144 | tf_op jit(solution)/shard_map/all_to_all | solution.py:20
  363.7 10.6 %all-to-all-start.20 = ((f32[8,1,4096]{2,1,0:T(1,128)}), f32[8,1,4096]{2,1,0:T(1,128)S(1)}, u32[]{:S(2)}, u32[]{:S(2)}) async-start(f32[8,1,4096]{2,1,0:T(1,128)} %broadcast_in_dim.312), calls=%async_computation.20 | async-start | bytes 262144 | tf_op jit(solution)/shard_map/all_to_all | solution.py:20
  393.6 13.3 %all-to-all-start.22 = ((f32[32,2,512]{2,1,0:T(2,128)}), f32[32,2,512]{2,1,0:T(2,128)S(1)}, u32[]{:S(2)}, u32[]{:S(2)}) async-start(f32[32,2,512]{2,1,0:T(2,128)} %broadcast_in_dim.315), calls=%async_computation.22 | async-start | bytes 262144 | tf_op jit(solution)/shard_map/all_to_all | solution.py:20
  415.6 10.6 %all-to-all-start.23 = ((f32[8,1,4096]{2,1,0:T(1,128)}), f32[8,1,4096]{2,1,0:T(1,128)S(1)}, u32[]{:S(2)}, u32[]{:S(2)}) async-start(f32[8,1,4096]{2,1,0:T(1,128)} %broadcast_in_dim.317), calls=%async_computation.23 | async-start | bytes 262144 | tf_op jit(solution)/shard_map/all_to_all | solution.py:20
  445.5 13.3 %all-to-all-start.25 = ((f32[32,2,512]{2,1,0:T(2,128)}), f32[32,2,512]{2,1,0:T(2,128)S(1)}, u32[]{:S(2)}, u32[]{:S(2)}) async-start(f32[32,2,512]{2,1,0:T(2,128)} %broadcast_in_dim.320), calls=%async_computation.25 | async-start | bytes 262144 | tf_op jit(solution)/shard_map/all_to_all | solution.py:20
  467.5 10.6 %all-to-all-start.26 = ((f32[8,1,4096]{2,1,0:T(1,128)}), f32[8,1,4096]{2,1,0:T(1,128)S(1)}, u32[]{:S(2)}, u32[]{:S(2)}) async-start(f32[8,1,4096]{2,1,0:T(1,128)} %broadcast_in_dim.322), calls=%async_computation.26 | async-start | bytes 262144 | tf_op jit(solution)/shard_map/all_to_all | solution.py:20
  497.4 13.5 %all-to-all-start.28 = ((f32[32,2,512]{2,1,0:T(2,128)}), f32[32,2,512]{2,1,0:T(2,128)S(1)}, u32[]{:S(2)}, u32[]{:S(2)}) async-start(f32[32,2,512]{2,1,0:T(2,128)} %broadcast_in_dim.325), calls=%async_computation.28 | async-start | bytes 262144 | tf_op jit(solution)/shard_map/all_to_all | solution.py:20
  519.7 10.6 %all-to-all-start.29 = ((f32[8,1,4096]{2,1,0:T(1,128)}), f32[8,1,4096]{2,1,0:T(1,128)S(1)}, u32[]{:S(2)}, u32[]{:S(2)}) async-start(f32[8,1,4096]{2,1,0:T(1,128)} %broadcast_in_dim.327), calls=%async_computation.29 | async-start | bytes 262144 | tf_op jit(solution)/shard_map/all_to_all | solution.py:20
  531.0 9.4 %all-to-all-start.30 = ((f32[8,1,4096]{2,1,0:T(1,128)}), f32[8,1,4096]{2,1,0:T(1,128)S(1)}, u32[]{:S(2)}, u32[]{:S(2)}) async-start(f32[8,1,4096]{2,1,0:T(1,128)} %broadcast_in_dim.329), calls=%async_computation.30 | async-start | bytes 262144 | tf_op jit(solution)/shard_map/all_to_all | solution.py:20
  550.8 13.3 %all-to-all-start.31 = ((f32[32,2,512]{2,1,0:T(2,128)}), f32[32,2,512]{2,1,0:T(2,128)S(1)}, u32[]{:S(2)}, u32[]{:S(2)}) async-start(f32[32,2,512]{2,1,0:T(2,128)} %broadcast_in_dim.330), calls=%async_computation.31 | async-start | bytes 262144 | tf_op jit(solution)/shard_map/all_to_all | solution.py:20
  (13 other events, 103.7 us)
where the time goes:
time: 623 us; the launch traced here: 610 us
  waiting for transfers between devices  188 us (30%)
  starting transfers between devices  157 us (25%)
  other arithmetic  82 us (13%)
  matrix products  74.7 us (12%)
  local copies, waits for them, and re-layouts  50.5 us (8%)
  blocking collectives  37 us (6%)
  between operations  16 us (3%)
    all_to_all x32, waiting for transfers between devices, from_everyone(): return lax.all_to_all(copies, axis, split_axis=0, concat_axis=0, tiled=True)  188 us
    all_to_all x32, starting transfers between devices, from_everyone(): return lax.all_to_all(copies, axis, split_axis=0, concat_axis=0, tiled=True)  157 us
    dot_general x160, matrix products, cost_block(): lax.dot_general(xb, col_embed, (((1,), (1,)), ((), ())), preferred_elemen...  74.7 us
    psum x4, blocking collectives, one_axis_at_a_time(): return functools.reduce(lax.psum, axes, x)  37 us
    reduce_sum x160, other arithmetic, cost_block(): row_sq = jnp.sum(xf * xf, axis=1)  31.5 us
    broadcast_in_dim x32, local copies, waits for them, and re-layouts, from_everyone(): copies = jnp.broadcast_to(x, (lax.axis_size(axis), *x.shape))  23.3 us
    reduce_sum x80, other arithmetic, one(): return (top, jnp.sum(jnp.exp(z - top[:, None]), axis=1))  15.8 us
    reduce_sum x80, other arithmetic, step(): jnp.sum(jnp.exp(z - newtop[None, :]), axis=0)  15.7 us
  transfers between devices with their start and end apart: 32, of which 30 were waited for; matrix products, arithmetic and copies ran while one was open for 6% of the time, Pallas kernels for 0%

commit v1 on v0

v1 whole, which is shorter than its diff:
```python
import functools
import math

import jax
import jax.numpy as jnp
from jax import lax
from jax.experimental import pallas as pl
from jax.experimental.pallas import tpu as pltpu
from jax.sharding import PartitionSpec as P

ITERS = 10
ROWS_OVER = ("gx", "gz")
COLS_OVER = "gy"
eps = 0.05
LOG2E = 1.0 / math.log(2.0)
LANES = 128
SMALLEST = 1e-26
f32 = jnp.float32


def log2(x):
    return jnp.log(x) * LOG2E


def lane_and_sublane():
    return (
        lax.broadcasted_iota(jnp.int32, (8, LANES), 1),
        lax.broadcasted_iota(jnp.int32, (8, LANES), 0),
    )


def total(x):
    return jnp.sum(jnp.sum(x, axis=1, keepdims=True), axis=0, keepdims=True)


def largest(x):
    return jnp.max(jnp.max(x, axis=1, keepdims=True), axis=0, keepdims=True)


def scaled_norms(embed, kappa):
    wide = embed.astype(f32)
    return kappa * jnp.sum(wide * wide, axis=1, keepdims=True)


def cross_of(y, xb):
    return lax.dot_general(y, xb, (((1,), (1,)), ((), ())), preferred_element_type=f32)


def joined(pieces):
    count = len(pieces)
    top = pieces[0]
    for k in range(1, count):
        top = jnp.maximum(top, pieces[k])
    weight = jnp.exp2(pieces[0] - top)
    for k in range(1, count):
        weight = weight + jnp.exp2(pieces[k] - top)
    return top + log2(weight)


def column_form(line, put):
    lane, sub = lane_and_sublane()
    for t in range(line.shape[0]):
        for q in range(LANES // 8):
            picked = jnp.where(lane == sub + 8 * q, line[t : t + 1, :], 0.0)
            put(t * LANES + 8 * q, jnp.broadcast_to(jnp.sum(picked, axis=1, keepdims=True), (8, LANES)))


def spread(out_ref, lines, extra):
    rows = lines.shape[0]
    for d in range(out_ref.shape[0]):
        out_ref[d, 0:rows, :] = lines
        if extra is not None:
            out_ref[d, rows : rows + extra.shape[0], :] = extra


def init_kernel(kappa, x_ref, y_ref, cm_ref, k_ref, mr_ref, xs_ref, out_ref, cs_ref, l_ref):
    cols = y_ref.shape[0]
    rows = x_ref.shape[0]
    wide = 512
    cs_ref[...] = jnp.broadcast_to(scaled_norms(y_ref[...], kappa), (cols, LANES))
    ones = jnp.ones((8, x_ref.shape[1]), f32)

    def chunk(c, carry):
        at = pl.multiple_of(c * wide, wide)
        xb = x_ref[pl.ds(at, wide), :]
        k_ref[:, pl.ds(at, wide)] = cross_of(y_ref[...], xb) * (2.0 * kappa)
        xf = xb.astype(f32)
        norms = kappa * lax.dot_general(
            ones, xf * xf, (((1,), (1,)), ((), ())),
            precision=lax.Precision.HIGHEST, preferred_element_type=f32,
        )
        for t in range(wide // LANES):
            here = pl.ds(pl.multiple_of(at + t * LANES, LANES), LANES)
            tops = [None] * 4
            for j in range(cols // 8):
                z = k_ref[8 * j : 8 * j + 8, here] - cs_ref[8 * j : 8 * j + 8, :]
                tops[j % 4] = z if tops[j % 4] is None else jnp.maximum(tops[j % 4], z)
            top = jnp.maximum(jnp.maximum(tops[0], tops[1]), jnp.maximum(tops[2], tops[3]))
            top = jnp.max(top, axis=0, keepdims=True)
            sums = [None] * 4
            for j in range(cols // 8):
                e = jnp.exp2(k_ref[8 * j : 8 * j + 8, here] - cs_ref[8 * j : 8 * j + 8, :] - top)
                k_ref[8 * j : 8 * j + 8, here] = e
                sums[j % 4] = e if sums[j % 4] is None else sums[j % 4] + e
            weight = jnp.sum((sums[0] + sums[1]) + (sums[2] + sums[3]), axis=0, keepdims=True)
            norm = norms[0:1, t * LANES : (t + 1) * LANES]
            line = pl.ds(c * (wide // LANES) + t, 1)
            xs_ref[line, :] = norm
            mr_ref[line, :] = top - norm
            l_ref[line, :] = (top - norm) + log2(weight)
        return carry

    lax.fori_loop(0, rows // wide, chunk, 0)
    mass = jnp.broadcast_to(jnp.sum(cm_ref[...], axis=0, keepdims=True), (8, LANES))
    spread(out_ref, l_ref[...], mass)


def exact_rows(kappa, x_ref, y_ref, gcol_ref, xs_ref, l_ref):
    cols = y_ref.shape[0]
    cs = scaled_norms(y_ref[...], kappa)

    def chunk(c, carry):
        at = pl.multiple_of(c * LANES, LANES)
        z = cross_of(y_ref[...], x_ref[pl.ds(at, LANES), :]) * (2.0 * kappa) - cs + gcol_ref[...]
        top = jnp.max(z, axis=0, keepdims=True)
        weight = jnp.sum(jnp.exp2(z - top), axis=0, keepdims=True)
        l_ref[pl.ds(c, 1), :] = top - xs_ref[pl.ds(c, 1), :] + log2(weight)
        return carry

    lax.fori_loop(0, x_ref.shape[0] // LANES, chunk, 0)


def exact_cols(kappa, x_ref, y_ref, fx_ref, s_ref, top_ref, weight_ref):
    cols = y_ref.shape[0]
    top_ref[...] = jnp.full(top_ref.shape, -jnp.inf, f32)
    weight_ref[...] = jnp.zeros(weight_ref.shape, f32)

    def chunk(c, carry):
        at = pl.multiple_of(c * LANES, LANES)
        z = cross_of(y_ref[...], x_ref[pl.ds(at, LANES), :]) * (2.0 * kappa) + fx_ref[pl.ds(c, 1), :]
        top = top_ref[...]
        newtop = jnp.maximum(top, jnp.max(z, axis=1, keepdims=True))
        weight_ref[...] = weight_ref[...] * jnp.exp2(top - newtop) + jnp.sum(
            jnp.exp2(z - newtop), axis=1, keepdims=True
        )
        top_ref[...] = newtop
        return carry

    lax.fori_loop(0, x_ref.shape[0] // LANES, chunk, 0)
    lse = top_ref[...] + log2(weight_ref[...]) - scaled_norms(y_ref[...], kappa)
    lane, sub = lane_and_sublane()
    for t in range(cols // LANES):
        line = jnp.zeros((8, LANES), f32)
        for q in range(LANES // 8):
            at = t * LANES + 8 * q
            line = line + jnp.where(lane == sub + 8 * q, lse[at : at + 8, :], 0.0)
        s_ref[t : t + 1, :] = jnp.sum(line, axis=0, keepdims=True)


def col_kernel(
    kappa, index, last,
    recv_ref, rm_ref, fprev_ref, mr_ref, xs_ref, sc_ref, errs_ref, k_ref, x_ref, y_ref,
    f_ref, sc_out_ref, errs_out_ref, out_ref,
    ubc_ref, s_ref, fx_ref, top_ref, weight_ref,
):
    rows, cols = k_ref.shape[1], k_ref.shape[0]
    lines = rows // LANES
    lane, sub = lane_and_sublane()
    lse = joined([recv_ref[d, 0:lines, :] for d in range(recv_ref.shape[0])])
    mass = rm_ref[...]
    la = log2(mass)
    sc = sc_ref[...]
    errs = errs_ref[...]
    if index == 0:
        f_new = la - lse
        mass_b = total(jnp.sum(recv_ref[:, lines : lines + 1, :], axis=0))
        sc_out_ref[...] = jnp.where(sub == 1, mass_b, 0.0)
        errs_out_ref[...] = errs
    else:
        mass_a = jnp.max(sc[0:1, :], axis=1, keepdims=True)
        shift = log2(mass_a)
        f_new = la - shift - lse
        share = mass / mass_a
        if index == 1:
            old = total(jnp.abs(jnp.exp2(la - fprev_ref[...]) - share))
            errs = jnp.where(lane == 0, old, errs)
            f_old = fprev_ref[...] - shift
        else:
            f_old = fprev_ref[...]
        now = total(jnp.abs(jnp.exp2(la - shift + (f_old - f_new)) - share))
        errs = jnp.where(lane == index, now, errs)
        sc_out_ref[...] = sc
        errs_out_ref[...] = errs
    f_ref[...] = f_new
    u = f_new + mr_ref[...]
    high = largest(u)
    u = jnp.exp2(u - high)
    for l in range(lines):
        ubc_ref[:, l * LANES : (l + 1) * LANES] = jnp.broadcast_to(u[l : l + 1, :], (8, LANES))

    def group(t, carry):
        line = jnp.zeros((8, LANES), f32)
        for half in range(2):
            acc = [None] * 8
            for l in range(lines):
                across = slice(l * LANES, (l + 1) * LANES)
                ul = ubc_ref[:, across]
                for q in range(8):
                    at = pl.multiple_of(t * LANES + half * 64 + 8 * q, 8)
                    term = k_ref[pl.ds(at, 8), across] * ul
                    acc[q] = term if acc[q] is None else acc[q] + term
            for q in range(8):
                full = jnp.sum(acc[q], axis=1, keepdims=True)
                line = line + jnp.where(lane == sub + (half * 64 + 8 * q), full, 0.0)
        s_ref[pl.ds(t, 1), :] = jnp.sum(line, axis=0, keepdims=True)
        return carry

    lax.fori_loop(0, cols // LANES, group, 0)
    sums = s_ref[...]
    least = jnp.min(sums)
    s_ref[...] = high + log2(sums)

    @pl.when(jnp.logical_not(least >= SMALLEST))
    def _():
        fx_ref[...] = f_new - xs_ref[...]
        exact_cols(kappa, x_ref, y_ref, fx_ref, s_ref, top_ref, weight_ref)

    extra = None
    if index == 0:
        extra = jnp.broadcast_to(jnp.sum(mass, axis=0, keepdims=True), (4, LANES))
    elif last:
        extra = errs[0:4, :]
    spread(out_ref, s_ref[...], extra)


def new_target(index, recv_ref, cm_ref, gprev_ref, sc_ref, errs_ref):
    lines = cm_ref.shape[0]
    lane, sub = lane_and_sublane()
    lse = joined([recv_ref[d, 0:lines, :] for d in range(recv_ref.shape[0])])
    sc = sc_ref[...]
    mass_b = jnp.max(sc[1:2, :], axis=1, keepdims=True)
    if index == 0:
        mass_a = total(jnp.sum(recv_ref[:, lines : lines + 1, :], axis=0))
        lse = lse - log2(mass_a)
        sc = jnp.where(sub == 0, mass_a, sc)
    mass = cm_ref[...]
    lb = log2(mass) - log2(mass_b)
    g_new = lb - lse
    now = total(jnp.abs(jnp.exp2(lb + (gprev_ref[...] - g_new)) - mass / mass_b))
    errs = jnp.where(lane == index, now, errs_ref[...])
    return g_new, sc, errs


def row_kernel(
    kappa, index,
    recv_ref, cm_ref, gprev_ref, mr_ref, xs_ref, sc_ref, errs_ref, k_ref, x_ref, y_ref,
    g_ref, sc_out_ref, errs_out_ref, out_ref,
    vbc_ref, r_ref, l_ref,
):
    rows, cols = k_ref.shape[1], k_ref.shape[0]
    g_new, sc, errs = new_target(index, recv_ref, cm_ref, gprev_ref, sc_ref, errs_ref)
    g_ref[...] = g_new
    sc_out_ref[...] = sc
    errs_out_ref[...] = errs
    high = largest(g_new)

    def put(at, piece):
        vbc_ref[at : at + 8, :] = piece

    column_form(jnp.exp2(g_new - high), put)
    together = 8

    def group(c, carry):
        acc = [None] * together
        for j in range(cols // 8):
            vj = vbc_ref[8 * j : 8 * j + 8, :]
            for t in range(together):
                at = pl.multiple_of(c * (together * LANES) + t * LANES, LANES)
                term = k_ref[8 * j : 8 * j + 8, pl.ds(at, LANES)] * vj
                acc[t] = term if acc[t] is None else acc[t] + term
        for t in range(together):
            r_ref[pl.ds(c * together + t, 1), :] = jnp.sum(acc[t], axis=0, keepdims=True)
        return carry

    lax.fori_loop(0, rows // (together * LANES), group, 0)
    sums = r_ref[...]
    least = jnp.min(sums)
    l_ref[...] = mr_ref[...] + (high + log2(sums))

    @pl.when(jnp.logical_not(least >= SMALLEST))
    def _():
        column_form(g_new, put)
        exact_rows(kappa, x_ref, y_ref, vbc_ref, xs_ref, l_ref)

    spread(out_ref, l_ref[...], None)


def last_kernel(
    index, recv_ref, cm_ref, gprev_ref, sc_ref, errs_ref, g_ref, row_ref, out_ref
):
    lines = cm_ref.shape[0]
    g_new, sc, errs = new_target(index, recv_ref, cm_ref, gprev_ref, sc_ref, errs_ref)
    g_ref[...] = g_new * (eps / LOG2E)
    row_ref[...] = jnp.broadcast_to(jnp.sum(recv_ref[:, lines : lines + 1, :], axis=0), (8, LANES))
    for d in range(out_ref.shape[0]):
        out_ref[d] = errs


def on_chip():
    return pl.BlockSpec(memory_space=pltpu.VMEM)


def call(kernel, args, outs, scratch, limit, name):
    return pl.pallas_call(
        kernel,
        in_specs=[on_chip() for _ in args],
        out_specs=[on_chip() for _ in outs],
        out_shape=[jax.ShapeDtypeStruct(shape, f32) for shape in outs],
        scratch_shapes=[pltpu.VMEM(shape, f32) for shape in scratch],
        compiler_params=pltpu.CompilerParams(vmem_limit_bytes=limit),
        name=name,
    )(*args)


def exchange(x, axis):
    return lax.all_to_all(x, axis, split_axis=0, concat_axis=0, tiled=True)


def on_device(row_embed, col_embed, row_mass, col_mass):
    rows, width = row_embed.shape
    cols = col_embed.shape[0]
    kappa = LOG2E / (width * eps)
    row_lines, col_lines = rows // LANES, cols // LANES
    by_col = lax.axis_size(COLS_OVER)
    by_row = lax.axis_size(ROWS_OVER)
    rm = row_mass.reshape(row_lines, LANES)
    cm = col_mass.reshape(col_lines, LANES)
    tile = (8, LANES)
    mib = 1 << 20
    k, mr, xs, out = call(
        functools.partial(init_kernel, kappa),
        (row_embed, col_embed, cm),
        [(cols, rows), (row_lines, LANES), (row_lines, LANES), (by_col, row_lines + 8, LANES)],
        [(cols, LANES), (row_lines, LANES)],
        24 * mib, "init",
    )
    f_pot = jnp.zeros((row_lines, LANES), f32)
    g_pot = jnp.zeros((col_lines, LANES), f32)
    sc = jnp.zeros(tile, f32)
    row_errs = jnp.zeros(tile, f32)
    col_errs = jnp.zeros(tile, f32)
    for index in range(ITERS):
        last = index == ITERS - 1
        got = exchange(out, COLS_OVER)
        more = 4 if index == 0 or last else 0
        f_pot, sc, row_errs, out = call(
            functools.partial(col_kernel, kappa, index, last),
            (got, rm, f_pot, mr, xs, sc, row_errs, k, row_embed, col_embed),
            [(row_lines, LANES), tile, tile, (by_row, col_lines + more, LANES)],
            [(8, rows), (col_lines, LANES), (row_lines, LANES), (cols, LANES), (cols, LANES)],
            24 * mib, f"cols{index}",
        )
        got = exchange(out, ROWS_OVER)
        if last:
            break
        g_pot, sc, col_errs, out = call(
            functools.partial(row_kernel, kappa, index),
            (got, cm, g_pot, mr, xs, sc, col_errs, k, row_embed, col_embed),
            [(col_lines, LANES), tile, tile, (by_col, row_lines, LANES)],
            [(cols, LANES), (row_lines, LANES), (row_lines, LANES)],
            24 * mib, f"rows{index}",
        )
    g_out, row_errs, out = call(
        functools.partial(last_kernel, ITERS - 1),
        (got, cm, g_pot, sc, col_errs),
        [(col_lines, LANES), tile, (by_col, 8, LANES)],
        [], 8 * mib, "finish",
    )
    got = exchange(out, COLS_OVER)
    col_vec = jnp.sum(got[:, 0, :ITERS], axis=0)
    errors = jnp.stack([row_errs[0, :ITERS], col_vec], axis=1)
    f_out = f_pot * (eps / LOG2E)
    return f_out.reshape(rows), g_out.reshape(cols), errors


def solution(mesh):
    return jax.shard_map(
        on_device,
        mesh=mesh,
        in_specs=(P(ROWS_OVER, None), P(COLS_OVER, None), P(ROWS_OVER), P(COLS_OVER)),
        out_specs=(P(ROWS_OVER), P(COLS_OVER), P()),
        check_vma=False,
    )
```

time: 623 us -> 500 us (0.80); the launches traced: 610 us -> 499 us
  Pallas kernels: 0 us -> 257 us
  blocking collectives: 37 us -> 214 us
  waiting for transfers between devices: 188 us -> 13.5 us
  starting transfers between devices: 157 us -> 9.18 us
  other arithmetic: 82 us -> 1.21 us
  matrix products: 74.7 us -> 0 us
  local copies, waits for them, and re-layouts: 50.5 us -> 3.53 us
  between operations: 16 us -> 0.78 us
    pallas_call x0 -> x21, Pallas kernels: none -> 257 us  [call(): pl.pallas_call(kernel, in_specs=[on_chip() for _ in args], out_specs=[on_...]
    all_to_all x0 -> x19, blocking collectives: none -> 214 us  [exchange(): return lax.all_to_all(x, axis, split_axis=0, concat_axis=0, tiled=True)]
    all_to_all x32 -> x2, waiting for transfers between devices: 188 us -> 13.5 us  [exchange(): return lax.all_to_all(x, axis, split_axis=0, concat_axis=0, tiled=True)]
    all_to_all x32 -> x2, starting transfers between devices: 157 us -> 9.18 us  [exchange(): return lax.all_to_all(x, axis, split_axis=0, concat_axis=0, tiled=True)]
    dot_general x160 -> x0, matrix products: 74.7 us -> none  [cost_block(): lax.dot_general(xb, col_embed, (((1,), (1,)), ((), ())), preferred_elemen...]
    reduce_sum x327 -> x1, other arithmetic: 69.9 us -> 0.03 us  [on_device(): col_vec = jnp.sum(got[:, 0, :ITERS], axis=0)]
    psum x4 -> x0, blocking collectives: 37 us -> none  [one_axis_at_a_time(): return functools.reduce(lax.psum, axes, x)]
    broadcast_in_dim x32 -> x2, local copies, waits for them, and re-layouts: 23.3 us -> 0.01 us  [the longest x1 0.01 us: on_device(): f_pot = jnp.zeros((row_lines, LANES), f32)]
  transfers between devices with their start and end apart: 32 -> 2, of which waited for: 30 -> 2; matrix products, arithmetic and copies ran while one was open for 6% -> 0% of each run, Pallas kernels for 0% -> 0%
where the time goes in v1:
time: 500 us; the launch traced here: 499 us
  Pallas kernels  257 us (51%)
  blocking collectives  214 us (43%)
  waiting for transfers between devices  13.5 us (3%)
  starting transfers between devices  9.18 us (2%)
    pallas_call x21, Pallas kernels, call(): pl.pallas_call(kernel, in_specs=[on_chip() for _ in args], out_specs=[on_...  257 us
    all_to_all x19, blocking collectives, exchange(): return lax.all_to_all(x, axis, split_axis=0, concat_axis=0, tiled=True)  214 us
    all_to_all x2, waiting for transfers between devices, exchange(): return lax.all_to_all(x, axis, split_axis=0, concat_axis=0, tiled=True)  13.5 us
  transfers between devices with their start and end apart: 2, of which 2 were waited for; matrix products, arithmetic and copies ran while one was open for 0% of the time, Pallas kernels for 0%

profile of v1, /device:TPU:1, one launch (start us, length us, event | category | flops | bytes accessed | tf_op | source)
XLA Modules:
  0.0 499.2 jit_solution(10173085297162729409)
XLA Ops:
  21.1 14.2 %cols0.1 = (f32[32,128]{1,0:T(8,128)S(1)}, f32[8,128]{1,0:T(8,128)S(1)}, f32[8,128]{1,0:T(8,128)S(1)}, f32[32,8,128]{2,1,0:T(8,128)S(1)}) custom-call(f32[8,40,128]{2,1,0:T(8,128)S(1)} %all_to_all.105.recv_ref, f32[32,128]{1,0:T(8,128)S(1)} %bitcast.8, f32[32,128]{1,0:T(8,128)S(1)} %broadcast_in_dim.6.fprev_ref, f32[32,128]{1,0:T(8,128)S(1)} %get-tuple-element.86.mr_ref, ...), custom_call_target="tpu_custom_call" | custom-call | tf_op jit(solution)/shard_map/cols0/pallas_call | solution.py:314
  35.3 20.2 %all_to_all.106.recv_ref = f32[32,8,128]{2,1,0:T(8,128)S(1)} all-to-all(f32[32,8,128]{2,1,0:T(8,128)S(1)} %get-tuple-element.89), channel_id=1, replica_groups=mesh['gx'=8,'gz'=4,'gy'=8] {'gx','gz'}, dimensions={0} | all-to-all | bytes 262144 | tf_op jit(solution)/shard_map/all_to_all | solution.py:326
  55.5 12.0 %rows0.1 = (f32[4,128]{1,0:T(4,128)S(1)}, f32[8,128]{1,0:T(8,128)S(1)}, f32[8,128]{1,0:T(8,128)S(1)}, f32[8,32,128]{2,1,0:T(8,128)S(1)}) custom-call(f32[32,8,128]{2,1,0:T(8,128)S(1)} %all_to_all.106.recv_ref, f32[4,128]{1,0:T(4,128)S(1)} %bitcast.19, f32[4,128]{1,0:T(4,128)S(1)} %broadcast_in_dim.7.gprev_ref, f32[32,128]{1,0:T(8,128)S(1)} %get-tuple-element.86.mr_ref, ...), custom_call_target="tpu_custom_call" | custom-call | tf_op jit(solution)/shard_map/rows0/pallas_call | solution.py:314
  77.5 14.1 %cols1.1 = (f32[32,128]{1,0:T(8,128)S(1)}, f32[8,128]{1,0:T(8,128)S(1)}, f32[8,128]{1,0:T(8,128)S(1)}, f32[32,4,128]{2,1,0:T(4,128)S(1)}) custom-call(f32[8,32,128]{2,1,0:T(8,128)S(1)} %all_to_all.107.recv_ref, f32[32,128]{1,0:T(8,128)S(1)} %bitcast.9, f32[32,128]{1,0:T(8,128)S(1)} %get-tuple-element.92.fprev_ref, f32[32,128]{1,0:T(8,128)S(1)} %get-tuple-element.86.mr_ref, ...), custom_call_target="tpu_custom_call" | custom-call | tf_op jit(solution)/shard_map/cols1/pallas_call | solution.py:314
  103.5 12.0 %rows1.1 = (f32[4,128]{1,0:T(4,128)S(1)}, f32[8,128]{1,0:T(8,128)S(1)}, f32[8,128]{1,0:T(8,128)S(1)}, f32[8,32,128]{2,1,0:T(8,128)S(1)}) custom-call(f32[32,4,128]{2,1,0:T(4,128)S(1)} %all_to_all.108.recv_ref, f32[4,128]{1,0:T(4,128)S(1)} %bitcast.20, f32[4,128]{1,0:T(4,128)S(1)} %get-tuple-element.96.gprev_ref, f32[32,128]{1,0:T(8,128)S(1)} %get-tuple-element.86.mr_ref, ...), custom_call_target="tpu_custom_call" | custom-call | tf_op jit(solution)/shard_map/rows1/pallas_call | solution.py:314
  125.4 14.1 %cols2.1 = (f32[32,128]{1,0:T(8,128)S(1)}, f32[8,128]{1,0:T(8,128)S(1)}, f32[8,128]{1,0:T(8,128)S(1)}, f32[32,4,128]{2,1,0:T(4,128)S(1)}) custom-call(f32[8,32,128]{2,1,0:T(8,128)S(1)} %all_to_all.109.recv_ref, f32[32,128]{1,0:T(8,128)S(1)} %bitcast.10, f32[32,128]{1,0:T(8,128)S(1)} %get-tuple-element.100.fprev_ref, f32[32,128]{1,0:T(8,128)S(1)} %get-tuple-element.86.mr_ref, ...), custom_call_target="tpu_custom_call" | custom-call | tf_op jit(solution)/shard_map/cols2/pallas_call | solution.py:314
  139.5 11.8 %all_to_all.110.recv_ref = f32[32,4,128]{2,1,0:T(4,128)S(1)} all-to-all(f32[32,4,128]{2,1,0:T(4,128)S(1)} %get-tuple-element.103), channel_id=1, replica_groups=mesh['gx'=8,'gz'=4,'gy'=8] {'gx','gz'}, dimensions={0} | all-to-all | bytes 131072 | tf_op jit(solution)/shard_map/all_to_all | solution.py:326
  151.4 12.0 %rows2.1 = (f32[4,128]{1,0:T(4,128)S(1)}, f32[8,128]{1,0:T(8,128)S(1)}, f32[8,128]{1,0:T(8,128)S(1)}, f32[8,32,128]{2,1,0:T(8,128)S(1)}) custom-call(f32[32,4,128]{2,1,0:T(4,128)S(1)} %all_to_all.110.recv_ref, f32[4,128]{1,0:T(4,128)S(1)} %bitcast.21, f32[4,128]{1,0:T(4,128)S(1)} %get-tuple-element.104.gprev_ref, f32[32,128]{1,0:T(8,128)S(1)} %get-tuple-element.86.mr_ref, ...), custom_call_target="tpu_custom_call" | custom-call | tf_op jit(solution)/shard_map/rows2/pallas_call | solution.py:314
  173.1 14.1 %cols3.1 = (f32[32,128]{1,0:T(8,128)S(1)}, f32[8,128]{1,0:T(8,128)S(1)}, f32[8,128]{1,0:T(8,128)S(1)}, f32[32,4,128]{2,1,0:T(4,128)S(1)}) custom-call(f32[8,32,128]{2,1,0:T(8,128)S(1)} %all_to_all.111.recv_ref, f32[32,128]{1,0:T(8,128)S(1)} %bitcast.11, f32[32,128]{1,0:T(8,128)S(1)} %get-tuple-element.108.fprev_ref, f32[32,128]{1,0:T(8,128)S(1)} %get-tuple-element.86.mr_ref, ...), custom_call_target="tpu_custom_call" | custom-call | tf_op jit(solution)/shard_map/cols3/pallas_call | solution.py:314
  199.1 12.0 %rows3.1 = (f32[4,128]{1,0:T(4,128)S(1)}, f32[8,128]{1,0:T(8,128)S(1)}, f32[8,128]{1,0:T(8,128)S(1)}, f32[8,32,128]{2,1,0:T(8,128)S(1)}) custom-call(f32[32,4,128]{2,1,0:T(4,128)S(1)} %all_to_all.112.recv_ref, f32[4,128]{1,0:T(4,128)S(1)} %bitcast.22, f32[4,128]{1,0:T(4,128)S(1)} %get-tuple-element.112.gprev_ref, f32[32,128]{1,0:T(8,128)S(1)} %get-tuple-element.86.mr_ref, ...), custom_call_target="tpu_custom_call" | custom-call | tf_op jit(solution)/shard_map/rows3/pallas_call | solution.py:314
  220.9 14.1 %cols4.1 = (f32[32,128]{1,0:T(8,128)S(1)}, f32[8,128]{1,0:T(8,128)S(1)}, f32[8,128]{1,0:T(8,128)S(1)}, f32[32,4,128]{2,1,0:T(4,128)S(1)}) custom-call(f32[8,32,128]{2,1,0:T(8,128)S(1)} %all_to_all.113.recv_ref, f32[32,128]{1,0:T(8,128)S(1)} %bitcast.12, f32[32,128]{1,0:T(8,128)S(1)} %get-tuple-element.116.fprev_ref, f32[32,128]{1,0:T(8,128)S(1)} %get-tuple-element.86.mr_ref, ...), custom_call_target="tpu_custom_call" | custom-call | tf_op jit(solution)/shard_map/cols4/pallas_call | solution.py:314
  235.0 11.8 %all_to_all.114.recv_ref = f32[32,4,128]{2,1,0:T(4,128)S(1)} all-to-all(f32[32,4,128]{2,1,0:T(4,128)S(1)} %get-tuple-element.119), channel_id=1, replica_groups=mesh['gx'=8,'gz'=4,'gy'=8] {'gx','gz'}, dimensions={0} | all-to-all | bytes 131072 | tf_op jit(solution)/shard_map/all_to_all | solution.py:326
  246.8 12.0 %rows4.1 = (f32[4,128]{1,0:T(4,128)S(1)}, f32[8,128]{1,0:T(8,128)S(1)}, f32[8,128]{1,0:T(8,128)S(1)}, f32[8,32,128]{2,1,0:T(8,128)S(1)}) custom-call(f32[32,4,128]{2,1,0:T(4,128)S(1)} %all_to_all.114.recv_ref, f32[4,128]{1,0:T(4,128)S(1)} %bitcast.23, f32[4,128]{1,0:T(4,128)S(1)} %get-tuple-element.120.gprev_ref, f32[32,128]{1,0:T(8,128)S(1)} %get-tuple-element.86.mr_ref, ...), custom_call_target="tpu_custom_call" | custom-call | tf_op jit(solution)/shard_map/rows4/pallas_call | solution.py:314
  268.6 14.3 %cols5.1 = (f32[32,128]{1,0:T(8,128)S(1)}, f32[8,128]{1,0:T(8,128)S(1)}, f32[8,128]{1,0:T(8,128)S(1)}, f32[32,4,128]{2,1,0:T(4,128)S(1)}) custom-call(f32[8,32,128]{2,1,0:T(8,128)S(1)} %all_to_all.115.recv_ref, f32[32,128]{1,0:T(8,128)S(1)} %bitcast.13, f32[32,128]{1,0:T(8,128)S(1)} %get-tuple-element.124.fprev_ref, f32[32,128]{1,0:T(8,128)S(1)} %get-tuple-element.86.mr_ref, ...), custom_call_target="tpu_custom_call" | custom-call | tf_op jit(solution)/shard_map/cols5/pallas_call | solution.py:314
  282.9 11.8 %all_to_all.116.recv_ref = f32[32,4,128]{2,1,0:T(4,128)S(1)} all-to-all(f32[32,4,128]{2,1,0:T(4,128)S(1)} %get-tuple-element.127), channel_id=1, replica_groups=mesh['gx'=8,'gz'=4,'gy'=8] {'gx','gz'}, dimensions={0} | all-to-all | bytes 131072 | tf_op jit(solution)/shard_map/all_to_all | solution.py:326
  294.8 12.0 %rows5.1 = (f32[4,128]{1,0:T(4,128)S(1)}, f32[8,128]{1,0:T(8,128)S(1)}, f32[8,128]{1,0:T(8,128)S(1)}, f32[8,32,128]{2,1,0:T(8,128)S(1)}) custom-call(f32[32,4,128]{2,1,0:T(4,128)S(1)} %all_to_all.116.recv_ref, f32[4,128]{1,0:T(4,128)S(1)} %bitcast.24, f32[4,128]{1,0:T(4,128)S(1)} %get-tuple-element.128.gprev_ref, f32[32,128]{1,0:T(8,128)S(1)} %get-tuple-element.86.mr_ref, ...), custom_call_target="tpu_custom_call" | custom-call | tf_op jit(solution)/shard_map/rows5/pallas_call | solution.py:314
  316.5 14.1 %cols6.1 = (f32[32,128]{1,0:T(8,128)S(1)}, f32[8,128]{1,0:T(8,128)S(1)}, f32[8,128]{1,0:T(8,128)S(1)}, f32[32,4,128]{2,1,0:T(4,128)S(1)}) custom-call(f32[8,32,128]{2,1,0:T(8,128)S(1)} %all_to_all.117.recv_ref, f32[32,128]{1,0:T(8,128)S(1)} %bitcast.14, f32[32,128]{1,0:T(8,128)S(1)} %get-tuple-element.132.fprev_ref, f32[32,128]{1,0:T(8,128)S(1)} %get-tuple-element.86.mr_ref, ...), custom_call_target="tpu_custom_call" | custom-call | tf_op jit(solution)/shard_map/cols6/pallas_call | solution.py:314
  342.5 12.0 %rows6.1 = (f32[4,128]{1,0:T(4,128)S(1)}, f32[8,128]{1,0:T(8,128)S(1)}, f32[8,128]{1,0:T(8,128)S(1)}, f32[8,32,128]{2,1,0:T(8,128)S(1)}) custom-call(f32[32,4,128]{2,1,0:T(4,128)S(1)} %all_to_all.118.recv_ref, f32[4,128]{1,0:T(4,128)S(1)} %bitcast.25, f32[4,128]{1,0:T(4,128)S(1)} %get-tuple-element.136.gprev_ref, f32[32,128]{1,0:T(8,128)S(1)} %get-tuple-element.86.mr_ref, ...), custom_call_target="tpu_custom_call" | custom-call | tf_op jit(solution)/shard_map/rows6/pallas_call | solution.py:314
  364.2 14.1 %cols7.1 = (f32[32,128]{1,0:T(8,128)S(1)}, f32[8,128]{1,0:T(8,128)S(1)}, f32[8,128]{1,0:T(8,128)S(1)}, f32[32,4,128]{2,1,0:T(4,128)S(1)}) custom-call(f32[8,32,128]{2,1,0:T(8,128)S(1)} %all_to_all.119.recv_ref, f32[32,128]{1,0:T(8,128)S(1)} %bitcast.15, f32[32,128]{1,0:T(8,128)S(1)} %get-tuple-element.140.fprev_ref, f32[32,128]{1,0:T(8,128)S(1)} %get-tuple-element.86.mr_ref, ...), custom_call_target="tpu_custom_call" | custom-call | tf_op jit(solution)/shard_map/cols7/pallas_call | solution.py:314
  378.4 11.8 %all_to_all.120.recv_ref = f32[32,4,128]{2,1,0:T(4,128)S(1)} all-to-all(f32[32,4,128]{2,1,0:T(4,128)S(1)} %get-tuple-element.143), channel_id=1, replica_groups=mesh['gx'=8,'gz'=4,'gy'=8] {'gx','gz'}, dimensions={0} | all-to-all | bytes 131072 | tf_op jit(solution)/shard_map/all_to_all | solution.py:326
  390.2 12.0 %rows7.1 = (f32[4,128]{1,0:T(4,128)S(1)}, f32[8,128]{1,0:T(8,128)S(1)}, f32[8,128]{1,0:T(8,128)S(1)}, f32[8,32,128]{2,1,0:T(8,128)S(1)}) custom-call(f32[32,4,128]{2,1,0:T(4,128)S(1)} %all_to_all.120.recv_ref, f32[4,128]{1,0:T(4,128)S(1)} %bitcast.26, f32[4,128]{1,0:T(4,128)S(1)} %get-tuple-element.144.gprev_ref, f32[32,128]{1,0:T(8,128)S(1)} %get-tuple-element.86.mr_ref, ...), custom_call_target="tpu_custom_call" | custom-call | tf_op jit(solution)/shard_map/rows7/pallas_call | solution.py:314
  412.0 14.1 %cols8.1 = (f32[32,128]{1,0:T(8,128)S(1)}, f32[8,128]{1,0:T(8,128)S(1)}, f32[8,128]{1,0:T(8,128)S(1)}, f32[32,4,128]{2,1,0:T(4,128)S(1)}) custom-call(f32[8,32,128]{2,1,0:T(8,128)S(1)} %all_to_all.121.recv_ref, f32[32,128]{1,0:T(8,128)S(1)} %bitcast.16, f32[32,128]{1,0:T(8,128)S(1)} %get-tuple-element.148.fprev_ref, f32[32,128]{1,0:T(8,128)S(1)} %get-tuple-element.86.mr_ref, ...), custom_call_target="tpu_custom_call" | custom-call | tf_op jit(solution)/shard_map/cols8/pallas_call | solution.py:314
  437.9 12.0 %rows8.1 = (f32[4,128]{1,0:T(4,128)S(1)}, f32[8,128]{1,0:T(8,128)S(1)}, f32[8,128]{1,0:T(8,128)S(1)}, f32[8,32,128]{2,1,0:T(8,128)S(1)}) custom-call(f32[32,4,128]{2,1,0:T(4,128)S(1)} %all_to_all.122.recv_ref, f32[4,128]{1,0:T(4,128)S(1)} %bitcast.27, f32[4,128]{1,0:T(4,128)S(1)} %get-tuple-element.152.gprev_ref, f32[32,128]{1,0:T(8,128)S(1)} %get-tuple-element.86.mr_ref, ...), custom_call_target="tpu_custom_call" | custom-call | tf_op jit(solution)/shard_map/rows8/pallas_call | solution.py:314
  459.7 14.8 %cols9.1 = (f32[32,128]{1,0:T(8,128)S(1)}, f32[8,128]{1,0:T(8,128)S(1)}, f32[8,128]{1,0:T(8,128)}, f32[32,8,128]{2,1,0:T(8,128)}) custom-call(f32[8,32,128]{2,1,0:T(8,128)S(1)} %all_to_all.123.recv_ref, f32[32,128]{1,0:T(8,128)S(1)} %bitcast.17, f32[32,128]{1,0:T(8,128)S(1)} %get-tuple-element.156.fprev_ref, f32[32,128]{1,0:T(8,128)S(1)} %get-tuple-element.86.mr_ref, ...), custom_call_target="tpu_custom_call" | custom-call | tf_op jit(solution)/shard_map/cols9/pallas_call | solution.py:314
  (39 shorter events, 180.7 us)
Async XLA Ops:
  0.6 1.2 copy-start
  1.9 0.9 copy-start.1
  2.8 0.7 copy-start.4
  20.4 0.7 copy-start.2
  21.1 56.4 %copy-start.3 = (f32[4096]{0:T(1024)S(1)}, f32[4096]{0:T(1024)}, u32[]{:S(2)}) copy-start(f32[4096]{0:T(1024)} %param.6) | copy-start | bytes 49156
  437.9 49.8 %copy-start.5 = (f32[512]{0:T(512)S(1)}, f32[512]{0:T(512)}, u32[]{:S(2)}) copy-start(f32[512]{0:T(512)} %param.7) | copy-start | bytes 6148
  474.5 13.3 %all-to-all-start.19 = ((f32[32,8,128]{2,1,0:T(8,128)}), f32[32,8,128]{2,1,0:T(8,128)S(1)}, u32[]{:S(2)}, u32[]{:S(2)}) async-start(f32[32,8,128]{2,1,0:T(8,128)} %get-tuple-element.160), calls=%async_computation.19 | async-start | bytes 262144 | tf_op jit(solution)/shard_map/all_to_all | solution.py:326
  488.5 10.1 %all-to-all-start.20 = ((f32[8,8,128]{2,1,0:T(8,128)}), f32[8,8,128]{2,1,0:T(8,128)S(1)}, u32[]{:S(2)}, u32[]{:S(2)}) async-start(f32[8,8,128]{2,1,0:T(8,128)} %get-tuple-element.166), calls=%async_computation.20 | async-start | bytes 65536 | tf_op jit(solution)/shard_map/all_to_all | solution.py:326

commit v2 on v1

v2 whole, which is shorter than its diff:
```python
import functools
import math

import jax
import jax.numpy as jnp
from jax import lax
from jax.experimental import pallas as pl
from jax.experimental.pallas import tpu as pltpu
from jax.sharding import PartitionSpec as P

ITERS = 10
ROWS_OVER = ("gx", "gz")
COLS_OVER = "gy"
eps = 0.05
LOG2E = 1.0 / math.log(2.0)
LANES = 128
SMALLEST = 1e-20
DRIFT = 20.0
f32 = jnp.float32


def log2(x):
    return jnp.log(x) * LOG2E


def lane_and_sublane():
    return (
        lax.broadcasted_iota(jnp.int32, (8, LANES), 1),
        lax.broadcasted_iota(jnp.int32, (8, LANES), 0),
    )


def total(x):
    return jnp.sum(jnp.sum(x, axis=1, keepdims=True), axis=0, keepdims=True)


def largest(x):
    return jnp.max(jnp.max(x, axis=1, keepdims=True), axis=0, keepdims=True)


def scaled_norms(embed, kappa):
    wide = embed.astype(f32)
    return kappa * jnp.sum(wide * wide, axis=1, keepdims=True)


def cross_of(y, xb):
    return lax.dot_general(y, xb, (((1,), (1,)), ((), ())), preferred_element_type=f32)


def in_pairs(pieces, combine):
    while len(pieces) > 1:
        rest = [pieces[-1]] if len(pieces) % 2 else []
        pieces = [combine(*pair) for pair in zip(pieces[::2], pieces[1::2])] + rest
    return pieces[0]


def joined(pieces):
    top = in_pairs(pieces, jnp.maximum)
    return top + log2(in_pairs([jnp.exp2(piece - top) for piece in pieces], jnp.add))


def column_form(line, put):
    lane, sub = lane_and_sublane()
    for t in range(line.shape[0]):
        for q in range(LANES // 8):
            picked = jnp.where(lane == sub + 8 * q, line[t : t + 1, :], 0.0)
            put(t * LANES + 8 * q, jnp.broadcast_to(jnp.sum(picked, axis=1, keepdims=True), (8, LANES)))


def spread(out_ref, lines, extra):
    rows = lines.shape[0]
    for d in range(out_ref.shape[0]):
        out_ref[d, 0:rows, :] = lines
        if extra is not None:
            out_ref[d, rows : rows + extra.shape[0], :] = extra


def noted(errs, index, terms):
    row = lax.broadcasted_iota(jnp.int32, errs.shape, 0)
    return jnp.where(row == index, jnp.sum(terms, axis=0, keepdims=True), errs)


def along_lanes(errs):
    row = lax.broadcasted_iota(jnp.int32, errs.shape, 0)
    lane = lax.broadcasted_iota(jnp.int32, errs.shape, 1)
    picked = jnp.where(row == lane, jnp.sum(errs, axis=1, keepdims=True), 0.0)
    return jnp.sum(picked, axis=0, keepdims=True)


def init_kernel(
    kappa, x_hbm, y_hbm, rm_hbm, cm_hbm,
    x_ref, y_ref, rm_ref, cm_ref, k_ref, mr_ref, xs_ref, out_ref, half_ref, l_ref, sems,
):
    pairs = ((y_hbm, y_ref), (x_hbm, x_ref), (cm_hbm, cm_ref), (rm_hbm, rm_ref))
    copies = [pltpu.make_async_copy(src, dst, sems.at[i]) for i, (src, dst) in enumerate(pairs)]
    for copy in copies:
        copy.start()
    cols = y_ref.shape[0]
    rows = x_ref.shape[0]
    wide, block = 512, 64
    tiles = wide // LANES
    copies[0].wait()
    half_ref[...] = jnp.broadcast_to(scaled_norms(y_ref[...], 0.5), (cols, LANES))
    ones = jnp.ones((8, x_ref.shape[1]), f32)
    copies[1].wait()

    def chunk(c, carry):
        at = pl.multiple_of(c * wide, wide)
        xb = x_ref[pl.ds(at, wide), :]
        k_ref[:, pl.ds(at, wide)] = cross_of(y_ref[...], xb)
        xf = xb.astype(f32)
        norms = kappa * lax.dot_general(
            ones, xf * xf, (((1,), (1,)), ((), ())),
            precision=lax.Precision.HIGHEST, preferred_element_type=f32,
        )
        here = [pl.ds(pl.multiple_of(at + t * LANES, LANES), LANES) for t in range(tiles)]

        def highest(b, tops):
            tops = list(tops)
            for j in range(block // 8):
                line = pl.ds(pl.multiple_of(b * block + 8 * j, 8), 8)
                half = half_ref[line, :]
                for t in range(tiles):
                    z = k_ref[line, here[t]] - half
                    k_ref[line, here[t]] = z
                    tops[t] = jnp.maximum(tops[t], z)
            return tuple(tops)

        low = jnp.full((8, LANES), -jnp.inf, f32)
        tops = lax.fori_loop(0, cols // block, highest, (low,) * tiles)
        tops = [jnp.max(top, axis=0, keepdims=True) for top in tops]
        spans = [jnp.broadcast_to(top, (8, LANES)) for top in tops]

        def weigh(b, sums):
            sums = list(sums)
            for j in range(block // 8):
                line = pl.ds(pl.multiple_of(b * block + 8 * j, 8), 8)
                for t in range(tiles):
                    e = jnp.exp2((k_ref[line, here[t]] - spans[t]) * (2.0 * kappa))
                    k_ref[line, here[t]] = e
                    sums[t] = sums[t] + e
            return tuple(sums)

        sums = lax.fori_loop(0, cols // block, weigh, (jnp.zeros((8, LANES), f32),) * tiles)
        for t in range(tiles):
            weight = jnp.sum(sums[t], axis=0, keepdims=True)
            norm = norms[0:1, t * LANES : (t + 1) * LANES]
            line = pl.ds(c * tiles + t, 1)
            base = tops[t] * (2.0 * kappa) - norm
            xs_ref[line, :] = norm
            mr_ref[line, :] = base
            l_ref[line, :] = base + log2(weight)
        return carry

    lax.fori_loop(0, rows // wide, chunk, 0)
    copies[2].wait()
    copies[3].wait()
    mass = jnp.broadcast_to(jnp.sum(cm_ref[...], axis=0, keepdims=True), (8, LANES))
    spread(out_ref, l_ref[...], mass)


def exact_rows(kappa, x_ref, y_ref, gcol_ref, xs_ref, l_ref):
    cols = y_ref.shape[0]
    cs = scaled_norms(y_ref[...], kappa)

    def chunk(c, carry):
        at = pl.multiple_of(c * LANES, LANES)
        z = cross_of(y_ref[...], x_ref[pl.ds(at, LANES), :]) * (2.0 * kappa) - cs + gcol_ref[...]
        top = jnp.max(z, axis=0, keepdims=True)
        weight = jnp.sum(jnp.exp2(z - top), axis=0, keepdims=True)
        l_ref[pl.ds(c, 1), :] = top - xs_ref[pl.ds(c, 1), :] + log2(weight)
        return carry

    lax.fori_loop(0, x_ref.shape[0] // LANES, chunk, 0)


def exact_cols(kappa, x_ref, y_ref, fx_ref, s_ref, top_ref, weight_ref):
    cols = y_ref.shape[0]
    top_ref[...] = jnp.full(top_ref.shape, -jnp.inf, f32)
    weight_ref[...] = jnp.zeros(weight_ref.shape, f32)

    def chunk(c, carry):
        at = pl.multiple_of(c * LANES, LANES)
        z = cross_of(y_ref[...], x_ref[pl.ds(at, LANES), :]) * (2.0 * kappa) + fx_ref[pl.ds(c, 1), :]
        top = top_ref[...]
        newtop = jnp.maximum(top, jnp.max(z, axis=1, keepdims=True))
        weight_ref[...] = weight_ref[...] * jnp.exp2(top - newtop) + jnp.sum(
            jnp.exp2(z - newtop), axis=1, keepdims=True
        )
        top_ref[...] = newtop
        return carry

    lax.fori_loop(0, x_ref.shape[0] // LANES, chunk, 0)
    lse = top_ref[...] + log2(weight_ref[...]) - scaled_norms(y_ref[...], kappa)
    lane, sub = lane_and_sublane()
    for t in range(cols // LANES):
        line = jnp.zeros((8, LANES), f32)
        for q in range(LANES // 8):
            at = t * LANES + 8 * q
            line = line + jnp.where(lane == sub + 8 * q, lse[at : at + 8, :], 0.0)
        s_ref[t : t + 1, :] = jnp.sum(line, axis=0, keepdims=True)


def col_kernel(
    kappa, index, last,
    recv_ref, rm_ref, fprev_ref, mr_ref, xs_ref, sc_ref, errs_ref, k_ref, x_ref, y_ref,
    f_ref, sc_out_ref, errs_out_ref, out_ref,
    ubc_ref, acc_ref, s_ref, fx_ref, top_ref, weight_ref,
):
    rows, cols = k_ref.shape[1], k_ref.shape[0]
    lines = rows // LANES
    lane, sub = lane_and_sublane()
    lse = joined([recv_ref[d, 0:lines, :] for d in range(recv_ref.shape[0])])
    mass = rm_ref[...]
    la = log2(mass)
    sc = sc_ref[...]
    errs = errs_ref[...]
    if index == 0:
        f_new = la - lse
        mass_b = total(jnp.sum(recv_ref[:, lines : lines + 1, :], axis=0))
        sc = jnp.where(sub == 1, mass_b, 0.0)
        u = f_new + mr_ref[...]
        newest = largest(u)
        high = newest
    else:
        mass_a = sc[0:1, :]
        shift = log2(mass_a)
        f_new = la - shift - lse
        u = f_new + mr_ref[...]
        high = sc[2:3, :]
        f_old = fprev_ref[...]
        share = mass / mass_a
        if index == 1:
            errs = noted(errs, 0, jnp.abs(jnp.exp2(la - f_old) - share))
            f_old = f_old - shift
            high = high - shift
        errs = noted(errs, index, jnp.abs(jnp.exp2(la - shift + (f_old - f_new)) - share))
        newest = largest(u)
    weights = jnp.exp2(u - high)
    for l in range(lines):
        ubc_ref[:, l * LANES : (l + 1) * LANES] = jnp.broadcast_to(weights[l : l + 1, :], (8, LANES))
    together = 8

    def group(t, carry):
        acc = [None] * together
        lines_at = [pl.ds(pl.multiple_of((t * together + q) * 8, 8), 8) for q in range(together)]
        for l in range(lines):
            across = slice(l * LANES, (l + 1) * LANES)
            ul = ubc_ref[:, across]
            for q in range(together):
                term = k_ref[lines_at[q], across] * ul
                acc[q] = term if acc[q] is None else acc[q] + term
        for q in range(together):
            acc_ref[lines_at[q], :] = acc[q]
        return carry

    lax.fori_loop(0, cols // (8 * together), group, 0)
    for t in range(cols // LANES):
        picked = []
        for q in range(LANES // 8):
            at = t * LANES + 8 * q
            full = jnp.sum(acc_ref[at : at + 8, :], axis=1, keepdims=True)
            picked.append(jnp.where(lane == sub + 8 * q, full, 0.0))
        s_ref[t : t + 1, :] = jnp.sum(in_pairs(picked, jnp.add), axis=0, keepdims=True)
    sums = s_ref[...]
    extra = None
    if index == 0:
        extra = jnp.broadcast_to(jnp.sum(mass, axis=0, keepdims=True), (4, LANES))
    elif last:
        extra = jnp.broadcast_to(along_lanes(errs), (4, LANES))
    spread(out_ref, high + log2(sums), extra)
    f_ref[...] = f_new * (eps / LOG2E) if last else f_new
    sc_out_ref[...] = jnp.where(sub == 2, newest, sc)
    errs_out_ref[...] = errs
    least = jnp.min(jnp.where(newest - high <= DRIFT, sums, 0.0))

    @pl.when(jnp.logical_not(least >= SMALLEST))
    def _():
        fx_ref[...] = f_new - xs_ref[...]
        exact_cols(kappa, x_ref, y_ref, fx_ref, s_ref, top_ref, weight_ref)
        spread(out_ref, s_ref[...], extra)


def new_target(index, recv_ref, cm_ref, gprev_ref, sc, errs_ref):
    lines = cm_ref.shape[0]
    lane, sub = lane_and_sublane()
    lse = joined([recv_ref[d, 0:lines, :] for d in range(recv_ref.shape[0])])
    mass_b = sc[1:2, :]
    if index == 0:
        mass_a = total(jnp.sum(recv_ref[:, lines : lines + 1, :], axis=0))
        lse = lse - log2(mass_a)
        sc = jnp.where(sub == 0, mass_a, sc)
    mass = cm_ref[...]
    lb = log2(mass) - log2(mass_b)
    g_new = lb - lse
    errs = noted(errs_ref[...], index, jnp.abs(jnp.exp2(lb + (gprev_ref[...] - g_new)) - mass / mass_b))
    return g_new, sc, errs


def row_kernel(
    kappa, index,
    recv_ref, cm_ref, gprev_ref, mr_ref, xs_ref, sc_ref, errs_ref, k_ref, x_ref, y_ref,
    g_ref, sc_out_ref, errs_out_ref, out_ref,
    vbc_ref, r_ref, l_ref,
):
    rows, cols = k_ref.shape[1], k_ref.shape[0]
    lines = rows // LANES
    lane, sub = lane_and_sublane()
    sc = sc_ref[...]
    g_new, sc, errs = new_target(index, recv_ref, cm_ref, gprev_ref, sc, errs_ref)
    newest = largest(g_new)
    high = newest if index == 0 else sc[3:4, :]

    def put(at, piece):
        vbc_ref[at : at + 8, :] = piece

    column_form(jnp.exp2(g_new - high), put)
    together, block = min(16, lines), 32

    for first in range(0, lines, together):

        def group(b, acc, first=first):
            acc = list(acc)
            for j in range(block // 8):
                line = pl.ds(pl.multiple_of(b * block + 8 * j, 8), 8)
                vj = vbc_ref[line, :]
                for t in range(together):
                    across = slice((first + t) * LANES, (first + t + 1) * LANES)
                    acc[t] = acc[t] + k_ref[line, across] * vj
            return tuple(acc)

        acc = lax.fori_loop(0, cols // block, group, (jnp.zeros((8, LANES), f32),) * together)
        for t in range(together):
            r_ref[first + t : first + t + 1, :] = jnp.sum(acc[t], axis=0, keepdims=True)
    sums = r_ref[...]
    spread(out_ref, mr_ref[...] + (high + log2(sums)), None)
    g_ref[...] = g_new
    sc_out_ref[...] = jnp.where(sub == 3, newest, sc)
    errs_out_ref[...] = errs
    least = jnp.min(jnp.where(newest - high <= DRIFT, sums, 0.0))

    @pl.when(jnp.logical_not(least >= SMALLEST))
    def _():
        column_form(g_new, put)
        exact_rows(kappa, x_ref, y_ref, vbc_ref, xs_ref, l_ref)
        spread(out_ref, l_ref[...], None)


def last_kernel(index, recv_ref, cm_ref, gprev_ref, sc_ref, errs_ref, g_ref, row_ref, out_ref):
    lines = cm_ref.shape[0]
    g_new, sc, errs = new_target(index, recv_ref, cm_ref, gprev_ref, sc_ref[...], errs_ref)
    g_ref[...] = g_new * (eps / LOG2E)
    row_ref[...] = jnp.broadcast_to(jnp.sum(recv_ref[:, lines : lines + 1, :], axis=0), (8, LANES))
    col_errs = jnp.broadcast_to(along_lanes(errs), (8, LANES))
    for d in range(out_ref.shape[0]):
        out_ref[d] = col_errs


def on_chip():
    return pl.BlockSpec(memory_space=pltpu.VMEM)


def call(kernel, args, outs, scratch, limit, name):
    return pl.pallas_call(
        kernel,
        in_specs=[on_chip() for _ in args],
        out_specs=[on_chip() for _ in outs],
        out_shape=[jax.ShapeDtypeStruct(shape, f32) for shape in outs],
        scratch_shapes=[pltpu.VMEM(shape, f32) for shape in scratch],
        compiler_params=pltpu.CompilerParams(vmem_limit_bytes=limit),
        name=name,
    )(*args)


def exchange(x, axis):
    return lax.all_to_all(x, axis, split_axis=0, concat_axis=0, tiled=True)


def on_device(row_embed, col_embed, row_mass, col_mass):
    rows, width = row_embed.shape
    cols = col_embed.shape[0]
    kappa = LOG2E / (width * eps)
    row_lines, col_lines = rows // LANES, cols // LANES
    by_col = lax.axis_size(COLS_OVER)
    by_row = lax.axis_size(ROWS_OVER)
    rm = row_mass.reshape(row_lines, LANES)
    cm = col_mass.reshape(col_lines, LANES)
    tile = (8, LANES)
    mib = 1 << 20
    given = (row_embed, col_embed, rm, cm)
    blocks = [(cols, rows), (row_lines, LANES), (row_lines, LANES), (by_col, row_lines + 8, LANES)]
    row_embed, col_embed, rm, cm, k, mr, xs, out = pl.pallas_call(
        functools.partial(init_kernel, kappa),
        in_specs=[pl.BlockSpec(memory_space=pl.ANY) for _ in given],
        out_specs=[on_chip() for _ in range(len(given) + len(blocks))],
        out_shape=[jax.ShapeDtypeStruct(x.shape, x.dtype) for x in given]
        + [jax.ShapeDtypeStruct(shape, f32) for shape in blocks],
        scratch_shapes=[
            pltpu.VMEM((cols, LANES), f32),
            pltpu.VMEM((row_lines, LANES), f32),
            pltpu.SemaphoreType.DMA((len(given),)),
        ],
        compiler_params=pltpu.CompilerParams(vmem_limit_bytes=24 * mib),
        name="init",
    )(*given)
    f_pot = jnp.zeros((row_lines, LANES), f32)
    g_pot = jnp.zeros((col_lines, LANES), f32)
    sc = jnp.zeros(tile, f32)
    noting = (16, LANES)
    row_errs = jnp.zeros(noting, f32)
    col_errs = jnp.zeros(noting, f32)
    for index in range(ITERS):
        last = index == ITERS - 1
        got = exchange(out, COLS_OVER)
        more = 4 if index == 0 or last else 0
        f_pot, sc, row_errs, out = call(
            functools.partial(col_kernel, kappa, index, last),
            (got, rm, f_pot, mr, xs, sc, row_errs, k, row_embed, col_embed),
            [(row_lines, LANES), tile, noting, (by_row, col_lines + more, LANES)],
            [(8, rows), (cols, LANES), (col_lines, LANES), (row_lines, LANES), (cols, LANES), (cols, LANES)],
            24 * mib, f"cols{index}",
        )
        got = exchange(out, ROWS_OVER)
        if last:
            break
        g_pot, sc, col_errs, out = call(
            functools.partial(row_kernel, kappa, index),
            (got, cm, g_pot, mr, xs, sc, col_errs, k, row_embed, col_embed),
            [(col_lines, LANES), tile, noting, (by_col, row_lines, LANES)],
            [(cols, LANES), (row_lines, LANES), (row_lines, LANES)],
            24 * mib, f"rows{index}",
        )
    g_out, row_errs, out = call(
        functools.partial(last_kernel, ITERS - 1),
        (got, cm, g_pot, sc, col_errs),
        [(col_lines, LANES), tile, (by_col, 8, LANES)],
        [], 8 * mib, "finish",
    )
    got, row_errs = lax.optimization_barrier((exchange(out, COLS_OVER), row_errs))
    col_vec = jnp.sum(got[:, 0, :ITERS], axis=0)
    errors = jnp.stack([row_errs[0, :ITERS], col_vec], axis=1)
    return f_pot.reshape(rows), g_out.reshape(cols), errors


def solution(mesh):
    return jax.shard_map(
        on_device,
        mesh=mesh,
        in_specs=(P(ROWS_OVER, None), P(COLS_OVER, None), P(ROWS_OVER), P(COLS_OVER)),
        out_specs=(P(ROWS_OVER), P(COLS_OVER), P()),
        check_vma=False,
    )
```

time: 500 us -> 514 us (1.028)
  blocking collectives: 214 us -> 236 us
  Pallas kernels: 257 us -> 272 us
  waiting for transfers between devices: 13.5 us -> 0 us
  starting transfers between devices: 9.18 us -> 0 us
    pallas_call x0 -> x1, Pallas kernels: none -> 28.6 us  [on_device(): pl.pallas_call(functools.partial(init_kernel, kappa), in_specs=[pl.BlockS...]
    all_to_all x19 -> x21, blocking collectives: 214 us -> 236 us  [exchange(): return lax.all_to_all(x, axis, split_axis=0, concat_axis=0, tiled=True)]
    all_to_all x2 -> x0, waiting for transfers between devices: 13.5 us -> none  [exchange(): return lax.all_to_all(x, axis, split_axis=0, concat_axis=0, tiled=True)]
    pallas_call x21 -> x20, Pallas kernels: 257 us -> 244 us  [call(): pl.pallas_call(kernel, in_specs=[on_chip() for _ in args], out_specs=[on_...]
    all_to_all x2 -> x0, starting transfers between devices: 9.18 us -> none  [exchange(): return lax.all_to_all(x, axis, split_axis=0, concat_axis=0, tiled=True)]
  transfers between devices with their start and end apart: 2 -> 0, of which waited for: 2 -> 0; matrix products, arithmetic and copies ran while one was open for 0% -> 0% of each run, Pallas kernels for 0% -> 0%
where the time goes in v2:
time: 514 us; the launch traced here: 513 us
  Pallas kernels  272 us (53%)
  blocking collectives  236 us (46%)
    pallas_call x20, Pallas kernels, call(): pl.pallas_call(kernel, in_specs=[on_chip() for _ in args], out_specs=[on_...  244 us
    all_to_all x21, blocking collectives, exchange(): return lax.all_to_all(x, axis, split_axis=0, concat_axis=0, tiled=True)  236 us
    pallas_call x1, Pallas kernels, on_device(): pl.pallas_call(functools.partial(init_kernel, kappa), in_specs=[pl.BlockS...  28.6 us

profile of v2, /device:TPU:1, one launch (start us, length us, event | category | flops | bytes accessed | tf_op | source)
XLA Modules:
  0.0 512.7 jit_solution(12903098098754042074)
XLA Ops:
  4.2 28.6 %init.1 = (bf16[4096,128]{1,0:T(8,128)(2,1)S(1)}, bf16[512,128]{1,0:T(8,128)(2,1)S(1)}, f32[32,128]{1,0:T(8,128)S(1)}, f32[4,128]{1,0:T(4,128)S(1)}, f32[512,409...) custom-call(bf16[4096,128]{1,0:T(8,128)(2,1)S(1)} %copy-done, ...), custom_call_target="tpu_custom_call" | custom-call | tf_op jit(solution)/shard_map/init/pallas_call | solution.py:392
  32.8 11.3 %all_to_all.105.recv_ref = f32[8,40,128]{2,1,0:T(8,128)S(1)} all-to-all(f32[8,40,128]{2,1,0:T(8,128)S(1)} %get-tuple-element.91), channel_id=1, replica_groups=mesh['gx'=8,'gz'=4,'gy'=8] {'gy'}, dimensions={0} | all-to-all | bytes 327680 | tf_op jit(solution)/shard_map/all_to_all | solution.py:376
  44.1 14.1 %cols0.1 = (f32[32,128]{1,0:T(8,128)S(1)}, f32[8,128]{1,0:T(8,128)S(1)}, f32[16,128]{1,0:T(8,128)S(1)}, f32[32,8,128]{2,1,0:T(8,128)S(1)}) custom-call(f32[8,40,128]{2,1,0:T(8,128)S(1)} %all_to_all.105.recv_ref, f32[32,128]{1,0:T(8,128)S(1)} %get-tuple-element.92.rm_ref, f32[32,128]{1,0:T(8,128)S(1)} %broadcast_in_dim.9.fprev_ref, ...), custom_call_target="tpu_custom_call" | custom-call | tf_op jit(solution)/shard_map/cols0/pallas_call | solution.py:364
  58.2 20.2 %all_to_all.106.recv_ref = f32[32,8,128]{2,1,0:T(8,128)S(1)} all-to-all(f32[32,8,128]{2,1,0:T(8,128)S(1)} %get-tuple-element.98), channel_id=1, replica_groups=mesh['gx'=8,'gz'=4,'gy'=8] {'gx','gz'}, dimensions={0} | all-to-all | bytes 262144 | tf_op jit(solution)/shard_map/all_to_all | solution.py:376
  78.4 11.4 %rows0.1 = (f32[4,128]{1,0:T(4,128)S(1)}, f32[8,128]{1,0:T(8,128)S(1)}, f32[16,128]{1,0:T(8,128)S(1)}, f32[8,32,128]{2,1,0:T(8,128)S(1)}) custom-call(f32[32,8,128]{2,1,0:T(8,128)S(1)} %all_to_all.106.recv_ref, f32[4,128]{1,0:T(4,128)S(1)} %get-tuple-element.99.cm_ref, f32[4,128]{1,0:T(4,128)S(1)} %broadcast_in_dim.11.gprev_ref, ...), custom_call_target="tpu_custom_call" | custom-call | tf_op jit(solution)/shard_map/rows0/pallas_call | solution.py:364
  99.8 14.1 %cols1.1 = (f32[32,128]{1,0:T(8,128)S(1)}, f32[8,128]{1,0:T(8,128)S(1)}, f32[16,128]{1,0:T(8,128)S(1)}, f32[32,4,128]{2,1,0:T(4,128)S(1)}) custom-call(f32[8,32,128]{2,1,0:T(8,128)S(1)} %all_to_all.107.recv_ref, f32[32,128]{1,0:T(8,128)S(1)} %get-tuple-element.92.rm_ref, f32[32,128]{1,0:T(8,128)S(1)} %get-tuple-element.102.fprev_ref, ...), custom_call_target="tpu_custom_call" | custom-call | tf_op jit(solution)/shard_map/cols1/pallas_call | solution.py:364
  114.0 11.8 %all_to_all.108.recv_ref = f32[32,4,128]{2,1,0:T(4,128)S(1)} all-to-all(f32[32,4,128]{2,1,0:T(4,128)S(1)} %get-tuple-element.105), channel_id=1, replica_groups=mesh['gx'=8,'gz'=4,'gy'=8] {'gx','gz'}, dimensions={0} | all-to-all | bytes 131072 | tf_op jit(solution)/shard_map/all_to_all | solution.py:376
  125.7 11.3 %rows1.1 = (f32[4,128]{1,0:T(4,128)S(1)}, f32[8,128]{1,0:T(8,128)S(1)}, f32[16,128]{1,0:T(8,128)S(1)}, f32[8,32,128]{2,1,0:T(8,128)S(1)}) custom-call(f32[32,4,128]{2,1,0:T(4,128)S(1)} %all_to_all.108.recv_ref, f32[4,128]{1,0:T(4,128)S(1)} %get-tuple-element.99.cm_ref, f32[4,128]{1,0:T(4,128)S(1)} %get-tuple-element.106.gprev_ref, ...), custom_call_target="tpu_custom_call" | custom-call | tf_op jit(solution)/shard_map/rows1/pallas_call | solution.py:364
  146.9 14.0 %cols2.1 = (f32[32,128]{1,0:T(8,128)S(1)}, f32[8,128]{1,0:T(8,128)S(1)}, f32[16,128]{1,0:T(8,128)S(1)}, f32[32,4,128]{2,1,0:T(4,128)S(1)}) custom-call(f32[8,32,128]{2,1,0:T(8,128)S(1)} %all_to_all.109.recv_ref, f32[32,128]{1,0:T(8,128)S(1)} %get-tuple-element.92.rm_ref, f32[32,128]{1,0:T(8,128)S(1)} %get-tuple-element.110.fprev_ref, ...), custom_call_target="tpu_custom_call" | custom-call | tf_op jit(solution)/shard_map/cols2/pallas_call | solution.py:364
  161.0 11.8 %all_to_all.110.recv_ref = f32[32,4,128]{2,1,0:T(4,128)S(1)} all-to-all(f32[32,4,128]{2,1,0:T(4,128)S(1)} %get-tuple-element.113), channel_id=1, replica_groups=mesh['gx'=8,'gz'=4,'gy'=8] {'gx','gz'}, dimensions={0} | all-to-all | bytes 131072 | tf_op jit(solution)/shard_map/all_to_all | solution.py:376
  193.9 14.0 %cols3.1 = (f32[32,128]{1,0:T(8,128)S(1)}, f32[8,128]{1,0:T(8,128)S(1)}, f32[16,128]{1,0:T(8,128)S(1)}, f32[32,4,128]{2,1,0:T(4,128)S(1)}) custom-call(f32[8,32,128]{2,1,0:T(8,128)S(1)} %all_to_all.111.recv_ref, f32[32,128]{1,0:T(8,128)S(1)} %get-tuple-element.92.rm_ref, f32[32,128]{1,0:T(8,128)S(1)} %get-tuple-element.118.fprev_ref, ...), custom_call_target="tpu_custom_call" | custom-call | tf_op jit(solution)/shard_map/cols3/pallas_call | solution.py:364
  207.9 11.8 %all_to_all.112.recv_ref = f32[32,4,128]{2,1,0:T(4,128)S(1)} all-to-all(f32[32,4,128]{2,1,0:T(4,128)S(1)} %get-tuple-element.121), channel_id=1, replica_groups=mesh['gx'=8,'gz'=4,'gy'=8] {'gx','gz'}, dimensions={0} | all-to-all | bytes 131072 | tf_op jit(solution)/shard_map/all_to_all | solution.py:376
  240.8 14.0 %cols4.1 = (f32[32,128]{1,0:T(8,128)S(1)}, f32[8,128]{1,0:T(8,128)S(1)}, f32[16,128]{1,0:T(8,128)S(1)}, f32[32,4,128]{2,1,0:T(4,128)S(1)}) custom-call(f32[8,32,128]{2,1,0:T(8,128)S(1)} %all_to_all.113.recv_ref, f32[32,128]{1,0:T(8,128)S(1)} %get-tuple-element.92.rm_ref, f32[32,128]{1,0:T(8,128)S(1)} %get-tuple-element.126.fprev_ref, ...), custom_call_target="tpu_custom_call" | custom-call | tf_op jit(solution)/shard_map/cols4/pallas_call | solution.py:364
  254.8 11.8 %all_to_all.114.recv_ref = f32[32,4,128]{2,1,0:T(4,128)S(1)} all-to-all(f32[32,4,128]{2,1,0:T(4,128)S(1)} %get-tuple-element.129), channel_id=1, replica_groups=mesh['gx'=8,'gz'=4,'gy'=8] {'gx','gz'}, dimensions={0} | all-to-all | bytes 131072 | tf_op jit(solution)/shard_map/all_to_all | solution.py:376
  287.7 14.0 %cols5.1 = (f32[32,128]{1,0:T(8,128)S(1)}, f32[8,128]{1,0:T(8,128)S(1)}, f32[16,128]{1,0:T(8,128)S(1)}, f32[32,4,128]{2,1,0:T(4,128)S(1)}) custom-call(f32[8,32,128]{2,1,0:T(8,128)S(1)} %all_to_all.115.recv_ref, f32[32,128]{1,0:T(8,128)S(1)} %get-tuple-element.92.rm_ref, f32[32,128]{1,0:T(8,128)S(1)} %get-tuple-element.134.fprev_ref, ...), custom_call_target="tpu_custom_call" | custom-call | tf_op jit(solution)/shard_map/cols5/pallas_call | solution.py:364
  301.7 11.8 %all_to_all.116.recv_ref = f32[32,4,128]{2,1,0:T(4,128)S(1)} all-to-all(f32[32,4,128]{2,1,0:T(4,128)S(1)} %get-tuple-element.137), channel_id=1, replica_groups=mesh['gx'=8,'gz'=4,'gy'=8] {'gx','gz'}, dimensions={0} | all-to-all | bytes 131072 | tf_op jit(solution)/shard_map/all_to_all | solution.py:376
  334.6 14.0 %cols6.1 = (f32[32,128]{1,0:T(8,128)S(1)}, f32[8,128]{1,0:T(8,128)S(1)}, f32[16,128]{1,0:T(8,128)S(1)}, f32[32,4,128]{2,1,0:T(4,128)S(1)}) custom-call(f32[8,32,128]{2,1,0:T(8,128)S(1)} %all_to_all.117.recv_ref, f32[32,128]{1,0:T(8,128)S(1)} %get-tuple-element.92.rm_ref, f32[32,128]{1,0:T(8,128)S(1)} %get-tuple-element.142.fprev_ref, ...), custom_call_target="tpu_custom_call" | custom-call | tf_op jit(solution)/shard_map/cols6/pallas_call | solution.py:364
  348.6 11.8 %all_to_all.118.recv_ref = f32[32,4,128]{2,1,0:T(4,128)S(1)} all-to-all(f32[32,4,128]{2,1,0:T(4,128)S(1)} %get-tuple-element.145), channel_id=1, replica_groups=mesh['gx'=8,'gz'=4,'gy'=8] {'gx','gz'}, dimensions={0} | all-to-all | bytes 131072 | tf_op jit(solution)/shard_map/all_to_all | solution.py:376
  381.5 14.0 %cols7.1 = (f32[32,128]{1,0:T(8,128)S(1)}, f32[8,128]{1,0:T(8,128)S(1)}, f32[16,128]{1,0:T(8,128)S(1)}, f32[32,4,128]{2,1,0:T(4,128)S(1)}) custom-call(f32[8,32,128]{2,1,0:T(8,128)S(1)} %all_to_all.119.recv_ref, f32[32,128]{1,0:T(8,128)S(1)} %get-tuple-element.92.rm_ref, f32[32,128]{1,0:T(8,128)S(1)} %get-tuple-element.150.fprev_ref, ...), custom_call_target="tpu_custom_call" | custom-call | tf_op jit(solution)/shard_map/cols7/pallas_call | solution.py:364
  395.5 11.8 %all_to_all.120.recv_ref = f32[32,4,128]{2,1,0:T(4,128)S(1)} all-to-all(f32[32,4,128]{2,1,0:T(4,128)S(1)} %get-tuple-element.153), channel_id=1, replica_groups=mesh['gx'=8,'gz'=4,'gy'=8] {'gx','gz'}, dimensions={0} | all-to-all | bytes 131072 | tf_op jit(solution)/shard_map/all_to_all | solution.py:376
  428.4 14.1 %cols8.1 = (f32[32,128]{1,0:T(8,128)S(1)}, f32[8,128]{1,0:T(8,128)S(1)}, f32[16,128]{1,0:T(8,128)S(1)}, f32[32,4,128]{2,1,0:T(4,128)S(1)}) custom-call(f32[8,32,128]{2,1,0:T(8,128)S(1)} %all_to_all.121.recv_ref, f32[32,128]{1,0:T(8,128)S(1)} %get-tuple-element.92.rm_ref, f32[32,128]{1,0:T(8,128)S(1)} %get-tuple-element.158.fprev_ref, ...), custom_call_target="tpu_custom_call" | custom-call | tf_op jit(solution)/shard_map/cols8/pallas_call | solution.py:364
  442.5 11.8 %all_to_all.122.recv_ref = f32[32,4,128]{2,1,0:T(4,128)S(1)} all-to-all(f32[32,4,128]{2,1,0:T(4,128)S(1)} %get-tuple-element.161), channel_id=1, replica_groups=mesh['gx'=8,'gz'=4,'gy'=8] {'gx','gz'}, dimensions={0} | all-to-all | bytes 131072 | tf_op jit(solution)/shard_map/all_to_all | solution.py:376
  475.3 14.6 %cols9.1 = (f32[32,128]{1,0:T(8,128)}, f32[8,128]{1,0:T(8,128)S(1)}, f32[16,128]{1,0:T(8,128)}, f32[32,8,128]{2,1,0:T(8,128)S(1)}) custom-call(f32[8,32,128]{2,1,0:T(8,128)S(1)} %all_to_all.123.recv_ref, f32[32,128]{1,0:T(8,128)S(1)} %get-tuple-element.92.rm_ref, f32[32,128]{1,0:T(8,128)S(1)} %get-tuple-element.166.fprev_ref, ...), custom_call_target="tpu_custom_call" | custom-call | tf_op jit(solution)/shard_map/cols9/pallas_call | solution.py:364
  490.0 12.4 %all_to_all.124.recv_ref = f32[32,8,128]{2,1,0:T(8,128)S(1)} all-to-all(f32[32,8,128]{2,1,0:T(8,128)S(1)} %get-tuple-element.170), channel_id=1, replica_groups=mesh['gx'=8,'gz'=4,'gy'=8] {'gx','gz'}, dimensions={0} | all-to-all | bytes 262144 | tf_op jit(solution)/shard_map/all_to_all | solution.py:376
  (33 shorter events, 180.9 us)
Async XLA Ops:
  0.6 1.2 copy-start
  1.9 0.9 copy-start.1
  2.8 0.7 copy-start.2
  3.5 0.7 copy-start.3

commit v3 on v2

--- a/solution.py
+++ b/solution.py
@@ -87,74 +87,44 @@
     return jnp.sum(picked, axis=0, keepdims=True)
 
 
-def init_kernel(
-    kappa, x_hbm, y_hbm, rm_hbm, cm_hbm,
-    x_ref, y_ref, rm_ref, cm_ref, k_ref, mr_ref, xs_ref, out_ref, half_ref, l_ref, sems,
-):
-    pairs = ((y_hbm, y_ref), (x_hbm, x_ref), (cm_hbm, cm_ref), (rm_hbm, rm_ref))
-    copies = [pltpu.make_async_copy(src, dst, sems.at[i]) for i, (src, dst) in enumerate(pairs)]
-    for copy in copies:
-        copy.start()
+def init_kernel(kappa, x_ref, y_ref, cm_ref, k_ref, mr_ref, xs_ref, out_ref, cs_ref, l_ref):
     cols = y_ref.shape[0]
     rows = x_ref.shape[0]
-    wide, block = 512, 64
-    tiles = wide // LANES
-    copies[0].wait()
-    half_ref[...] = jnp.broadcast_to(scaled_norms(y_ref[...], 0.5), (cols, LANES))
+    wide = 512
+    cs_ref[...] = jnp.broadcast_to(scaled_norms(y_ref[...], kappa), (cols, LANES))
     ones = jnp.ones((8, x_ref.shape[1]), f32)
-    copies[1].wait()
 
     def chunk(c, carry):
         at = pl.multiple_of(c * wide, wide)
         xb = x_ref[pl.ds(at, wide), :]
-        k_ref[:, pl.ds(at, wide)] = cross_of(y_ref[...], xb)
+        k_ref[:, pl.ds(at, wide)] = cross_of(y_ref[...], xb) * (2.0 * kappa)
         xf = xb.astype(f32)
         norms = kappa * lax.dot_general(
             ones, xf * xf, (((1,), (1,)), ((), ())),
             precision=lax.Precision.HIGHEST, preferred_element_type=f32,
         )
-        here = [pl.ds(pl.multiple_of(at + t * LANES, LANES), LANES) for t in range(tiles)]
-
-        def highest(b, tops):
-            tops = list(tops)
-            for j in range(block // 8):
-                line = pl.ds(pl.multiple_of(b * block + 8 * j, 8), 8)
-                half = half_ref[line, :]
-                for t in range(tiles):
-                    z = k_ref[line, here[t]] - half
-                    k_ref[line, here[t]] = z
-                    tops[t] = jnp.maximum(tops[t], z)
-            return tuple(tops)
-
-        low = jnp.full((8, LANES), -jnp.inf, f32)
-        tops = lax.fori_loop(0, cols // block, highest, (low,) * tiles)
-        tops = [jnp.max(top, axis=0, keepdims=True) for top in tops]
-        spans = [jnp.broadcast_to(top, (8, LANES)) for top in tops]
-
-        def weigh(b, sums):
-            sums = list(sums)
-            for j in range(block // 8):
-                line = pl.ds(pl.multiple_of(b * block + 8 * j, 8), 8)
-                for t in range(tiles):
-                    e = jnp.exp2((k_ref[line, here[t]] - spans[t]) * (2.0 * kappa))
-                    k_ref[line, here[t]] = e
-                    sums[t] = sums[t] + e
-            return tuple(sums)
-
-        sums = lax.fori_loop(0, cols // block, weigh, (jnp.zeros((8, LANES), f32),) * tiles)
-        for t in range(tiles):
-            weight = jnp.sum(sums[t], axis=0, keepdims=True)
+        for t in range(wide // LANES):
+            here = pl.ds(pl.multiple_of(at + t * LANES, LANES), LANES)
+            tops = [None] * 4
+            for j in range(cols // 8):
+                z = k_ref[8 * j : 8 * j + 8, here] - cs_ref[8 * j : 8 * j + 8, :]
+                tops[j % 4] = z if tops[j % 4] is None else jnp.maximum(tops[j % 4], z)
+            top = jnp.maximum(jnp.maximum(tops[0], tops[1]), jnp.maximum(tops[2], tops[3]))
+            top = jnp.max(top, axis=0, keepdims=True)
+            sums = [None] * 4
+            for j in range(cols // 8):
+                e = jnp.exp2(k_ref[8 * j : 8 * j + 8, here] - cs_ref[8 * j : 8 * j + 8, :] - top)
+                k_ref[8 * j : 8 * j + 8, here] = e
+                sums[j % 4] = e if sums[j % 4] is None else sums[j % 4] + e
+            weight = jnp.sum((sums[0] + sums[1]) + (sums[2] + sums[3]), axis=0, keepdims=True)
             norm = norms[0:1, t * LANES : (t + 1) * LANES]
-            line = pl.ds(c * tiles + t, 1)
-            base = tops[t] * (2.0 * kappa) - norm
+            line = pl.ds(c * (wide // LANES) + t, 1)
             xs_ref[line, :] = norm
-            mr_ref[line, :] = base
-            l_ref[line, :] = base + log2(weight)
+            mr_ref[line, :] = top - norm
+            l_ref[line, :] = (top - norm) + log2(weight)
         return carry
 
     lax.fori_loop(0, rows // wide, chunk, 0)
-    copies[2].wait()
-    copies[3].wait()
     mass = jnp.broadcast_to(jnp.sum(cm_ref[...], axis=0, keepdims=True), (8, LANES))
     spread(out_ref, l_ref[...], mass)
 
@@ -205,7 +175,7 @@
     kappa, index, last,
     recv_ref, rm_ref, fprev_ref, mr_ref, xs_ref, sc_ref, errs_ref, k_ref, x_ref, y_ref,
     f_ref, sc_out_ref, errs_out_ref, out_ref,
-    ubc_ref, acc_ref, s_ref, fx_ref, top_ref, weight_ref,
+    acc_ref, s_ref, fx_ref, top_ref, weight_ref,
 ):
     rows, cols = k_ref.shape[1], k_ref.shape[0]
     lines = rows // LANES
@@ -237,19 +207,19 @@
         errs = noted(errs, index, jnp.abs(jnp.exp2(la - shift + (f_old - f_new)) - share))
         newest = largest(u)
     weights = jnp.exp2(u - high)
-    for l in range(lines):
-        ubc_ref[:, l * LANES : (l + 1) * LANES] = jnp.broadcast_to(weights[l : l + 1, :], (8, LANES))
+    us = [jnp.broadcast_to(weights[l : l + 1, :], (8, LANES)) for l in range(lines)]
     together = 8
 
     def group(t, carry):
         acc = [None] * together
         lines_at = [pl.ds(pl.multiple_of((t * together + q) * 8, 8), 8) for q in range(together)]
-        for l in range(lines):
-            across = slice(l * LANES, (l + 1) * LANES)
-            ul = ubc_ref[:, across]
-            for q in range(together):
-                term = k_ref[lines_at[q], across] * ul
-                acc[q] = term if acc[q] is None else acc[q] + term
+        for q in range(together):
+            parts = [None] * 2
+            for l in range(lines):
+                across = slice(l * LANES, (l + 1) * LANES)
+                term = k_ref[lines_at[q], across] * us[l]
+                parts[l % 2] = term if parts[l % 2] is None else parts[l % 2] + term
+            acc[q] = parts[0] + parts[1]
         for q in range(together):
             acc_ref[lines_at[q], :] = acc[q]
         return carry
@@ -315,7 +285,7 @@
         vbc_ref[at : at + 8, :] = piece
 
     column_form(jnp.exp2(g_new - high), put)
-    together, block = min(16, lines), 32
+    together, block = min(16, lines), 64
 
     for first in range(0, lines, together):
 
@@ -387,22 +357,13 @@
     cm = col_mass.reshape(col_lines, LANES)
     tile = (8, LANES)
     mib = 1 << 20
-    given = (row_embed, col_embed, rm, cm)
-    blocks = [(cols, rows), (row_lines, LANES), (row_lines, LANES), (by_col, row_lines + 8, LANES)]
-    row_embed, col_embed, rm, cm, k, mr, xs, out = pl.pallas_call(
+    k, mr, xs, out = call(
         functools.partial(init_kernel, kappa),
-        in_specs=[pl.BlockSpec(memory_space=pl.ANY) for _ in given],
-        out_specs=[on_chip() for _ in range(len(given) + len(blocks))],
-        out_shape=[jax.ShapeDtypeStruct(x.shape, x.dtype) for x in given]
-        + [jax.ShapeDtypeStruct(shape, f32) for shape in blocks],
-        scratch_shapes=[
-            pltpu.VMEM((cols, LANES), f32),
-            pltpu.VMEM((row_lines, LANES), f32),
-            pltpu.SemaphoreType.DMA((len(given),)),
-        ],
-        compiler_params=pltpu.CompilerParams(vmem_limit_bytes=24 * mib),
-        name="init",
-    )(*given)
+        (row_embed, col_embed, cm),
+        [(cols, rows), (row_lines, LANES), (row_lines, LANES), (by_col, row_lines + 8, LANES)],
+        [(cols, LANES), (row_lines, LANES)],
+        24 * mib, "init",
+    )
     f_pot = jnp.zeros((row_lines, LANES), f32)
     g_pot = jnp.zeros((col_lines, LANES), f32)
     sc = jnp.zeros(tile, f32)
@@ -417,7 +378,7 @@
             functools.partial(col_kernel, kappa, index, last),
             (got, rm, f_pot, mr, xs, sc, row_errs, k, row_embed, col_embed),
             [(row_lines, LANES), tile, noting, (by_row, col_lines + more, LANES)],
-            [(8, rows), (cols, LANES), (col_lines, LANES), (row_lines, LANES), (cols, LANES), (cols, LANES)],
+            [(cols, LANES), (col_lines, LANES), (row_lines, LANES), (cols, LANES), (cols, LANES)],
             24 * mib, f"cols{index}",
         )
         got = exchange(out, ROWS_OVER)

time: 514 us -> 485 us (0.944)
  Pallas kernels: 272 us -> 243 us
    pallas_call x1 -> x0, Pallas kernels: 28.6 us -> none  [on_device(): pl.pallas_call(functools.partial(init_kernel, kappa), in_specs=[pl.BlockS...]
    pallas_call x20 -> x21, Pallas kernels: 244 us -> 243 us  [call(): pl.pallas_call(kernel, in_specs=[on_chip() for _ in args], out_specs=[on_...]
where the time goes in v3:
time: 485 us; the launch traced here: 484 us
  Pallas kernels  243 us (50%)
  blocking collectives  236 us (49%)
    pallas_call x21, Pallas kernels, call(): pl.pallas_call(kernel, in_specs=[on_chip() for _ in args], out_specs=[on_...  243 us
    all_to_all x21, blocking collectives, exchange(): return lax.all_to_all(x, axis, split_axis=0, concat_axis=0, tiled=True)  236 us

profile of v3, /device:TPU:1, one launch (start us, length us, event | category | flops | bytes accessed | tf_op | source)
XLA Modules:
  0.0 484.4 jit_solution(8111595976624325802)
XLA Ops:
  9.1 11.3 %all_to_all.105.recv_ref = f32[8,40,128]{2,1,0:T(8,128)S(1)} all-to-all(f32[8,40,128]{2,1,0:T(8,128)S(1)} %get-tuple-element.87), channel_id=1, replica_groups=mesh['gx'=8,'gz'=4,'gy'=8] {'gy'}, dimensions={0} | all-to-all | bytes 327680 | tf_op jit(solution)/shard_map/all_to_all | solution.py:346
  21.1 13.7 %cols0.1 = (f32[32,128]{1,0:T(8,128)S(1)}, f32[8,128]{1,0:T(8,128)S(1)}, f32[16,128]{1,0:T(8,128)S(1)}, f32[32,8,128]{2,1,0:T(8,128)S(1)}) custom-call(f32[8,40,128]{2,1,0:T(8,128)S(1)} %all_to_all.105.recv_ref, f32[32,128]{1,0:T(8,128)S(1)} %bitcast.7, f32[32,128]{1,0:T(8,128)S(1)} %broadcast_in_dim.9.fprev_ref, f32[32,128]{1,0:T(8,128)S(1)} %get-tuple-element.88.mr_ref, ...), custom_call_target="tpu_custom_call" | custom-call | tf_op jit(solution)/shard_map/cols0/pallas_call | solution.py:334
  34.8 20.2 %all_to_all.106.recv_ref = f32[32,8,128]{2,1,0:T(8,128)S(1)} all-to-all(f32[32,8,128]{2,1,0:T(8,128)S(1)} %get-tuple-element.91), channel_id=1, replica_groups=mesh['gx'=8,'gz'=4,'gy'=8] {'gx','gz'}, dimensions={0} | all-to-all | bytes 262144 | tf_op jit(solution)/shard_map/all_to_all | solution.py:346
  55.0 11.3 %rows0.1 = (f32[4,128]{1,0:T(4,128)S(1)}, f32[8,128]{1,0:T(8,128)S(1)}, f32[16,128]{1,0:T(8,128)S(1)}, f32[8,32,128]{2,1,0:T(8,128)S(1)}) custom-call(f32[32,8,128]{2,1,0:T(8,128)S(1)} %all_to_all.106.recv_ref, f32[4,128]{1,0:T(4,128)S(1)} %bitcast.18, f32[4,128]{1,0:T(4,128)S(1)} %broadcast_in_dim.11.gprev_ref, f32[32,128]{1,0:T(8,128)S(1)} %get-tuple-element.88.mr_ref, ...), custom_call_target="tpu_custom_call" | custom-call | tf_op jit(solution)/shard_map/rows0/pallas_call | solution.py:334
  76.3 13.7 %cols1.1 = (f32[32,128]{1,0:T(8,128)S(1)}, f32[8,128]{1,0:T(8,128)S(1)}, f32[16,128]{1,0:T(8,128)S(1)}, f32[32,4,128]{2,1,0:T(4,128)S(1)}) custom-call(f32[8,32,128]{2,1,0:T(8,128)S(1)} %all_to_all.107.recv_ref, f32[32,128]{1,0:T(8,128)S(1)} %bitcast.8, f32[32,128]{1,0:T(8,128)S(1)} %get-tuple-element.94.fprev_ref, f32[32,128]{1,0:T(8,128)S(1)} %get-tuple-element.88.mr_ref, ...), custom_call_target="tpu_custom_call" | custom-call | tf_op jit(solution)/shard_map/cols1/pallas_call | solution.py:334
  90.0 11.8 %all_to_all.108.recv_ref = f32[32,4,128]{2,1,0:T(4,128)S(1)} all-to-all(f32[32,4,128]{2,1,0:T(4,128)S(1)} %get-tuple-element.97), channel_id=1, replica_groups=mesh['gx'=8,'gz'=4,'gy'=8] {'gx','gz'}, dimensions={0} | all-to-all | bytes 131072 | tf_op jit(solution)/shard_map/all_to_all | solution.py:346
  101.8 11.1 %rows1.1 = (f32[4,128]{1,0:T(4,128)S(1)}, f32[8,128]{1,0:T(8,128)S(1)}, f32[16,128]{1,0:T(8,128)S(1)}, f32[8,32,128]{2,1,0:T(8,128)S(1)}) custom-call(f32[32,4,128]{2,1,0:T(4,128)S(1)} %all_to_all.108.recv_ref, f32[4,128]{1,0:T(4,128)S(1)} %bitcast.19, f32[4,128]{1,0:T(4,128)S(1)} %get-tuple-element.98.gprev_ref, f32[32,128]{1,0:T(8,128)S(1)} %get-tuple-element.88.mr_ref, ...), custom_call_target="tpu_custom_call" | custom-call | tf_op jit(solution)/shard_map/rows1/pallas_call | solution.py:334
  122.8 13.7 %cols2.1 = (f32[32,128]{1,0:T(8,128)S(1)}, f32[8,128]{1,0:T(8,128)S(1)}, f32[16,128]{1,0:T(8,128)S(1)}, f32[32,4,128]{2,1,0:T(4,128)S(1)}) custom-call(f32[8,32,128]{2,1,0:T(8,128)S(1)} %all_to_all.109.recv_ref, f32[32,128]{1,0:T(8,128)S(1)} %bitcast.9, f32[32,128]{1,0:T(8,128)S(1)} %get-tuple-element.102.fprev_ref, f32[32,128]{1,0:T(8,128)S(1)} %get-tuple-element.88.mr_ref, ...), custom_call_target="tpu_custom_call" | custom-call | tf_op jit(solution)/shard_map/cols2/pallas_call | solution.py:334
  136.5 11.8 %all_to_all.110.recv_ref = f32[32,4,128]{2,1,0:T(4,128)S(1)} all-to-all(f32[32,4,128]{2,1,0:T(4,128)S(1)} %get-tuple-element.105), channel_id=1, replica_groups=mesh['gx'=8,'gz'=4,'gy'=8] {'gx','gz'}, dimensions={0} | all-to-all | bytes 131072 | tf_op jit(solution)/shard_map/all_to_all | solution.py:346
  169.1 13.7 %cols3.1 = (f32[32,128]{1,0:T(8,128)S(1)}, f32[8,128]{1,0:T(8,128)S(1)}, f32[16,128]{1,0:T(8,128)S(1)}, f32[32,4,128]{2,1,0:T(4,128)S(1)}) custom-call(f32[8,32,128]{2,1,0:T(8,128)S(1)} %all_to_all.111.recv_ref, f32[32,128]{1,0:T(8,128)S(1)} %bitcast.10, f32[32,128]{1,0:T(8,128)S(1)} %get-tuple-element.110.fprev_ref, ...), custom_call_target="tpu_custom_call" | custom-call | tf_op jit(solution)/shard_map/cols3/pallas_call | solution.py:334
  182.8 11.8 %all_to_all.112.recv_ref = f32[32,4,128]{2,1,0:T(4,128)S(1)} all-to-all(f32[32,4,128]{2,1,0:T(4,128)S(1)} %get-tuple-element.113), channel_id=1, replica_groups=mesh['gx'=8,'gz'=4,'gy'=8] {'gx','gz'}, dimensions={0} | all-to-all | bytes 131072 | tf_op jit(solution)/shard_map/all_to_all | solution.py:346
  215.5 13.7 %cols4.1 = (f32[32,128]{1,0:T(8,128)S(1)}, f32[8,128]{1,0:T(8,128)S(1)}, f32[16,128]{1,0:T(8,128)S(1)}, f32[32,4,128]{2,1,0:T(4,128)S(1)}) custom-call(f32[8,32,128]{2,1,0:T(8,128)S(1)} %all_to_all.113.recv_ref, f32[32,128]{1,0:T(8,128)S(1)} %bitcast.11, f32[32,128]{1,0:T(8,128)S(1)} %get-tuple-element.118.fprev_ref, ...), custom_call_target="tpu_custom_call" | custom-call | tf_op jit(solution)/shard_map/cols4/pallas_call | solution.py:334
  229.1 11.8 %all_to_all.114.recv_ref = f32[32,4,128]{2,1,0:T(4,128)S(1)} all-to-all(f32[32,4,128]{2,1,0:T(4,128)S(1)} %get-tuple-element.121), channel_id=1, replica_groups=mesh['gx'=8,'gz'=4,'gy'=8] {'gx','gz'}, dimensions={0} | all-to-all | bytes 131072 | tf_op jit(solution)/shard_map/all_to_all | solution.py:346
  261.8 13.7 %cols5.1 = (f32[32,128]{1,0:T(8,128)S(1)}, f32[8,128]{1,0:T(8,128)S(1)}, f32[16,128]{1,0:T(8,128)S(1)}, f32[32,4,128]{2,1,0:T(4,128)S(1)}) custom-call(f32[8,32,128]{2,1,0:T(8,128)S(1)} %all_to_all.115.recv_ref, f32[32,128]{1,0:T(8,128)S(1)} %bitcast.12, f32[32,128]{1,0:T(8,128)S(1)} %get-tuple-element.126.fprev_ref, ...), custom_call_target="tpu_custom_call" | custom-call | tf_op jit(solution)/shard_map/cols5/pallas_call | solution.py:334
  275.5 11.8 %all_to_all.116.recv_ref = f32[32,4,128]{2,1,0:T(4,128)S(1)} all-to-all(f32[32,4,128]{2,1,0:T(4,128)S(1)} %get-tuple-element.129), channel_id=1, replica_groups=mesh['gx'=8,'gz'=4,'gy'=8] {'gx','gz'}, dimensions={0} | all-to-all | bytes 131072 | tf_op jit(solution)/shard_map/all_to_all | solution.py:346
  308.4 13.7 %cols6.1 = (f32[32,128]{1,0:T(8,128)S(1)}, f32[8,128]{1,0:T(8,128)S(1)}, f32[16,128]{1,0:T(8,128)S(1)}, f32[32,4,128]{2,1,0:T(4,128)S(1)}) custom-call(f32[8,32,128]{2,1,0:T(8,128)S(1)} %all_to_all.117.recv_ref, f32[32,128]{1,0:T(8,128)S(1)} %bitcast.13, f32[32,128]{1,0:T(8,128)S(1)} %get-tuple-element.134.fprev_ref, ...), custom_call_target="tpu_custom_call" | custom-call | tf_op jit(solution)/shard_map/cols6/pallas_call | solution.py:334
  322.0 11.8 %all_to_all.118.recv_ref = f32[32,4,128]{2,1,0:T(4,128)S(1)} all-to-all(f32[32,4,128]{2,1,0:T(4,128)S(1)} %get-tuple-element.137), channel_id=1, replica_groups=mesh['gx'=8,'gz'=4,'gy'=8] {'gx','gz'}, dimensions={0} | all-to-all | bytes 131072 | tf_op jit(solution)/shard_map/all_to_all | solution.py:346
  354.7 13.7 %cols7.1 = (f32[32,128]{1,0:T(8,128)S(1)}, f32[8,128]{1,0:T(8,128)S(1)}, f32[16,128]{1,0:T(8,128)S(1)}, f32[32,4,128]{2,1,0:T(4,128)S(1)}) custom-call(f32[8,32,128]{2,1,0:T(8,128)S(1)} %all_to_all.119.recv_ref, f32[32,128]{1,0:T(8,128)S(1)} %bitcast.14, f32[32,128]{1,0:T(8,128)S(1)} %get-tuple-element.142.fprev_ref, ...), custom_call_target="tpu_custom_call" | custom-call | tf_op jit(solution)/shard_map/cols7/pallas_call | solution.py:334
  368.3 11.8 %all_to_all.120.recv_ref = f32[32,4,128]{2,1,0:T(4,128)S(1)} all-to-all(f32[32,4,128]{2,1,0:T(4,128)S(1)} %get-tuple-element.145), channel_id=1, replica_groups=mesh['gx'=8,'gz'=4,'gy'=8] {'gx','gz'}, dimensions={0} | all-to-all | bytes 131072 | tf_op jit(solution)/shard_map/all_to_all | solution.py:346
  380.2 11.1 %rows7.1 = (f32[4,128]{1,0:T(4,128)S(1)}, f32[8,128]{1,0:T(8,128)S(1)}, f32[16,128]{1,0:T(8,128)S(1)}, f32[8,32,128]{2,1,0:T(8,128)S(1)}) custom-call(f32[32,4,128]{2,1,0:T(4,128)S(1)} %all_to_all.120.recv_ref, f32[4,128]{1,0:T(4,128)S(1)} %bitcast.25, f32[4,128]{1,0:T(4,128)S(1)} %get-tuple-element.146.gprev_ref, f32[32,128]{1,0:T(8,128)S(1)} %get-tuple-element.88.mr_ref, ...), custom_call_target="tpu_custom_call" | custom-call | tf_op jit(solution)/shard_map/rows7/pallas_call | solution.py:334
  401.0 13.7 %cols8.1 = (f32[32,128]{1,0:T(8,128)S(1)}, f32[8,128]{1,0:T(8,128)S(1)}, f32[16,128]{1,0:T(8,128)S(1)}, f32[32,4,128]{2,1,0:T(4,128)S(1)}) custom-call(f32[8,32,128]{2,1,0:T(8,128)S(1)} %all_to_all.121.recv_ref, f32[32,128]{1,0:T(8,128)S(1)} %bitcast.15, f32[32,128]{1,0:T(8,128)S(1)} %get-tuple-element.150.fprev_ref, ...), custom_call_target="tpu_custom_call" | custom-call | tf_op jit(solution)/shard_map/cols8/pallas_call | solution.py:334
  414.7 11.8 %all_to_all.122.recv_ref = f32[32,4,128]{2,1,0:T(4,128)S(1)} all-to-all(f32[32,4,128]{2,1,0:T(4,128)S(1)} %get-tuple-element.153), channel_id=1, replica_groups=mesh['gx'=8,'gz'=4,'gy'=8] {'gx','gz'}, dimensions={0} | all-to-all | bytes 131072 | tf_op jit(solution)/shard_map/all_to_all | solution.py:346
  447.3 14.3 %cols9.1 = (f32[32,128]{1,0:T(8,128)}, f32[8,128]{1,0:T(8,128)S(1)}, f32[16,128]{1,0:T(8,128)}, f32[32,8,128]{2,1,0:T(8,128)S(1)}) custom-call(f32[8,32,128]{2,1,0:T(8,128)S(1)} %all_to_all.123.recv_ref, f32[32,128]{1,0:T(8,128)S(1)} %bitcast.16, f32[32,128]{1,0:T(8,128)S(1)} %get-tuple-element.158.fprev_ref, f32[32,128]{1,0:T(8,128)S(1)} %get-tuple-element.88.mr_ref, ...), custom_call_target="tpu_custom_call" | custom-call | tf_op jit(solution)/shard_map/cols9/pallas_call | solution.py:334
  461.6 12.4 %all_to_all.124.recv_ref = f32[32,8,128]{2,1,0:T(8,128)S(1)} all-to-all(f32[32,8,128]{2,1,0:T(8,128)S(1)} %get-tuple-element.162), channel_id=1, replica_groups=mesh['gx'=8,'gz'=4,'gy'=8] {'gx','gz'}, dimensions={0} | all-to-all | bytes 262144 | tf_op jit(solution)/shard_map/all_to_all | solution.py:346
  (35 shorter events, 174.4 us)
Async XLA Ops:
  0.6 1.2 copy-start
  1.9 0.9 copy-start.1
  2.8 0.7 copy-start.4
  20.4 0.7 copy-start.2
  21.1 55.2 %copy-start.3 = (f32[4096]{0:T(1024)S(1)}, f32[4096]{0:T(1024)}, u32[]{:S(2)}) copy-start(f32[4096]{0:T(1024)} %param.6) | copy-start | bytes 49156

commit v4 on v3

--- a/solution.py
+++ b/solution.py
@@ -90,38 +90,45 @@
 def init_kernel(kappa, x_ref, y_ref, cm_ref, k_ref, mr_ref, xs_ref, out_ref, cs_ref, l_ref):
     cols = y_ref.shape[0]
     rows = x_ref.shape[0]
-    wide = 512
+    wide = 1024
     cs_ref[...] = jnp.broadcast_to(scaled_norms(y_ref[...], kappa), (cols, LANES))
-    ones = jnp.ones((8, x_ref.shape[1]), f32)
+    ones = jnp.ones((16, x_ref.shape[1]), jnp.bfloat16)
 
     def chunk(c, carry):
         at = pl.multiple_of(c * wide, wide)
         xb = x_ref[pl.ds(at, wide), :]
-        k_ref[:, pl.ds(at, wide)] = cross_of(y_ref[...], xb) * (2.0 * kappa)
-        xf = xb.astype(f32)
-        norms = kappa * lax.dot_general(
-            ones, xf * xf, (((1,), (1,)), ((), ())),
-            precision=lax.Precision.HIGHEST, preferred_element_type=f32,
-        )
-        for t in range(wide // LANES):
-            here = pl.ds(pl.multiple_of(at + t * LANES, LANES), LANES)
-            tops = [None] * 4
-            for j in range(cols // 8):
-                z = k_ref[8 * j : 8 * j + 8, here] - cs_ref[8 * j : 8 * j + 8, :]
-                tops[j % 4] = z if tops[j % 4] is None else jnp.maximum(tops[j % 4], z)
-            top = jnp.maximum(jnp.maximum(tops[0], tops[1]), jnp.maximum(tops[2], tops[3]))
-            top = jnp.max(top, axis=0, keepdims=True)
-            sums = [None] * 4
-            for j in range(cols // 8):
-                e = jnp.exp2(k_ref[8 * j : 8 * j + 8, here] - cs_ref[8 * j : 8 * j + 8, :] - top)
-                k_ref[8 * j : 8 * j + 8, here] = e
-                sums[j % 4] = e if sums[j % 4] is None else sums[j % 4] + e
-            weight = jnp.sum((sums[0] + sums[1]) + (sums[2] + sums[3]), axis=0, keepdims=True)
+        kc_ref = k_ref.at[:, pl.ds(at, wide)]
+        kc_ref[...] = cross_of(y_ref[...], xb) * (2.0 * kappa)
+        squares = xb.astype(f32) * xb.astype(f32)
+        upper = squares.astype(jnp.bfloat16)
+        lower = (squares - upper.astype(f32)).astype(jnp.bfloat16)
+        norms = kappa * (cross_of(ones, upper) + cross_of(ones, lower))
+        tiles = wide // LANES
+        here = [slice(t * LANES, (t + 1) * LANES) for t in range(tiles)]
+        tops = [[None] * 2 for t in range(tiles)]
+        for j in range(cols // 8):
+            line = slice(8 * j, 8 * j + 8)
+            cs = cs_ref[line, :]
+            for t in range(tiles):
+                z = kc_ref[line, here[t]] - cs
+                tops[t][j % 2] = z if j < 2 else jnp.maximum(tops[t][j % 2], z)
+        tops = [jnp.max(jnp.maximum(*pair), axis=0, keepdims=True) for pair in tops]
+        spans = [jnp.broadcast_to(top, (8, LANES)) for top in tops]
+        sums = [[None] * 2 for t in range(tiles)]
+        for j in range(cols // 8):
+            line = slice(8 * j, 8 * j + 8)
+            cs = cs_ref[line, :]
+            for t in range(tiles):
+                e = jnp.exp2(kc_ref[line, here[t]] - cs - spans[t])
+                kc_ref[line, here[t]] = e
+                sums[t][j % 2] = e if j < 2 else sums[t][j % 2] + e
+        for t in range(tiles):
+            weight = jnp.sum(sums[t][0] + sums[t][1], axis=0, keepdims=True)
             norm = norms[0:1, t * LANES : (t + 1) * LANES]
-            line = pl.ds(c * (wide // LANES) + t, 1)
+            line = pl.ds(c * tiles + t, 1)
             xs_ref[line, :] = norm
-            mr_ref[line, :] = top - norm
-            l_ref[line, :] = (top - norm) + log2(weight)
+            mr_ref[line, :] = tops[t] - norm
+            l_ref[line, :] = (tops[t] - norm) + log2(weight)
         return carry
 
     lax.fori_loop(0, rows // wide, chunk, 0)
@@ -171,16 +178,19 @@
         s_ref[t : t + 1, :] = jnp.sum(line, axis=0, keepdims=True)
 
 
-def col_kernel(
-    kappa, index, last,
-    recv_ref, rm_ref, fprev_ref, mr_ref, xs_ref, sc_ref, errs_ref, k_ref, x_ref, y_ref,
-    f_ref, sc_out_ref, errs_out_ref, out_ref,
-    acc_ref, s_ref, fx_ref, top_ref, weight_ref,
-):
+def col_kernel(kappa, index, last, count, *refs):
+    got, refs = refs[:count], refs[count:]
+    rm_ref, fprev_ref, mr_ref, xs_ref, sc_ref, errs_ref, k_ref, x_ref, y_ref, *refs = refs
+    f_ref, sc_out_ref, errs_out_ref, out_ref, *refs = refs
+    acc_ref, s_ref, fx_ref, top_ref, weight_ref = refs
     rows, cols = k_ref.shape[1], k_ref.shape[0]
     lines = rows // LANES
     lane, sub = lane_and_sublane()
-    lse = joined([recv_ref[d, 0:lines, :] for d in range(recv_ref.shape[0])])
+    if index == 0:
+        recv_ref = got[0]
+        lse = joined([recv_ref[d, 0:lines, :] for d in range(recv_ref.shape[0])])
+    else:
+        lse = joined([ref[...] for ref in got])
     mass = rm_ref[...]
     la = log2(mass)
     sc = sc_ref[...]
@@ -303,7 +313,7 @@
         for t in range(together):
             r_ref[first + t : first + t + 1, :] = jnp.sum(acc[t], axis=0, keepdims=True)
     sums = r_ref[...]
-    spread(out_ref, mr_ref[...] + (high + log2(sums)), None)
+    out_ref[...] = mr_ref[...] + (high + log2(sums))
     g_ref[...] = g_new
     sc_out_ref[...] = jnp.where(sub == 3, newest, sc)
     errs_out_ref[...] = errs
@@ -313,7 +323,7 @@
     def _():
         column_form(g_new, put)
         exact_rows(kappa, x_ref, y_ref, vbc_ref, xs_ref, l_ref)
-        spread(out_ref, l_ref[...], None)
+        out_ref[...] = l_ref[...]
 
 
 def last_kernel(index, recv_ref, cm_ref, gprev_ref, sc_ref, errs_ref, g_ref, row_ref, out_ref):
@@ -344,6 +354,16 @@
 
 def exchange(x, axis):
     return lax.all_to_all(x, axis, split_axis=0, concat_axis=0, tiled=True)
+
+
+def paired(x, axis):
+    count = lax.axis_size(axis)
+
+    def swapped(x, by):
+        return lax.ppermute(x, axis, [(i, i ^ by) for i in range(count)])
+
+    both = joined([x, swapped(x, 1)])
+    return (both, *(swapped(both, by) for by in range(2, count, 2)))
 
 
 def on_device(row_embed, col_embed, row_mass, col_mass):
@@ -372,11 +392,11 @@
     col_errs = jnp.zeros(noting, f32)
     for index in range(ITERS):
         last = index == ITERS - 1
-        got = exchange(out, COLS_OVER)
+        got = (exchange(out, COLS_OVER),) if index == 0 else paired(out, COLS_OVER)
         more = 4 if index == 0 or last else 0
         f_pot, sc, row_errs, out = call(
-            functools.partial(col_kernel, kappa, index, last),
-            (got, rm, f_pot, mr, xs, sc, row_errs, k, row_embed, col_embed),
+            functools.partial(col_kernel, kappa, index, last, len(got)),
+            (*got, rm, f_pot, mr, xs, sc, row_errs, k, row_embed, col_embed),
             [(row_lines, LANES), tile, noting, (by_row, col_lines + more, LANES)],
             [(cols, LANES), (col_lines, LANES), (row_lines, LANES), (cols, LANES), (cols, LANES)],
             24 * mib, f"cols{index}",
@@ -387,7 +407,7 @@
         g_pot, sc, col_errs, out = call(
             functools.partial(row_kernel, kappa, index),
             (got, cm, g_pot, mr, xs, sc, col_errs, k, row_embed, col_embed),
-            [(col_lines, LANES), tile, noting, (by_col, row_lines, LANES)],
+            [(col_lines, LANES), tile, noting, (row_lines, LANES)],
             [(cols, LANES), (row_lines, LANES), (row_lines, LANES)],
             24 * mib, f"rows{index}",
         )

time: 485 us -> 502 us (1.035)
  blocking collectives: 236 us -> 150 us
  starting transfers between devices: 0 us -> 72.9 us
  waiting for transfers between devices: 0 us -> 28.7 us
    all_to_all x21 -> x12, blocking collectives: 236 us -> 150 us  [exchange(): return lax.all_to_all(x, axis, split_axis=0, concat_axis=0, tiled=True)]
    ppermute x0 -> x36, starting transfers between devices: none -> 72.9 us  [swapped(): return lax.ppermute(x, axis, [(i, i ^ by) for i in range(count)])]
    ppermute x0 -> x36, waiting for transfers between devices: none -> 28.7 us  [swapped(): return lax.ppermute(x, axis, [(i, i ^ by) for i in range(count)])]
  transfers between devices with their start and end apart: 0 -> 36, of which waited for: 0 -> 26; matrix products, arithmetic and copies ran while one was open for 0% -> 0% of each run, Pallas kernels for 0% -> 0%
where the time goes in v4:
time: 502 us; the launch traced here: 498 us
  Pallas kernels  241 us (48%)
  blocking collectives  150 us (30%)
  starting transfers between devices  72.9 us (15%)
  waiting for transfers between devices  28.7 us (6%)
    pallas_call x21, Pallas kernels, call(): pl.pallas_call(kernel, in_specs=[on_chip() for _ in args], out_specs=[on_...  241 us
    all_to_all x12, blocking collectives, exchange(): return lax.all_to_all(x, axis, split_axis=0, concat_axis=0, tiled=True)  150 us
    ppermute x36, starting transfers between devices, swapped(): return lax.ppermute(x, axis, [(i, i ^ by) for i in range(count)])  72.9 us
    ppermute x36, waiting for transfers between devices, swapped(): return lax.ppermute(x, axis, [(i, i ^ by) for i in range(count)])  28.7 us
  transfers between devices with their start and end apart: 36, of which 26 were waited for; matrix products, arithmetic and copies ran while one was open for 0% of the time, Pallas kernels for 0%

profile of v4, /device:TPU:1, one launch (start us, length us, event | category | flops | bytes accessed | tf_op | source)
XLA Modules:
  0.0 497.5 jit_solution(18025121530967825087)
XLA Ops:
  6.6 11.3 %all_to_all.60.refs_0_ = f32[8,40,128]{2,1,0:T(8,128)S(1)} all-to-all(f32[8,40,128]{2,1,0:T(8,128)S(1)} %get-tuple-element.87), channel_id=1, replica_groups=mesh['gx'=8,'gz'=4,'gy'=8] {'gy'}, dimensions={0} | all-to-all | bytes 327680 | tf_op jit(solution)/shard_map/all_to_all | solution.py:356
  18.6 13.7 %cols0.1 = (f32[32,128]{1,0:T(8,128)S(1)}, f32[8,128]{1,0:T(8,128)S(1)}, f32[16,128]{1,0:T(8,128)S(1)}, f32[32,8,128]{2,1,0:T(8,128)S(1)}) custom-call(f32[8,40,128]{2,1,0:T(8,128)S(1)} %all_to_all.60.refs_0_, f32[32,128]{1,0:T(8,128)S(1)} %bitcast.7, f32[32,128]{1,0:T(8,128)S(1)} %broadcast_in_dim.9.refs_2_, ...), custom_call_target="tpu_custom_call" | custom-call | tf_op jit(solution)/shard_map/cols0/pallas_call | solution.py:344
  32.3 20.2 %all_to_all.61.recv_ref = f32[32,8,128]{2,1,0:T(8,128)S(1)} all-to-all(f32[32,8,128]{2,1,0:T(8,128)S(1)} %get-tuple-element.91), channel_id=1, replica_groups=mesh['gx'=8,'gz'=4,'gy'=8] {'gx','gz'}, dimensions={0} | all-to-all | bytes 262144 | tf_op jit(solution)/shard_map/all_to_all | solution.py:356
  52.5 11.3 %rows0.1 = (f32[4,128]{1,0:T(4,128)S(1)}, f32[8,128]{1,0:T(8,128)S(1)}, f32[16,128]{1,0:T(8,128)S(1)}, f32[32,128]{1,0:T(8,128)S(1)}) custom-call(f32[32,8,128]{2,1,0:T(8,128)S(1)} %all_to_all.61.recv_ref, f32[4,128]{1,0:T(4,128)S(1)} %bitcast.18, f32[4,128]{1,0:T(4,128)S(1)} %broadcast_in_dim.11.gprev_ref, ...), custom_call_target="tpu_custom_call" | custom-call | tf_op jit(solution)/shard_map/rows0/pallas_call | solution.py:344
  73.1 13.6 %cols1.1 = (f32[32,128]{1,0:T(8,128)S(1)}, f32[8,128]{1,0:T(8,128)S(1)}, f32[16,128]{1,0:T(8,128)S(1)}, f32[32,4,128]{2,1,0:T(4,128)S(1)}) custom-call(f32[32,128]{1,0:T(8,128)S(1)} %multiply_add_fusion.8.refs_0_, f32[32,128]{1,0:T(8,128)S(1)} %collective-permute-done.1.refs_1_, f32[32,128]{1,0:T(8,128)S(1)} %collective-permute-done.2.refs_2_, ...), custom_call_target="tpu_custom_call" | custom-call | tf_op jit(solution)/shard_map/cols1/pallas_call | solution.py:344
  86.7 11.8 %all_to_all.62.recv_ref = f32[32,4,128]{2,1,0:T(4,128)S(1)} all-to-all(f32[32,4,128]{2,1,0:T(4,128)S(1)} %get-tuple-element.97), channel_id=1, replica_groups=mesh['gx'=8,'gz'=4,'gy'=8] {'gx','gz'}, dimensions={0} | all-to-all | bytes 131072 | tf_op jit(solution)/shard_map/all_to_all | solution.py:356
  120.9 13.7 %cols2.1 = (f32[32,128]{1,0:T(8,128)S(1)}, f32[8,128]{1,0:T(8,128)S(1)}, f32[16,128]{1,0:T(8,128)S(1)}, f32[32,4,128]{2,1,0:T(4,128)S(1)}) custom-call(f32[32,128]{1,0:T(8,128)S(1)} %multiply_add_fusion.7.refs_0_, f32[32,128]{1,0:T(8,128)S(1)} %collective-permute-done.5.refs_1_, f32[32,128]{1,0:T(8,128)S(1)} %collective-permute-done.6.refs_2_, ...), custom_call_target="tpu_custom_call" | custom-call | tf_op jit(solution)/shard_map/cols2/pallas_call | solution.py:344
  134.5 11.8 %all_to_all.63.recv_ref = f32[32,4,128]{2,1,0:T(4,128)S(1)} all-to-all(f32[32,4,128]{2,1,0:T(4,128)S(1)} %get-tuple-element.105), channel_id=1, replica_groups=mesh['gx'=8,'gz'=4,'gy'=8] {'gx','gz'}, dimensions={0} | all-to-all | bytes 131072 | tf_op jit(solution)/shard_map/all_to_all | solution.py:356
  166.1 13.7 %cols3.1 = (f32[32,128]{1,0:T(8,128)S(1)}, f32[8,128]{1,0:T(8,128)S(1)}, f32[16,128]{1,0:T(8,128)S(1)}, f32[32,4,128]{2,1,0:T(4,128)S(1)}) custom-call(f32[32,128]{1,0:T(8,128)S(1)} %multiply_add_fusion.6.refs_0_, f32[32,128]{1,0:T(8,128)S(1)} %collective-permute-done.9.refs_1_, f32[32,128]{1,0:T(8,128)S(1)} %collective-permute-done.10.refs_2_, ...), custom_call_target="tpu_custom_call" | custom-call | tf_op jit(solution)/shard_map/cols3/pallas_call | solution.py:344
  179.8 11.8 %all_to_all.64.recv_ref = f32[32,4,128]{2,1,0:T(4,128)S(1)} all-to-all(f32[32,4,128]{2,1,0:T(4,128)S(1)} %get-tuple-element.113), channel_id=1, replica_groups=mesh['gx'=8,'gz'=4,'gy'=8] {'gx','gz'}, dimensions={0} | all-to-all | bytes 131072 | tf_op jit(solution)/shard_map/all_to_all | solution.py:356
  191.6 11.1 %rows3.1 = (f32[4,128]{1,0:T(4,128)S(1)}, f32[8,128]{1,0:T(8,128)S(1)}, f32[16,128]{1,0:T(8,128)S(1)}, f32[32,128]{1,0:T(8,128)S(1)}) custom-call(f32[32,4,128]{2,1,0:T(4,128)S(1)} %all_to_all.64.recv_ref, f32[4,128]{1,0:T(4,128)S(1)} %bitcast.21, f32[4,128]{1,0:T(4,128)S(1)} %get-tuple-element.114.gprev_ref, ...), custom_call_target="tpu_custom_call" | custom-call | tf_op jit(solution)/shard_map/rows3/pallas_call | solution.py:344
  213.6 13.7 %cols4.1 = (f32[32,128]{1,0:T(8,128)S(1)}, f32[8,128]{1,0:T(8,128)S(1)}, f32[16,128]{1,0:T(8,128)S(1)}, f32[32,4,128]{2,1,0:T(4,128)S(1)}) custom-call(f32[32,128]{1,0:T(8,128)S(1)} %multiply_add_fusion.5.refs_0_, f32[32,128]{1,0:T(8,128)S(1)} %collective-permute-done.13.refs_1_, f32[32,128]{1,0:T(8,128)S(1)} %collective-permute-done.14.refs_2_, ...), custom_call_target="tpu_custom_call" | custom-call | tf_op jit(solution)/shard_map/cols4/pallas_call | solution.py:344
  227.2 11.8 %all_to_all.65.recv_ref = f32[32,4,128]{2,1,0:T(4,128)S(1)} all-to-all(f32[32,4,128]{2,1,0:T(4,128)S(1)} %get-tuple-element.121), channel_id=1, replica_groups=mesh['gx'=8,'gz'=4,'gy'=8] {'gx','gz'}, dimensions={0} | all-to-all | bytes 131072 | tf_op jit(solution)/shard_map/all_to_all | solution.py:356
  260.3 13.7 %cols5.1 = (f32[32,128]{1,0:T(8,128)S(1)}, f32[8,128]{1,0:T(8,128)S(1)}, f32[16,128]{1,0:T(8,128)S(1)}, f32[32,4,128]{2,1,0:T(4,128)S(1)}) custom-call(f32[32,128]{1,0:T(8,128)S(1)} %multiply_add_fusion.4.refs_0_, f32[32,128]{1,0:T(8,128)S(1)} %collective-permute-done.17.refs_1_, f32[32,128]{1,0:T(8,128)S(1)} %collective-permute-done.18.refs_2_, ...), custom_call_target="tpu_custom_call" | custom-call | tf_op jit(solution)/shard_map/cols5/pallas_call | solution.py:344
  273.9 11.8 %all_to_all.66.recv_ref = f32[32,4,128]{2,1,0:T(4,128)S(1)} all-to-all(f32[32,4,128]{2,1,0:T(4,128)S(1)} %get-tuple-element.129), channel_id=1, replica_groups=mesh['gx'=8,'gz'=4,'gy'=8] {'gx','gz'}, dimensions={0} | all-to-all | bytes 131072 | tf_op jit(solution)/shard_map/all_to_all | solution.py:356
  316.9 13.7 %cols6.1 = (f32[32,128]{1,0:T(8,128)S(1)}, f32[8,128]{1,0:T(8,128)S(1)}, f32[16,128]{1,0:T(8,128)S(1)}, f32[32,4,128]{2,1,0:T(4,128)S(1)}) custom-call(f32[32,128]{1,0:T(8,128)S(1)} %multiply_add_fusion.3.refs_0_, f32[32,128]{1,0:T(8,128)S(1)} %collective-permute-done.21.refs_1_, f32[32,128]{1,0:T(8,128)S(1)} %collective-permute-done.22.refs_2_, ...), custom_call_target="tpu_custom_call" | custom-call | tf_op jit(solution)/shard_map/cols6/pallas_call | solution.py:344
  330.5 11.8 %all_to_all.67.recv_ref = f32[32,4,128]{2,1,0:T(4,128)S(1)} all-to-all(f32[32,4,128]{2,1,0:T(4,128)S(1)} %get-tuple-element.137), channel_id=1, replica_groups=mesh['gx'=8,'gz'=4,'gy'=8] {'gx','gz'}, dimensions={0} | all-to-all | bytes 131072 | tf_op jit(solution)/shard_map/all_to_all | solution.py:356
  363.8 13.7 %cols7.1 = (f32[32,128]{1,0:T(8,128)S(1)}, f32[8,128]{1,0:T(8,128)S(1)}, f32[16,128]{1,0:T(8,128)S(1)}, f32[32,4,128]{2,1,0:T(4,128)S(1)}) custom-call(f32[32,128]{1,0:T(8,128)S(1)} %multiply_add_fusion.2.refs_0_, f32[32,128]{1,0:T(8,128)S(1)} %collective-permute-done.25.refs_1_, f32[32,128]{1,0:T(8,128)S(1)} %collective-permute-done.26.refs_2_, ...), custom_call_target="tpu_custom_call" | custom-call | tf_op jit(solution)/shard_map/cols7/pallas_call | solution.py:344
  377.5 11.8 %all_to_all.68.recv_ref = f32[32,4,128]{2,1,0:T(4,128)S(1)} all-to-all(f32[32,4,128]{2,1,0:T(4,128)S(1)} %get-tuple-element.145), channel_id=1, replica_groups=mesh['gx'=8,'gz'=4,'gy'=8] {'gx','gz'}, dimensions={0} | all-to-all | bytes 131072 | tf_op jit(solution)/shard_map/all_to_all | solution.py:356
  411.4 13.6 %cols8.1 = (f32[32,128]{1,0:T(8,128)S(1)}, f32[8,128]{1,0:T(8,128)S(1)}, f32[16,128]{1,0:T(8,128)S(1)}, f32[32,4,128]{2,1,0:T(4,128)S(1)}) custom-call(f32[32,128]{1,0:T(8,128)S(1)} %multiply_add_fusion.1.refs_0_, f32[32,128]{1,0:T(8,128)S(1)} %collective-permute-done.29.refs_1_, f32[32,128]{1,0:T(8,128)S(1)} %collective-permute-done.30.refs_2_, ...), custom_call_target="tpu_custom_call" | custom-call | tf_op jit(solution)/shard_map/cols8/pallas_call | solution.py:344
  425.0 11.8 %all_to_all.69.recv_ref = f32[32,4,128]{2,1,0:T(4,128)S(1)} all-to-all(f32[32,4,128]{2,1,0:T(4,128)S(1)} %get-tuple-element.153), channel_id=1, replica_groups=mesh['gx'=8,'gz'=4,'gy'=8] {'gx','gz'}, dimensions={0} | all-to-all | bytes 131072 | tf_op jit(solution)/shard_map/all_to_all | solution.py:356
  458.3 14.3 %cols9.1 = (f32[32,128]{1,0:T(8,128)}, f32[8,128]{1,0:T(8,128)S(1)}, f32[16,128]{1,0:T(8,128)}, f32[32,8,128]{2,1,0:T(8,128)S(1)}) custom-call(f32[32,128]{1,0:T(8,128)S(1)} %multiply_add_fusion.refs_0_, f32[32,128]{1,0:T(8,128)S(1)} %collective-permute-done.33.refs_1_, f32[32,128]{1,0:T(8,128)S(1)} %collective-permute-done.34.refs_2_, ...), custom_call_target="tpu_custom_call" | custom-call | tf_op jit(solution)/shard_map/cols9/pallas_call | solution.py:344
  472.6 12.4 %all_to_all.70.recv_ref = f32[32,8,128]{2,1,0:T(8,128)S(1)} all-to-all(f32[32,8,128]{2,1,0:T(8,128)S(1)} %get-tuple-element.162), channel_id=1, replica_groups=mesh['gx'=8,'gz'=4,'gy'=8] {'gx','gz'}, dimensions={0} | all-to-all | bytes 262144 | tf_op jit(solution)/shard_map/all_to_all | solution.py:356
  485.6 11.2 %all_to_all.71 = f32[8,8,128]{2,1,0:T(8,128)S(1)} all-to-all(f32[8,8,128]{2,1,0:T(8,128)S(1)} %get-tuple-element.167), channel_id=1, replica_groups=mesh['gx'=8,'gz'=4,'gy'=8] {'gy'}, dimensions={0} | all-to-all | bytes 65536 | tf_op jit(solution)/shard_map/all_to_all | solution.py:356
  (107 shorter events, 187.2 us)
Async XLA Ops:
  67.1 3.9 collective-permute-start.1
  67.5 4.1 collective-permute-start.2
  109.6 4.4 collective-permute-start.4
  114.1 4.3 collective-permute-start.6
  157.4 4.3 collective-permute-start.8
  161.7 4.2 collective-permute-start.10
  161.9 4.2 collective-permute-start.11
  206.5 4.3 collective-permute-start.13
  208.3 4.1 collective-permute-start.14
  209.5 4.1 collective-permute-start.15
  254.1 3.9 collective-permute-start.17
  254.2 4.3 collective-permute-start.18
  296.8 4.2 collective-permute-start.20
  301.1 13.0 %collective-permute-start.21 = (f32[32,128]{1,0:T(8,128)S(1)}, f32[32,128]{1,0:T(8,128)S(1)}, u32[]{:S(2)}, u32[]{:S(2)}) collective-permute-start(f32[32,128]{1,0:T(8,128)S(1)} %multiply_add_fusion.3.refs_0_), channel_id=1, source_target_pairs={{0,2},{1,3},{2,0},{3,1},{4,6},{5,7},{6,4},{7,5},{8,10},{9,11},{10,... | collective-permute-start | bytes 49160 | tf_op jit(solution)/shard_map/ppermute | solution.py:363
  301.2 12.9 %collective-permute-start.22 = (f32[32,128]{1,0:T(8,128)S(1)}, f32[32,128]{1,0:T(8,128)S(1)}, u32[]{:S(2)}, u32[]{:S(2)}) collective-permute-start(f32[32,128]{1,0:T(8,128)S(1)} %multiply_add_fusion.3.refs_0_), channel_id=1, source_target_pairs={{0,4},{1,5},{2,6},{3,7},{4,0},{5,1},{6,2},{7,3},{8,12},{9,13},{10,... | collective-permute-start | bytes 49160 | tf_op jit(solution)/shard_map/ppermute | solution.py:363
  304.0 12.9 %collective-permute-start.23 = (f32[32,128]{1,0:T(8,128)S(1)}, f32[32,128]{1,0:T(8,128)S(1)}, u32[]{:S(2)}, u32[]{:S(2)}) collective-permute-start(f32[32,128]{1,0:T(8,128)S(1)} %multiply_add_fusion.3.refs_0_), channel_id=1, source_target_pairs={{0,6},{1,7},{2,4},{3,5},{4,2},{5,3},{6,0},{7,1},{8,14},{9,15},{10,... | collective-permute-start | bytes 49160 | tf_op jit(solution)/shard_map/ppermute | solution.py:363
  353.4 4.3 collective-permute-start.24
  357.7 3.9 collective-permute-start.25
  357.8 4.3 collective-permute-start.26
  400.4 4.3 collective-permute-start.28
  404.6 3.9 collective-permute-start.29
  404.7 4.2 collective-permute-start.30
  448.0 4.2 collective-permute-start.32
  452.3 4.3 collective-permute-start.34
  (17 other events, 102.7 us)

commit v5 on v4

--- a/solution.py
+++ b/solution.py
@@ -7,6 +7,7 @@
 from jax.experimental import pallas as pl
 from jax.experimental.pallas import tpu as pltpu
 from jax.sharding import PartitionSpec as P
+
 
 ITERS = 10
 ROWS_OVER = ("gx", "gz")
@@ -105,7 +106,7 @@
         norms = kappa * (cross_of(ones, upper) + cross_of(ones, lower))
         tiles = wide // LANES
         here = [slice(t * LANES, (t + 1) * LANES) for t in range(tiles)]
-        tops = [[None] * 2 for t in range(tiles)]
+        tops = [[None] * 2 for _ in range(tiles)]
         for j in range(cols // 8):
             line = slice(8 * j, 8 * j + 8)
             cs = cs_ref[line, :]
@@ -114,7 +115,7 @@
                 tops[t][j % 2] = z if j < 2 else jnp.maximum(tops[t][j % 2], z)
         tops = [jnp.max(jnp.maximum(*pair), axis=0, keepdims=True) for pair in tops]
         spans = [jnp.broadcast_to(top, (8, LANES)) for top in tops]
-        sums = [[None] * 2 for t in range(tiles)]
+        sums = [[None] * 2 for _ in range(tiles)]
         for j in range(cols // 8):
             line = slice(8 * j, 8 * j + 8)
             cs = cs_ref[line, :]
@@ -137,14 +138,20 @@
 
 
 def exact_rows(kappa, x_ref, y_ref, gcol_ref, xs_ref, l_ref):
-    cols = y_ref.shape[0]
-    cs = scaled_norms(y_ref[...], kappa)
-
     def chunk(c, carry):
-        at = pl.multiple_of(c * LANES, LANES)
-        z = cross_of(y_ref[...], x_ref[pl.ds(at, LANES), :]) * (2.0 * kappa) - cs + gcol_ref[...]
-        top = jnp.max(z, axis=0, keepdims=True)
-        weight = jnp.sum(jnp.exp2(z - top), axis=0, keepdims=True)
+        xb = x_ref[pl.ds(pl.multiple_of(c * LANES, LANES), LANES), :]
+
+        def part(b, kept):
+            top, weight = kept
+            here = pl.ds(pl.multiple_of(b * LANES, LANES), LANES)
+            y = y_ref[here, :]
+            z = cross_of(y, xb) * (2.0 * kappa) - scaled_norms(y, kappa) + gcol_ref[here, :]
+            newtop = jnp.maximum(top, jnp.max(z, axis=0, keepdims=True))
+            added = jnp.sum(jnp.exp2(z - newtop), axis=0, keepdims=True)
+            return newtop, weight * jnp.exp2(top - newtop) + added
+
+        nothing = (jnp.full((1, LANES), -jnp.inf, f32), jnp.zeros((1, LANES), f32))
+        top, weight = lax.fori_loop(0, y_ref.shape[0] // LANES, part, nothing)
         l_ref[pl.ds(c, 1), :] = top - xs_ref[pl.ds(c, 1), :] + log2(weight)
         return carry
 
@@ -152,30 +159,32 @@
 
 
 def exact_cols(kappa, x_ref, y_ref, fx_ref, s_ref, top_ref, weight_ref):
-    cols = y_ref.shape[0]
-    top_ref[...] = jnp.full(top_ref.shape, -jnp.inf, f32)
-    weight_ref[...] = jnp.zeros(weight_ref.shape, f32)
-
-    def chunk(c, carry):
-        at = pl.multiple_of(c * LANES, LANES)
-        z = cross_of(y_ref[...], x_ref[pl.ds(at, LANES), :]) * (2.0 * kappa) + fx_ref[pl.ds(c, 1), :]
-        top = top_ref[...]
-        newtop = jnp.maximum(top, jnp.max(z, axis=1, keepdims=True))
-        weight_ref[...] = weight_ref[...] * jnp.exp2(top - newtop) + jnp.sum(
-            jnp.exp2(z - newtop), axis=1, keepdims=True
-        )
-        top_ref[...] = newtop
-        return carry
-
-    lax.fori_loop(0, x_ref.shape[0] // LANES, chunk, 0)
-    lse = top_ref[...] + log2(weight_ref[...]) - scaled_norms(y_ref[...], kappa)
     lane, sub = lane_and_sublane()
-    for t in range(cols // LANES):
+
+    def part(b, carry):
+        y = y_ref[pl.ds(pl.multiple_of(b * LANES, LANES), LANES), :]
+        top_ref[...] = jnp.full(top_ref.shape, -jnp.inf, f32)
+        weight_ref[...] = jnp.zeros(weight_ref.shape, f32)
+
+        def chunk(c, inner):
+            xb = x_ref[pl.ds(pl.multiple_of(c * LANES, LANES), LANES), :]
+            z = cross_of(y, xb) * (2.0 * kappa) + fx_ref[pl.ds(c, 1), :]
+            top = top_ref[...]
+            newtop = jnp.maximum(top, jnp.max(z, axis=1, keepdims=True))
+            added = jnp.sum(jnp.exp2(z - newtop), axis=1, keepdims=True)
+            weight_ref[...] = weight_ref[...] * jnp.exp2(top - newtop) + added
+            top_ref[...] = newtop
+            return inner
+
+        lax.fori_loop(0, x_ref.shape[0] // LANES, chunk, 0)
+        lse = top_ref[...] + log2(weight_ref[...]) - scaled_norms(y, kappa)
         line = jnp.zeros((8, LANES), f32)
         for q in range(LANES // 8):
-            at = t * LANES + 8 * q
-            line = line + jnp.where(lane == sub + 8 * q, lse[at : at + 8, :], 0.0)
-        s_ref[t : t + 1, :] = jnp.sum(line, axis=0, keepdims=True)
+            line = line + jnp.where(lane == sub + 8 * q, lse[8 * q : 8 * q + 8, :], 0.0)
+        s_ref[pl.ds(b, 1), :] = jnp.sum(line, axis=0, keepdims=True)
+        return carry
+
+    lax.fori_loop(0, y_ref.shape[0] // LANES, part, 0)
 
 
 def col_kernel(kappa, index, last, count, *refs):
@@ -263,7 +272,7 @@
 
 def new_target(index, recv_ref, cm_ref, gprev_ref, sc, errs_ref):
     lines = cm_ref.shape[0]
-    lane, sub = lane_and_sublane()
+    _, sub = lane_and_sublane()
     lse = joined([recv_ref[d, 0:lines, :] for d in range(recv_ref.shape[0])])
     mass_b = sc[1:2, :]
     if index == 0:
@@ -285,7 +294,7 @@
 ):
     rows, cols = k_ref.shape[1], k_ref.shape[0]
     lines = rows // LANES
-    lane, sub = lane_and_sublane()
+    _, sub = lane_and_sublane()
     sc = sc_ref[...]
     g_new, sc, errs = new_target(index, recv_ref, cm_ref, gprev_ref, sc, errs_ref)
     newest = largest(g_new)
@@ -328,7 +337,7 @@
 
 def last_kernel(index, recv_ref, cm_ref, gprev_ref, sc_ref, errs_ref, g_ref, row_ref, out_ref):
     lines = cm_ref.shape[0]
-    g_new, sc, errs = new_target(index, recv_ref, cm_ref, gprev_ref, sc_ref[...], errs_ref)
+    g_new, _, errs = new_target(index, recv_ref, cm_ref, gprev_ref, sc_ref[...], errs_ref)
     g_ref[...] = g_new * (eps / LOG2E)
     row_ref[...] = jnp.broadcast_to(jnp.sum(recv_ref[:, lines : lines + 1, :], axis=0), (8, LANES))
     col_errs = jnp.broadcast_to(along_lanes(errs), (8, LANES))
@@ -340,7 +349,7 @@
     return pl.BlockSpec(memory_space=pltpu.VMEM)
 
 
-def call(kernel, args, outs, scratch, limit, name):
+def call(kernel, args, outs, scratch, limit):
     return pl.pallas_call(
         kernel,
         in_specs=[on_chip() for _ in args],
@@ -348,7 +357,6 @@
         out_shape=[jax.ShapeDtypeStruct(shape, f32) for shape in outs],
         scratch_shapes=[pltpu.VMEM(shape, f32) for shape in scratch],
         compiler_params=pltpu.CompilerParams(vmem_limit_bytes=limit),
-        name=name,
     )(*args)
 
 
@@ -382,7 +390,7 @@
         (row_embed, col_embed, cm),
         [(cols, rows), (row_lines, LANES), (row_lines, LANES), (by_col, row_lines + 8, LANES)],
         [(cols, LANES), (row_lines, LANES)],
-        24 * mib, "init",
+        24 * mib,
     )
     f_pot = jnp.zeros((row_lines, LANES), f32)
     g_pot = jnp.zeros((col_lines, LANES), f32)
@@ -398,8 +406,8 @@
             functools.partial(col_kernel, kappa, index, last, len(got)),
             (*got, rm, f_pot, mr, xs, sc, row_errs, k, row_embed, col_embed),
             [(row_lines, LANES), tile, noting, (by_row, col_lines + more, LANES)],
-            [(cols, LANES), (col_lines, LANES), (row_lines, LANES), (cols, LANES), (cols, LANES)],
-            24 * mib, f"cols{index}",
+            [(cols, LANES), (col_lines, LANES), (row_lines, LANES), (LANES, LANES), (LANES, LANES)],
+            24 * mib,
         )
         got = exchange(out, ROWS_OVER)
         if last:
@@ -409,13 +417,13 @@
             (got, cm, g_pot, mr, xs, sc, col_errs, k, row_embed, col_embed),
             [(col_lines, LANES), tile, noting, (row_lines, LANES)],
             [(cols, LANES), (row_lines, LANES), (row_lines, LANES)],
-            24 * mib, f"rows{index}",
+            24 * mib,
         )
     g_out, row_errs, out = call(
         functools.partial(last_kernel, ITERS - 1),
         (got, cm, g_pot, sc, col_errs),
         [(col_lines, LANES), tile, (by_col, 8, LANES)],
-        [], 8 * mib, "finish",
+        [], 8 * mib,
     )
     got, row_errs = lax.optimization_barrier((exchange(out, COLS_OVER), row_errs))
     col_vec = jnp.sum(got[:, 0, :ITERS], axis=0)

time: 502 us -> 933 us (1.86)
  Pallas kernels: 241 us -> 685 us
  starting transfers between devices: 72.9 us -> 63.5 us
    pallas_call x21, Pallas kernels: 241 us -> 685 us  [call(): pl.pallas_call(kernel, in_specs=[on_chip() for _ in args], out_specs=[on_...]
    ppermute x36, starting transfers between devices: 72.9 us -> 63.5 us  [swapped(): return lax.ppermute(x, axis, [(i, i ^ by) for i in range(count)])]
where the time goes in v5:
time: 933 us; the launch traced here: 932 us
  Pallas kernels  685 us (73%)
  blocking collectives  150 us (16%)
  starting transfers between devices  63.5 us (7%)
  waiting for transfers between devices  28.8 us (3%)
    pallas_call x21, Pallas kernels, call(): pl.pallas_call(kernel, in_specs=[on_chip() for _ in args], out_specs=[on_...  685 us
    all_to_all x12, blocking collectives, exchange(): return lax.all_to_all(x, axis, split_axis=0, concat_axis=0, tiled=True)  150 us
    ppermute x36, starting transfers between devices, swapped(): return lax.ppermute(x, axis, [(i, i ^ by) for i in range(count)])  63.5 us
    ppermute x36, waiting for transfers between devices, swapped(): return lax.ppermute(x, axis, [(i, i ^ by) for i in range(count)])  28.8 us
  transfers between devices with their start and end apart: 36, of which 26 were waited for; matrix products, arithmetic and copies ran while one was open for 0% of the time, Pallas kernels for 0%

profile of v5, /device:TPU:1, one launch (start us, length us, event | category | flops | bytes accessed | tf_op | source)
XLA Modules:
  0.0 932.5 jit_solution(11446407122494204102)
XLA Ops:
  18.6 43.5 %shard_map.68 = (f32[32,128]{1,0:T(8,128)S(1)}, f32[8,128]{1,0:T(8,128)S(1)}, f32[16,128]{1,0:T(8,128)S(1)}, f32[32,8,128]{2,1,0:T(8,128)S(1)}) custom-call(f32[8,40,128]{2,1,0:T(8,128)S(1)} %all_to_all.60.refs_0_, f32[32,128]{1,0:T(8,128)S(1)} %bitcast.7, f32[32,128]{1,0:T(8,128)S(1)} %broadcast_in_dim.9.refs_2_, ...), custom_call_target="tpu_custom_call" | custom-call | tf_op jit(solution)/shard_map/pallas_call | solution.py:353
  62.1 20.2 %all_to_all.61.recv_ref = f32[32,8,128]{2,1,0:T(8,128)S(1)} all-to-all(f32[32,8,128]{2,1,0:T(8,128)S(1)} %get-tuple-element.91), channel_id=1, replica_groups=mesh['gx'=8,'gz'=4,'gy'=8] {'gx','gz'}, dimensions={0} | all-to-all | bytes 262144 | tf_op jit(solution)/shard_map/all_to_all | solution.py:364
  82.3 27.5 %shard_map.69 = (f32[4,128]{1,0:T(4,128)S(1)}, f32[8,128]{1,0:T(8,128)S(1)}, f32[16,128]{1,0:T(8,128)S(1)}, f32[32,128]{1,0:T(8,128)S(1)}) custom-call(f32[32,8,128]{2,1,0:T(8,128)S(1)} %all_to_all.61.recv_ref, f32[4,128]{1,0:T(4,128)S(1)} %bitcast.18, f32[4,128]{1,0:T(4,128)S(1)} %broadcast_in_dim.11.gprev_ref, ...), custom_call_target="tpu_custom_call" | custom-call | tf_op jit(solution)/shard_map/pallas_call | solution.py:353
  119.1 43.4 %shard_map.70 = (f32[32,128]{1,0:T(8,128)S(1)}, f32[8,128]{1,0:T(8,128)S(1)}, f32[16,128]{1,0:T(8,128)S(1)}, f32[32,4,128]{2,1,0:T(4,128)S(1)}) custom-call(f32[32,128]{1,0:T(8,128)S(1)} %multiply_add_fusion.8.refs_0_, f32[32,128]{1,0:T(8,128)S(1)} %collective-permute-done.1.refs_1_, f32[32,128]{1,0:T(8,128)S(1)} %collective-permute-done.2.refs_2_, ...), custom_call_target="tpu_custom_call" | custom-call | tf_op jit(solution)/shard_map/pallas_call | solution.py:353
  174.3 27.4 %shard_map.71 = (f32[4,128]{1,0:T(4,128)S(1)}, f32[8,128]{1,0:T(8,128)S(1)}, f32[16,128]{1,0:T(8,128)S(1)}, f32[32,128]{1,0:T(8,128)S(1)}) custom-call(f32[32,4,128]{2,1,0:T(4,128)S(1)} %all_to_all.62.recv_ref, f32[4,128]{1,0:T(4,128)S(1)} %bitcast.19, f32[4,128]{1,0:T(4,128)S(1)} %get-tuple-element.98.gprev_ref, ...), custom_call_target="tpu_custom_call" | custom-call | tf_op jit(solution)/shard_map/pallas_call | solution.py:353
  212.9 43.4 %shard_map.72 = (f32[32,128]{1,0:T(8,128)S(1)}, f32[8,128]{1,0:T(8,128)S(1)}, f32[16,128]{1,0:T(8,128)S(1)}, f32[32,4,128]{2,1,0:T(4,128)S(1)}) custom-call(f32[32,128]{1,0:T(8,128)S(1)} %multiply_add_fusion.7.refs_0_, f32[32,128]{1,0:T(8,128)S(1)} %collective-permute-done.5.refs_1_, f32[32,128]{1,0:T(8,128)S(1)} %collective-permute-done.6.refs_2_, ...), custom_call_target="tpu_custom_call" | custom-call | tf_op jit(solution)/shard_map/pallas_call | solution.py:353
  256.4 11.8 %all_to_all.63.recv_ref = f32[32,4,128]{2,1,0:T(4,128)S(1)} all-to-all(f32[32,4,128]{2,1,0:T(4,128)S(1)} %get-tuple-element.105), channel_id=1, replica_groups=mesh['gx'=8,'gz'=4,'gy'=8] {'gx','gz'}, dimensions={0} | all-to-all | bytes 131072 | tf_op jit(solution)/shard_map/all_to_all | solution.py:364
  268.2 27.4 %shard_map.73 = (f32[4,128]{1,0:T(4,128)S(1)}, f32[8,128]{1,0:T(8,128)S(1)}, f32[16,128]{1,0:T(8,128)S(1)}, f32[32,128]{1,0:T(8,128)S(1)}) custom-call(f32[32,4,128]{2,1,0:T(4,128)S(1)} %all_to_all.63.recv_ref, f32[4,128]{1,0:T(4,128)S(1)} %bitcast.20, f32[4,128]{1,0:T(4,128)S(1)} %get-tuple-element.106.gprev_ref, ...), custom_call_target="tpu_custom_call" | custom-call | tf_op jit(solution)/shard_map/pallas_call | solution.py:353
  304.0 43.4 %shard_map.74 = (f32[32,128]{1,0:T(8,128)S(1)}, f32[8,128]{1,0:T(8,128)S(1)}, f32[16,128]{1,0:T(8,128)S(1)}, f32[32,4,128]{2,1,0:T(4,128)S(1)}) custom-call(f32[32,128]{1,0:T(8,128)S(1)} %multiply_add_fusion.6.refs_0_, f32[32,128]{1,0:T(8,128)S(1)} %collective-permute-done.9.refs_1_, f32[32,128]{1,0:T(8,128)S(1)} %collective-permute-done.10.refs_2_, ...), custom_call_target="tpu_custom_call" | custom-call | tf_op jit(solution)/shard_map/pallas_call | solution.py:353
  347.5 12.1 %all_to_all.64.recv_ref = f32[32,4,128]{2,1,0:T(4,128)S(1)} all-to-all(f32[32,4,128]{2,1,0:T(4,128)S(1)} %get-tuple-element.113), channel_id=1, replica_groups=mesh['gx'=8,'gz'=4,'gy'=8] {'gx','gz'}, dimensions={0} | all-to-all | bytes 131072 | tf_op jit(solution)/shard_map/all_to_all | solution.py:364
  359.6 27.4 %shard_map.75 = (f32[4,128]{1,0:T(4,128)S(1)}, f32[8,128]{1,0:T(8,128)S(1)}, f32[16,128]{1,0:T(8,128)S(1)}, f32[32,128]{1,0:T(8,128)S(1)}) custom-call(f32[32,4,128]{2,1,0:T(4,128)S(1)} %all_to_all.64.recv_ref, f32[4,128]{1,0:T(4,128)S(1)} %bitcast.21, f32[4,128]{1,0:T(4,128)S(1)} %get-tuple-element.114.gprev_ref, ...), custom_call_target="tpu_custom_call" | custom-call | tf_op jit(solution)/shard_map/pallas_call | solution.py:353
  397.6 43.4 %shard_map.76 = (f32[32,128]{1,0:T(8,128)S(1)}, f32[8,128]{1,0:T(8,128)S(1)}, f32[16,128]{1,0:T(8,128)S(1)}, f32[32,4,128]{2,1,0:T(4,128)S(1)}) custom-call(f32[32,128]{1,0:T(8,128)S(1)} %multiply_add_fusion.5.refs_0_, f32[32,128]{1,0:T(8,128)S(1)} %collective-permute-done.13.refs_1_, f32[32,128]{1,0:T(8,128)S(1)} %collective-permute-done.14.refs_2_, ...), custom_call_target="tpu_custom_call" | custom-call | tf_op jit(solution)/shard_map/pallas_call | solution.py:353
  441.1 11.8 %all_to_all.65.recv_ref = f32[32,4,128]{2,1,0:T(4,128)S(1)} all-to-all(f32[32,4,128]{2,1,0:T(4,128)S(1)} %get-tuple-element.121), channel_id=1, replica_groups=mesh['gx'=8,'gz'=4,'gy'=8] {'gx','gz'}, dimensions={0} | all-to-all | bytes 131072 | tf_op jit(solution)/shard_map/all_to_all | solution.py:364
  452.9 27.4 %shard_map.77 = (f32[4,128]{1,0:T(4,128)S(1)}, f32[8,128]{1,0:T(8,128)S(1)}, f32[16,128]{1,0:T(8,128)S(1)}, f32[32,128]{1,0:T(8,128)S(1)}) custom-call(f32[32,4,128]{2,1,0:T(4,128)S(1)} %all_to_all.65.recv_ref, f32[4,128]{1,0:T(4,128)S(1)} %bitcast.22, f32[4,128]{1,0:T(4,128)S(1)} %get-tuple-element.122.gprev_ref, ...), custom_call_target="tpu_custom_call" | custom-call | tf_op jit(solution)/shard_map/pallas_call | solution.py:353
  490.5 43.4 %shard_map.78 = (f32[32,128]{1,0:T(8,128)S(1)}, f32[8,128]{1,0:T(8,128)S(1)}, f32[16,128]{1,0:T(8,128)S(1)}, f32[32,4,128]{2,1,0:T(4,128)S(1)}) custom-call(f32[32,128]{1,0:T(8,128)S(1)} %multiply_add_fusion.4.refs_0_, f32[32,128]{1,0:T(8,128)S(1)} %collective-permute-done.17.refs_1_, f32[32,128]{1,0:T(8,128)S(1)} %collective-permute-done.18.refs_2_, ...), custom_call_target="tpu_custom_call" | custom-call | tf_op jit(solution)/shard_map/pallas_call | solution.py:353
  545.7 27.4 %shard_map.79 = (f32[4,128]{1,0:T(4,128)S(1)}, f32[8,128]{1,0:T(8,128)S(1)}, f32[16,128]{1,0:T(8,128)S(1)}, f32[32,128]{1,0:T(8,128)S(1)}) custom-call(f32[32,4,128]{2,1,0:T(4,128)S(1)} %all_to_all.66.recv_ref, f32[4,128]{1,0:T(4,128)S(1)} %bitcast.23, f32[4,128]{1,0:T(4,128)S(1)} %get-tuple-element.130.gprev_ref, ...), custom_call_target="tpu_custom_call" | custom-call | tf_op jit(solution)/shard_map/pallas_call | solution.py:353
  583.9 43.4 %shard_map.80 = (f32[32,128]{1,0:T(8,128)S(1)}, f32[8,128]{1,0:T(8,128)S(1)}, f32[16,128]{1,0:T(8,128)S(1)}, f32[32,4,128]{2,1,0:T(4,128)S(1)}) custom-call(f32[32,128]{1,0:T(8,128)S(1)} %multiply_add_fusion.3.refs_0_, f32[32,128]{1,0:T(8,128)S(1)} %collective-permute-done.21.refs_1_, f32[32,128]{1,0:T(8,128)S(1)} %collective-permute-done.22.refs_2_, ...), custom_call_target="tpu_custom_call" | custom-call | tf_op jit(solution)/shard_map/pallas_call | solution.py:353
  639.2 27.4 %shard_map.81 = (f32[4,128]{1,0:T(4,128)S(1)}, f32[8,128]{1,0:T(8,128)S(1)}, f32[16,128]{1,0:T(8,128)S(1)}, f32[32,128]{1,0:T(8,128)S(1)}) custom-call(f32[32,4,128]{2,1,0:T(4,128)S(1)} %all_to_all.67.recv_ref, f32[4,128]{1,0:T(4,128)S(1)} %bitcast.24, f32[4,128]{1,0:T(4,128)S(1)} %get-tuple-element.138.gprev_ref, ...), custom_call_target="tpu_custom_call" | custom-call | tf_op jit(solution)/shard_map/pallas_call | solution.py:353
  677.2 43.4 %shard_map.82 = (f32[32,128]{1,0:T(8,128)S(1)}, f32[8,128]{1,0:T(8,128)S(1)}, f32[16,128]{1,0:T(8,128)S(1)}, f32[32,4,128]{2,1,0:T(4,128)S(1)}) custom-call(f32[32,128]{1,0:T(8,128)S(1)} %multiply_add_fusion.2.refs_0_, f32[32,128]{1,0:T(8,128)S(1)} %collective-permute-done.25.refs_1_, f32[32,128]{1,0:T(8,128)S(1)} %collective-permute-done.26.refs_2_, ...), custom_call_target="tpu_custom_call" | custom-call | tf_op jit(solution)/shard_map/pallas_call | solution.py:353
  732.4 27.4 %shard_map.83 = (f32[4,128]{1,0:T(4,128)S(1)}, f32[8,128]{1,0:T(8,128)S(1)}, f32[16,128]{1,0:T(8,128)S(1)}, f32[32,128]{1,0:T(8,128)S(1)}) custom-call(f32[32,4,128]{2,1,0:T(4,128)S(1)} %all_to_all.68.recv_ref, f32[4,128]{1,0:T(4,128)S(1)} %bitcast.25, f32[4,128]{1,0:T(4,128)S(1)} %get-tuple-element.146.gprev_ref, ...), custom_call_target="tpu_custom_call" | custom-call | tf_op jit(solution)/shard_map/pallas_call | solution.py:353
  770.7 43.4 %shard_map.84 = (f32[32,128]{1,0:T(8,128)S(1)}, f32[8,128]{1,0:T(8,128)S(1)}, f32[16,128]{1,0:T(8,128)S(1)}, f32[32,4,128]{2,1,0:T(4,128)S(1)}) custom-call(f32[32,128]{1,0:T(8,128)S(1)} %multiply_add_fusion.1.refs_0_, f32[32,128]{1,0:T(8,128)S(1)} %collective-permute-done.29.refs_1_, f32[32,128]{1,0:T(8,128)S(1)} %collective-permute-done.30.refs_2_, ...), custom_call_target="tpu_custom_call" | custom-call | tf_op jit(solution)/shard_map/pallas_call | solution.py:353
  825.9 27.4 %shard_map.85 = (f32[4,128]{1,0:T(4,128)S(1)}, f32[8,128]{1,0:T(8,128)S(1)}, f32[16,128]{1,0:T(8,128)S(1)}, f32[32,128]{1,0:T(8,128)S(1)}) custom-call(f32[32,4,128]{2,1,0:T(4,128)S(1)} %all_to_all.69.recv_ref, f32[4,128]{1,0:T(4,128)S(1)} %bitcast.26, f32[4,128]{1,0:T(4,128)S(1)} %get-tuple-element.154.gprev_ref, ...), custom_call_target="tpu_custom_call" | custom-call | tf_op jit(solution)/shard_map/pallas_call | solution.py:353
  863.7 44.0 %shard_map.86 = (f32[32,128]{1,0:T(8,128)}, f32[8,128]{1,0:T(8,128)S(1)}, f32[16,128]{1,0:T(8,128)}, f32[32,8,128]{2,1,0:T(8,128)S(1)}) custom-call(f32[32,128]{1,0:T(8,128)S(1)} %multiply_add_fusion.refs_0_, f32[32,128]{1,0:T(8,128)S(1)} %collective-permute-done.33.refs_1_, f32[32,128]{1,0:T(8,128)S(1)} %collective-permute-done.34.refs_2_, ...), custom_call_target="tpu_custom_call" | custom-call | tf_op jit(solution)/shard_map/pallas_call | solution.py:353
  907.8 12.4 %all_to_all.70.recv_ref = f32[32,8,128]{2,1,0:T(8,128)S(1)} all-to-all(f32[32,8,128]{2,1,0:T(8,128)S(1)} %get-tuple-element.162), channel_id=1, replica_groups=mesh['gx'=8,'gz'=4,'gy'=8] {'gx','gz'}, dimensions={0} | all-to-all | bytes 262144 | tf_op jit(solution)/shard_map/all_to_all | solution.py:364
  (107 shorter events, 181.9 us)
Async XLA Ops:
  113.1 3.9 collective-permute-start.1
  113.5 4.1 collective-permute-start.2
  201.7 4.4 collective-permute-start.4
  206.1 3.9 collective-permute-start.5
  206.2 4.3 collective-permute-start.6
  295.6 4.2 collective-permute-start.8
  299.8 4.2 collective-permute-start.10
  300.0 4.0 collective-permute-start.11
  390.7 4.1 collective-permute-start.13
  392.3 4.1 collective-permute-start.14
  393.5 4.1 collective-permute-start.15
  480.3 4.0 collective-permute-start.16
  484.3 3.9 collective-permute-start.17
  484.4 4.3 collective-permute-start.18
  573.1 4.1 collective-permute-start.20
  577.3 3.9 collective-permute-start.21
  577.4 4.2 collective-permute-start.22
  666.5 4.2 collective-permute-start.24
  670.8 4.2 collective-permute-start.25
  671.1 4.3 collective-permute-start.26
  759.8 4.2 collective-permute-start.28
  764.2 4.2 collective-permute-start.30
  853.3 4.2 collective-permute-start.32
  857.7 4.3 collective-permute-start.34
  (17 other events, 148.6 us)

commit v6 on v5

--- a/solution.py
+++ b/solution.py
@@ -7,7 +7,6 @@
 from jax.experimental import pallas as pl
 from jax.experimental.pallas import tpu as pltpu
 from jax.sharding import PartitionSpec as P
-
 
 ITERS = 10
 ROWS_OVER = ("gx", "gz")
@@ -106,7 +105,7 @@
         norms = kappa * (cross_of(ones, upper) + cross_of(ones, lower))
         tiles = wide // LANES
         here = [slice(t * LANES, (t + 1) * LANES) for t in range(tiles)]
-        tops = [[None] * 2 for _ in range(tiles)]
+        tops = [[None] * 2 for t in range(tiles)]
         for j in range(cols // 8):
             line = slice(8 * j, 8 * j + 8)
             cs = cs_ref[line, :]
@@ -115,7 +114,7 @@
                 tops[t][j % 2] = z if j < 2 else jnp.maximum(tops[t][j % 2], z)
         tops = [jnp.max(jnp.maximum(*pair), axis=0, keepdims=True) for pair in tops]
         spans = [jnp.broadcast_to(top, (8, LANES)) for top in tops]
-        sums = [[None] * 2 for _ in range(tiles)]
+        sums = [[None] * 2 for t in range(tiles)]
         for j in range(cols // 8):
             line = slice(8 * j, 8 * j + 8)
             cs = cs_ref[line, :]
@@ -137,28 +136,64 @@
     spread(out_ref, l_ref[...], mass)
 
 
-def exact_rows(kappa, x_ref, y_ref, gcol_ref, xs_ref, l_ref):
+def widen_kernel(
+    kappa, recv_ref, x_ref, other_ref, cm_ref, xs_ref, k_ref, mr_ref, y_ref, cmb_ref, cs_ref, base_ref
+):
+    cols, rows = k_ref.shape
+    lines, col_lines = rows // LANES, cm_ref.shape[0]
+    lse = joined([recv_ref[d, 0:lines, :] for d in range(recv_ref.shape[0])])
+    mr_ref[...] = lse
+    base_ref[...] = lse + xs_ref[...]
+    y_ref[...] = other_ref[0:cols, :].astype(jnp.bfloat16)
+    cs_ref[...] = jnp.broadcast_to(scaled_norms(other_ref[0:cols, :], kappa), (cols, LANES))
+    cmb_ref[0:col_lines, :] = cm_ref[...]
+    cmb_ref[col_lines : 2 * col_lines, :] = other_ref[cols : cols + col_lines, :]
+    wide = 1024
+    tiles = wide // LANES
+
+    def chunk(c, carry):
+        at = pl.multiple_of(c * wide, wide)
+        kc_ref = k_ref.at[:, pl.ds(at, wide)]
+        kc_ref[...] = cross_of(y_ref[...], x_ref[pl.ds(at, wide), :]) * (2.0 * kappa)
+        spans = [jnp.broadcast_to(base_ref[pl.ds(c * tiles + t, 1), :], (8, LANES)) for t in range(tiles)]
+        for j in range(cols // 8):
+            line = slice(8 * j, 8 * j + 8)
+            cs = cs_ref[line, :]
+            for t in range(tiles):
+                across = slice(t * LANES, (t + 1) * LANES)
+                kc_ref[line, across] = jnp.exp2(kc_ref[line, across] - cs - spans[t])
+        return carry
+
+    lax.fori_loop(0, rows // wide, chunk, 0)
+
+
+def exact_rows(kappa, x_ref, y_refs, gcol_ref, xs_ref, l_ref):
     def chunk(c, carry):
         xb = x_ref[pl.ds(pl.multiple_of(c * LANES, LANES), LANES), :]
 
-        def part(b, kept):
+        def part(b, kept, y_ref, first):
             top, weight = kept
-            here = pl.ds(pl.multiple_of(b * LANES, LANES), LANES)
-            y = y_ref[here, :]
-            z = cross_of(y, xb) * (2.0 * kappa) - scaled_norms(y, kappa) + gcol_ref[here, :]
+            y = y_ref[pl.ds(pl.multiple_of(b * LANES, LANES), LANES), :]
+            gain = gcol_ref[pl.ds(pl.multiple_of(first + b * LANES, LANES), LANES), :]
+            z = cross_of(y, xb) * (2.0 * kappa) - scaled_norms(y, kappa) + gain
             newtop = jnp.maximum(top, jnp.max(z, axis=0, keepdims=True))
             added = jnp.sum(jnp.exp2(z - newtop), axis=0, keepdims=True)
             return newtop, weight * jnp.exp2(top - newtop) + added
 
-        nothing = (jnp.full((1, LANES), -jnp.inf, f32), jnp.zeros((1, LANES), f32))
-        top, weight = lax.fori_loop(0, y_ref.shape[0] // LANES, part, nothing)
+        kept = (jnp.full((1, LANES), -jnp.inf, f32), jnp.zeros((1, LANES), f32))
+        first = 0
+        for y_ref in y_refs:
+            one = functools.partial(part, y_ref=y_ref, first=first)
+            kept = lax.fori_loop(0, y_ref.shape[0] // LANES, one, kept)
+            first += y_ref.shape[0]
+        top, weight = kept
         l_ref[pl.ds(c, 1), :] = top - xs_ref[pl.ds(c, 1), :] + log2(weight)
         return carry
 
     lax.fori_loop(0, x_ref.shape[0] // LANES, chunk, 0)
 
 
-def exact_cols(kappa, x_ref, y_ref, fx_ref, s_ref, top_ref, weight_ref):
+def exact_cols(kappa, x_ref, y_ref, first, fx_ref, s_ref, top_ref, weight_ref):
     lane, sub = lane_and_sublane()
 
     def part(b, carry):
@@ -181,7 +216,7 @@
         line = jnp.zeros((8, LANES), f32)
         for q in range(LANES // 8):
             line = line + jnp.where(lane == sub + 8 * q, lse[8 * q : 8 * q + 8, :], 0.0)
-        s_ref[pl.ds(b, 1), :] = jnp.sum(line, axis=0, keepdims=True)
+        s_ref[pl.ds(first + b, 1), :] = jnp.sum(line, axis=0, keepdims=True)
         return carry
 
     lax.fori_loop(0, y_ref.shape[0] // LANES, part, 0)
@@ -189,7 +224,7 @@
 
 def col_kernel(kappa, index, last, count, *refs):
     got, refs = refs[:count], refs[count:]
-    rm_ref, fprev_ref, mr_ref, xs_ref, sc_ref, errs_ref, k_ref, x_ref, y_ref, *refs = refs
+    rm_ref, fprev_ref, mr_ref, mr2_ref, xs_ref, sc_ref, errs_ref, k_ref, k2_ref, x_ref, y_ref, y2_ref, *refs = refs
     f_ref, sc_out_ref, errs_out_ref, out_ref, *refs = refs
     acc_ref, s_ref, fx_ref, top_ref, weight_ref = refs
     rows, cols = k_ref.shape[1], k_ref.shape[0]
@@ -208,43 +243,40 @@
         f_new = la - lse
         mass_b = total(jnp.sum(recv_ref[:, lines : lines + 1, :], axis=0))
         sc = jnp.where(sub == 1, mass_b, 0.0)
-        u = f_new + mr_ref[...]
-        newest = largest(u)
+        u = [f_new + ref[...] for ref in (mr_ref, mr2_ref)]
+        newest = [largest(part) for part in u]
         high = newest
     else:
         mass_a = sc[0:1, :]
         shift = log2(mass_a)
         f_new = la - shift - lse
-        u = f_new + mr_ref[...]
-        high = sc[2:3, :]
+        u = [f_new + ref[...] for ref in (mr_ref, mr2_ref)]
+        high = [sc[2:3, :], sc[4:5, :]]
         f_old = fprev_ref[...]
         share = mass / mass_a
         if index == 1:
             errs = noted(errs, 0, jnp.abs(jnp.exp2(la - f_old) - share))
             f_old = f_old - shift
-            high = high - shift
+            high = [part - shift for part in high]
         errs = noted(errs, index, jnp.abs(jnp.exp2(la - shift + (f_old - f_new)) - share))
-        newest = largest(u)
-    weights = jnp.exp2(u - high)
-    us = [jnp.broadcast_to(weights[l : l + 1, :], (8, LANES)) for l in range(lines)]
+        newest = [largest(part) for part in u]
     together = 8
-
-    def group(t, carry):
-        acc = [None] * together
-        lines_at = [pl.ds(pl.multiple_of((t * together + q) * 8, 8), 8) for q in range(together)]
-        for q in range(together):
-            parts = [None] * 2
-            for l in range(lines):
-                across = slice(l * LANES, (l + 1) * LANES)
-                term = k_ref[lines_at[q], across] * us[l]
-                parts[l % 2] = term if parts[l % 2] is None else parts[l % 2] + term
-            acc[q] = parts[0] + parts[1]
-        for q in range(together):
-            acc_ref[lines_at[q], :] = acc[q]
-        return carry
-
-    lax.fori_loop(0, cols // (8 * together), group, 0)
-    for t in range(cols // LANES):
+    for half, matrix in enumerate((k_ref, k2_ref)):
+        weights = jnp.exp2(u[half] - high[half])
+        us = [jnp.broadcast_to(weights[l : l + 1, :], (8, LANES)) for l in range(lines)]
+
+        def group(t, carry, us=us, matrix=matrix, first=half * cols):
+            for q in range(together):
+                line = pl.ds(pl.multiple_of((t * together + q) * 8, 8), 8)
+                parts = [None] * 2
+                for l in range(lines):
+                    term = matrix[line, l * LANES : (l + 1) * LANES] * us[l]
+                    parts[l % 2] = term if parts[l % 2] is None else parts[l % 2] + term
+                acc_ref[pl.ds(pl.multiple_of(first + (t * together + q) * 8, 8), 8), :] = parts[0] + parts[1]
+            return carry
+
+        lax.fori_loop(0, cols // (8 * together), group, 0)
+    for t in range(2 * cols // LANES):
         picked = []
         for q in range(LANES // 8):
             at = t * LANES + 8 * q
@@ -254,25 +286,28 @@
     sums = s_ref[...]
     extra = None
     if index == 0:
-        extra = jnp.broadcast_to(jnp.sum(mass, axis=0, keepdims=True), (4, LANES))
+        extra = jnp.broadcast_to(jnp.sum(mass, axis=0, keepdims=True), (8, LANES))
     elif last:
-        extra = jnp.broadcast_to(along_lanes(errs), (4, LANES))
-    spread(out_ref, high + log2(sums), extra)
+        extra = jnp.broadcast_to(along_lanes(errs), (8, LANES))
+    own = lax.broadcasted_iota(jnp.int32, sums.shape, 0) < cols // LANES
+    spread(out_ref, jnp.where(own, high[0], high[1]) + log2(sums), extra)
     f_ref[...] = f_new * (eps / LOG2E) if last else f_new
-    sc_out_ref[...] = jnp.where(sub == 2, newest, sc)
+    sc_out_ref[...] = jnp.where(sub == 2, newest[0], jnp.where(sub == 4, newest[1], sc))
     errs_out_ref[...] = errs
-    least = jnp.min(jnp.where(newest - high <= DRIFT, sums, 0.0))
+    drift = jnp.maximum(newest[0] - high[0], newest[1] - high[1])
+    least = jnp.min(jnp.where(drift <= DRIFT, sums, 0.0))
 
     @pl.when(jnp.logical_not(least >= SMALLEST))
     def _():
         fx_ref[...] = f_new - xs_ref[...]
-        exact_cols(kappa, x_ref, y_ref, fx_ref, s_ref, top_ref, weight_ref)
+        exact_cols(kappa, x_ref, y_ref, 0, fx_ref, s_ref, top_ref, weight_ref)
+        exact_cols(kappa, x_ref, y2_ref, cols // LANES, fx_ref, s_ref, top_ref, weight_ref)
         spread(out_ref, s_ref[...], extra)
 
 
 def new_target(index, recv_ref, cm_ref, gprev_ref, sc, errs_ref):
     lines = cm_ref.shape[0]
-    _, sub = lane_and_sublane()
+    lane, sub = lane_and_sublane()
     lse = joined([recv_ref[d, 0:lines, :] for d in range(recv_ref.shape[0])])
     mass_b = sc[1:2, :]
     if index == 0:
@@ -282,19 +317,20 @@
     mass = cm_ref[...]
     lb = log2(mass) - log2(mass_b)
     g_new = lb - lse
-    errs = noted(errs_ref[...], index, jnp.abs(jnp.exp2(lb + (gprev_ref[...] - g_new)) - mass / mass_b))
+    terms = jnp.abs(jnp.exp2(lb + (gprev_ref[...] - g_new)) - mass / mass_b)
+    errs = noted(errs_ref[...], index, terms[0 : lines // 2, :])
     return g_new, sc, errs
 
 
 def row_kernel(
     kappa, index,
-    recv_ref, cm_ref, gprev_ref, mr_ref, xs_ref, sc_ref, errs_ref, k_ref, x_ref, y_ref,
+    recv_ref, cm_ref, gprev_ref, mr_ref, mr2_ref, xs_ref, sc_ref, errs_ref, k_ref, k2_ref, x_ref, y_ref, y2_ref,
     g_ref, sc_out_ref, errs_out_ref, out_ref,
     vbc_ref, r_ref, l_ref,
 ):
     rows, cols = k_ref.shape[1], k_ref.shape[0]
     lines = rows // LANES
-    _, sub = lane_and_sublane()
+    lane, sub = lane_and_sublane()
     sc = sc_ref[...]
     g_new, sc, errs = new_target(index, recv_ref, cm_ref, gprev_ref, sc, errs_ref)
     newest = largest(g_new)
@@ -306,39 +342,41 @@
     column_form(jnp.exp2(g_new - high), put)
     together, block = min(16, lines), 64
 
-    for first in range(0, lines, together):
-
-        def group(b, acc, first=first):
-            acc = list(acc)
-            for j in range(block // 8):
-                line = pl.ds(pl.multiple_of(b * block + 8 * j, 8), 8)
-                vj = vbc_ref[line, :]
-                for t in range(together):
-                    across = slice((first + t) * LANES, (first + t + 1) * LANES)
-                    acc[t] = acc[t] + k_ref[line, across] * vj
-            return tuple(acc)
-
-        acc = lax.fori_loop(0, cols // block, group, (jnp.zeros((8, LANES), f32),) * together)
-        for t in range(together):
-            r_ref[first + t : first + t + 1, :] = jnp.sum(acc[t], axis=0, keepdims=True)
-    sums = r_ref[...]
-    out_ref[...] = mr_ref[...] + (high + log2(sums))
+    for half, matrix in enumerate((k_ref, k2_ref)):
+        for first in range(0, lines, together):
+
+            def group(b, acc, first=first, matrix=matrix, start=half * cols):
+                acc = list(acc)
+                for j in range(block // 8):
+                    line = pl.ds(pl.multiple_of(b * block + 8 * j, 8), 8)
+                    vj = vbc_ref[pl.ds(pl.multiple_of(start + b * block + 8 * j, 8), 8), :]
+                    for t in range(together):
+                        across = slice((first + t) * LANES, (first + t + 1) * LANES)
+                        acc[t] = acc[t] + matrix[line, across] * vj
+                return tuple(acc)
+
+            acc = lax.fori_loop(0, cols // block, group, (jnp.zeros((8, LANES), f32),) * together)
+            for t in range(together):
+                at = half * lines + first + t
+                r_ref[at : at + 1, :] = jnp.sum(acc[t], axis=0, keepdims=True)
+    sums = [r_ref[0:lines, :], r_ref[lines : 2 * lines, :]]
+    out_ref[...] = joined([ref[...] + (high + log2(part)) for ref, part in zip((mr_ref, mr2_ref), sums)])
     g_ref[...] = g_new
     sc_out_ref[...] = jnp.where(sub == 3, newest, sc)
     errs_out_ref[...] = errs
-    least = jnp.min(jnp.where(newest - high <= DRIFT, sums, 0.0))
+    least = jnp.min(jnp.where(newest - high <= DRIFT, jnp.minimum(*sums), 0.0))
 
     @pl.when(jnp.logical_not(least >= SMALLEST))
     def _():
         column_form(g_new, put)
-        exact_rows(kappa, x_ref, y_ref, vbc_ref, xs_ref, l_ref)
+        exact_rows(kappa, x_ref, (y_ref, y2_ref), vbc_ref, xs_ref, l_ref)
         out_ref[...] = l_ref[...]
 
 
 def last_kernel(index, recv_ref, cm_ref, gprev_ref, sc_ref, errs_ref, g_ref, row_ref, out_ref):
     lines = cm_ref.shape[0]
-    g_new, _, errs = new_target(index, recv_ref, cm_ref, gprev_ref, sc_ref[...], errs_ref)
-    g_ref[...] = g_new * (eps / LOG2E)
+    g_new, sc, errs = new_target(index, recv_ref, cm_ref, gprev_ref, sc_ref[...], errs_ref)
+    g_ref[...] = g_new[0 : lines // 2, :] * (eps / LOG2E)
     row_ref[...] = jnp.broadcast_to(jnp.sum(recv_ref[:, lines : lines + 1, :], axis=0), (8, LANES))
     col_errs = jnp.broadcast_to(along_lanes(errs), (8, LANES))
     for d in range(out_ref.shape[0]):
@@ -349,7 +387,7 @@
     return pl.BlockSpec(memory_space=pltpu.VMEM)
 
 
-def call(kernel, args, outs, scratch, limit):
+def call(kernel, args, outs, scratch, limit, name):
     return pl.pallas_call(
         kernel,
         in_specs=[on_chip() for _ in args],
@@ -357,6 +395,7 @@
         out_shape=[jax.ShapeDtypeStruct(shape, f32) for shape in outs],
         scratch_shapes=[pltpu.VMEM(shape, f32) for shape in scratch],
         compiler_params=pltpu.CompilerParams(vmem_limit_bytes=limit),
+        name=name,
     )(*args)
 
 
@@ -364,14 +403,14 @@
     return lax.all_to_all(x, axis, split_axis=0, concat_axis=0, tiled=True)
 
 
-def paired(x, axis):
-    count = lax.axis_size(axis)
-
-    def swapped(x, by):
-        return lax.ppermute(x, axis, [(i, i ^ by) for i in range(count)])
-
+def swapped(x, by):
+    count = lax.axis_size(COLS_OVER)
+    return lax.ppermute(x, COLS_OVER, [(i, i ^ by) for i in range(count)])
+
+
+def paired(x):
     both = joined([x, swapped(x, 1)])
-    return (both, *(swapped(both, by) for by in range(2, count, 2)))
+    return (both, *(swapped(both, by) for by in range(2, lax.axis_size(COLS_OVER) // 2, 2)))
 
 
 def on_device(row_embed, col_embed, row_mass, col_mass):
@@ -384,46 +423,67 @@
     rm = row_mass.reshape(row_lines, LANES)
     cm = col_mass.reshape(col_lines, LANES)
     tile = (8, LANES)
+    padding = jnp.zeros((-col_lines % 8, LANES), f32)
+    other = swapped(jnp.concatenate([col_embed.astype(f32), cm, padding]), by_col // 2)
     mib = 1 << 20
     k, mr, xs, out = call(
         functools.partial(init_kernel, kappa),
         (row_embed, col_embed, cm),
         [(cols, rows), (row_lines, LANES), (row_lines, LANES), (by_col, row_lines + 8, LANES)],
         [(cols, LANES), (row_lines, LANES)],
-        24 * mib,
+        24 * mib, "init",
     )
     f_pot = jnp.zeros((row_lines, LANES), f32)
-    g_pot = jnp.zeros((col_lines, LANES), f32)
+    g_pot = jnp.zeros((2 * col_lines, LANES), f32)
     sc = jnp.zeros(tile, f32)
     noting = (16, LANES)
     row_errs = jnp.zeros(noting, f32)
     col_errs = jnp.zeros(noting, f32)
+    vmem = pltpu.VMEM
     for index in range(ITERS):
         last = index == ITERS - 1
-        got = (exchange(out, COLS_OVER),) if index == 0 else paired(out, COLS_OVER)
-        more = 4 if index == 0 or last else 0
+        if index == 0:
+            got = (exchange(out, COLS_OVER),)
+            k2, mr2, y2, cmb = pl.pallas_call(
+                functools.partial(widen_kernel, kappa),
+                in_specs=[on_chip() for _ in range(5)],
+                out_specs=[on_chip() for _ in range(4)],
+                out_shape=[
+                    jax.ShapeDtypeStruct((cols, rows), f32),
+                    jax.ShapeDtypeStruct((row_lines, LANES), f32),
+                    jax.ShapeDtypeStruct(col_embed.shape, col_embed.dtype),
+                    jax.ShapeDtypeStruct((2 * col_lines, LANES), f32),
+                ],
+                scratch_shapes=[vmem((cols, LANES), f32), vmem((row_lines, LANES), f32)],
+                compiler_params=pltpu.CompilerParams(vmem_limit_bytes=24 * mib),
+                name="widen",
+            )(got[0], row_embed, other, cm, xs)
+        else:
+            got = paired(out)
+        more = 8 if index == 0 or last else 0
+        fixed = (k, k2, row_embed, col_embed, y2)
         f_pot, sc, row_errs, out = call(
             functools.partial(col_kernel, kappa, index, last, len(got)),
-            (*got, rm, f_pot, mr, xs, sc, row_errs, k, row_embed, col_embed),
-            [(row_lines, LANES), tile, noting, (by_row, col_lines + more, LANES)],
-            [(cols, LANES), (col_lines, LANES), (row_lines, LANES), (LANES, LANES), (LANES, LANES)],
-            24 * mib,
+            (*got, rm, f_pot, mr, mr2, xs, sc, row_errs, *fixed),
+            [(row_lines, LANES), tile, noting, (by_row, 2 * col_lines + more, LANES)],
+            [(2 * cols, LANES), (2 * col_lines, LANES), (row_lines, LANES), (LANES, LANES), (LANES, LANES)],
+            24 * mib, f"cols{index}",
         )
         got = exchange(out, ROWS_OVER)
         if last:
             break
         g_pot, sc, col_errs, out = call(
             functools.partial(row_kernel, kappa, index),
-            (got, cm, g_pot, mr, xs, sc, col_errs, k, row_embed, col_embed),
-            [(col_lines, LANES), tile, noting, (row_lines, LANES)],
-            [(cols, LANES), (row_lines, LANES), (row_lines, LANES)],
-            24 * mib,
+            (got, cmb, g_pot, mr, mr2, xs, sc, col_errs, *fixed),
+            [(2 * col_lines, LANES), tile, noting, (row_lines, LANES)],
+            [(2 * cols, LANES), (2 * row_lines, LANES), (row_lines, LANES)],
+            24 * mib, f"rows{index}",
         )
     g_out, row_errs, out = call(
         functools.partial(last_kernel, ITERS - 1),
-        (got, cm, g_pot, sc, col_errs),
+        (got, cmb, g_pot, sc, col_errs),
         [(col_lines, LANES), tile, (by_col, 8, LANES)],
-        [], 8 * mib,
+        [], 8 * mib, "finish",
     )
     got, row_errs = lax.optimization_barrier((exchange(out, COLS_OVER), row_errs))
     col_vec = jnp.sum(got[:, 0, :ITERS], axis=0)

time: 933 us -> 1590 us (1.70)
  Pallas kernels: 685 us -> 1360 us
  starting transfers between devices: 63.5 us -> 33.8 us
    pallas_call x21, Pallas kernels: 685 us -> 1360 us  [call(): pl.pallas_call(kernel, in_specs=[on_chip() for _ in args], out_specs=[on_...]
    ppermute x36 -> x19, starting transfers between devices: 63.5 us -> 33.8 us  [swapped(): return lax.ppermute(x, COLS_OVER, [(i, i ^ by) for i in range(count)])]
  transfers between devices with their start and end apart: 36 -> 19, of which waited for: 26 -> 18; matrix products, arithmetic and copies ran while one was open for 0% -> 0% of each run, Pallas kernels for 0% -> 0%
where the time goes in v6:
time: 1590 us; the launch traced here: 1580 us
  Pallas kernels  1360 us (86%)
  blocking collectives  155 us (10%)
  starting transfers between devices  33.8 us (2%)
  waiting for transfers between devices  28.3 us (2%)
    pallas_call x21, Pallas kernels, call(): pl.pallas_call(kernel, in_specs=[on_chip() for _ in args], out_specs=[on_...  1360 us
    all_to_all x12, blocking collectives, exchange(): return lax.all_to_all(x, axis, split_axis=0, concat_axis=0, tiled=True)  155 us
    ppermute x19, starting transfers between devices, swapped(): return lax.ppermute(x, COLS_OVER, [(i, i ^ by) for i in range(count)])  33.8 us
  transfers between devices with their start and end apart: 19, of which 18 were waited for; matrix products, arithmetic and copies ran while one was open for 0% of the time, Pallas kernels for 0%

profile of v6, /device:TPU:1, one launch (start us, length us, event | category | flops | bytes accessed | tf_op | source)
XLA Modules:
  0.0 1584.1 jit_solution(15222605367111458101)
XLA Ops:
  25.5 86.5 %cols0.1 = (f32[32,128]{1,0:T(8,128)S(1)}, f32[8,128]{1,0:T(8,128)S(1)}, f32[16,128]{1,0:T(8,128)S(1)}, f32[32,16,128]{2,1,0:T(8,128)S(1)}) custom-call(f32[8,40,128]{2,1,0:T(8,128)S(1)} %all_to_all.60.recv_ref.refs_0_, f32[32,128]{1,0:T(8,128)S(1)} %bitcast.7, f32[32,128]{1,0:T(8,128)S(1)} %broadcast_in_dim.6.refs_2_, ...), custom_call_target="tpu_custom_call" | custom-call | tf_op jit(solution)/shard_map/cols0/pallas_call | solution.py:391
  112.0 21.2 %all_to_all.61.recv_ref = f32[32,16,128]{2,1,0:T(8,128)S(1)} all-to-all(f32[32,16,128]{2,1,0:T(8,128)S(1)} %get-tuple-element.98), channel_id=1, replica_groups=mesh['gx'=8,'gz'=4,'gy'=8] {'gx','gz'}, dimensions={0} | all-to-all | bytes 524288 | tf_op jit(solution)/shard_map/all_to_all | solution.py:403
  133.2 54.4 %rows0.1 = (f32[8,128]{1,0:T(8,128)S(1)}, f32[8,128]{1,0:T(8,128)S(1)}, f32[16,128]{1,0:T(8,128)S(1)}, f32[32,128]{1,0:T(8,128)S(1)}) custom-call(f32[32,16,128]{2,1,0:T(8,128)S(1)} %all_to_all.61.recv_ref, f32[8,128]{1,0:T(8,128)S(1)} %get-tuple-element.99.cm_ref, f32[8,128]{1,0:T(8,128)S(1)} %broadcast_7_refs_6__gprev_ref.2.refs_6_.gprev_ref, ...), custom_call_target="tpu_custom_call" | custom-call | tf_op jit(solution)/shard_map/rows0/pallas_call | solution.py:391
  193.8 86.5 %cols1.1 = (f32[32,128]{1,0:T(8,128)S(1)}, f32[8,128]{1,0:T(8,128)S(1)}, f32[16,128]{1,0:T(8,128)S(1)}, f32[32,8,128]{2,1,0:T(8,128)S(1)}) custom-call(f32[32,128]{1,0:T(8,128)S(1)} %multiply_add_fusion.8.refs_0_, f32[32,128]{1,0:T(8,128)S(1)} %collective-permute-done.2.refs_1_, f32[32,128]{1,0:T(8,128)S(1)} %bitcast.8, ...), custom_call_target="tpu_custom_call" | custom-call | tf_op jit(solution)/shard_map/cols1/pallas_call | solution.py:391
  280.2 13.0 all_to_all.62.recv_ref
  293.2 54.3 %rows1.1 = (f32[8,128]{1,0:T(8,128)S(1)}, f32[8,128]{1,0:T(8,128)S(1)}, f32[16,128]{1,0:T(8,128)S(1)}, f32[32,128]{1,0:T(8,128)S(1)}) custom-call(f32[32,8,128]{2,1,0:T(8,128)S(1)} %all_to_all.62.recv_ref, f32[8,128]{1,0:T(8,128)S(1)} %get-tuple-element.99.cm_ref, f32[8,128]{1,0:T(8,128)S(1)} %get-tuple-element.106.gprev_ref, ...), custom_call_target="tpu_custom_call" | custom-call | tf_op jit(solution)/shard_map/rows1/pallas_call | solution.py:391
  354.1 86.5 %cols2.1 = (f32[32,128]{1,0:T(8,128)S(1)}, f32[8,128]{1,0:T(8,128)S(1)}, f32[16,128]{1,0:T(8,128)S(1)}, f32[32,8,128]{2,1,0:T(8,128)S(1)}) custom-call(f32[32,128]{1,0:T(8,128)S(1)} %multiply_add_fusion.7.refs_0_, f32[32,128]{1,0:T(8,128)S(1)} %collective-permute-done.4.refs_1_, f32[32,128]{1,0:T(8,128)S(1)} %bitcast.9, ...), custom_call_target="tpu_custom_call" | custom-call | tf_op jit(solution)/shard_map/cols2/pallas_call | solution.py:391
  453.0 54.3 %rows2.1 = (f32[8,128]{1,0:T(8,128)S(1)}, f32[8,128]{1,0:T(8,128)S(1)}, f32[16,128]{1,0:T(8,128)S(1)}, f32[32,128]{1,0:T(8,128)S(1)}) custom-call(f32[32,8,128]{2,1,0:T(8,128)S(1)} %all_to_all.63.recv_ref, f32[8,128]{1,0:T(8,128)S(1)} %get-tuple-element.99.cm_ref, f32[8,128]{1,0:T(8,128)S(1)} %get-tuple-element.114.gprev_ref, ...), custom_call_target="tpu_custom_call" | custom-call | tf_op jit(solution)/shard_map/rows2/pallas_call | solution.py:391
  513.7 86.5 %cols3.1 = (f32[32,128]{1,0:T(8,128)S(1)}, f32[8,128]{1,0:T(8,128)S(1)}, f32[16,128]{1,0:T(8,128)S(1)}, f32[32,8,128]{2,1,0:T(8,128)S(1)}) custom-call(f32[32,128]{1,0:T(8,128)S(1)} %multiply_add_fusion.6.refs_0_, f32[32,128]{1,0:T(8,128)S(1)} %collective-permute-done.6.refs_1_, f32[32,128]{1,0:T(8,128)S(1)} %bitcast.10, ...), custom_call_target="tpu_custom_call" | custom-call | tf_op jit(solution)/shard_map/cols3/pallas_call | solution.py:391
  600.2 12.5 all_to_all.64.recv_ref
  612.6 54.3 %rows3.1 = (f32[8,128]{1,0:T(8,128)S(1)}, f32[8,128]{1,0:T(8,128)S(1)}, f32[16,128]{1,0:T(8,128)S(1)}, f32[32,128]{1,0:T(8,128)S(1)}) custom-call(f32[32,8,128]{2,1,0:T(8,128)S(1)} %all_to_all.64.recv_ref, f32[8,128]{1,0:T(8,128)S(1)} %get-tuple-element.99.cm_ref, f32[8,128]{1,0:T(8,128)S(1)} %get-tuple-element.122.gprev_ref, ...), custom_call_target="tpu_custom_call" | custom-call | tf_op jit(solution)/shard_map/rows3/pallas_call | solution.py:391
  673.6 86.5 %cols4.1 = (f32[32,128]{1,0:T(8,128)S(1)}, f32[8,128]{1,0:T(8,128)S(1)}, f32[16,128]{1,0:T(8,128)S(1)}, f32[32,8,128]{2,1,0:T(8,128)S(1)}) custom-call(f32[32,128]{1,0:T(8,128)S(1)} %multiply_add_fusion.5.refs_0_, f32[32,128]{1,0:T(8,128)S(1)} %collective-permute-done.8.refs_1_, f32[32,128]{1,0:T(8,128)S(1)} %bitcast.11, ...), custom_call_target="tpu_custom_call" | custom-call | tf_op jit(solution)/shard_map/cols4/pallas_call | solution.py:391
  772.4 54.3 %rows4.1 = (f32[8,128]{1,0:T(8,128)S(1)}, f32[8,128]{1,0:T(8,128)S(1)}, f32[16,128]{1,0:T(8,128)S(1)}, f32[32,128]{1,0:T(8,128)S(1)}) custom-call(f32[32,8,128]{2,1,0:T(8,128)S(1)} %all_to_all.65.recv_ref, f32[8,128]{1,0:T(8,128)S(1)} %get-tuple-element.99.cm_ref, f32[8,128]{1,0:T(8,128)S(1)} %get-tuple-element.130.gprev_ref, ...), custom_call_target="tpu_custom_call" | custom-call | tf_op jit(solution)/shard_map/rows4/pallas_call | solution.py:391
  833.1 86.5 %cols5.1 = (f32[32,128]{1,0:T(8,128)S(1)}, f32[8,128]{1,0:T(8,128)S(1)}, f32[16,128]{1,0:T(8,128)S(1)}, f32[32,8,128]{2,1,0:T(8,128)S(1)}) custom-call(f32[32,128]{1,0:T(8,128)S(1)} %multiply_add_fusion.4.refs_0_, f32[32,128]{1,0:T(8,128)S(1)} %collective-permute-done.10.refs_1_, f32[32,128]{1,0:T(8,128)S(1)} %bitcast.12, ...), custom_call_target="tpu_custom_call" | custom-call | tf_op jit(solution)/shard_map/cols5/pallas_call | solution.py:391
  931.9 54.3 %rows5.1 = (f32[8,128]{1,0:T(8,128)S(1)}, f32[8,128]{1,0:T(8,128)S(1)}, f32[16,128]{1,0:T(8,128)S(1)}, f32[32,128]{1,0:T(8,128)S(1)}) custom-call(f32[32,8,128]{2,1,0:T(8,128)S(1)} %all_to_all.66.recv_ref, f32[8,128]{1,0:T(8,128)S(1)} %get-tuple-element.99.cm_ref, f32[8,128]{1,0:T(8,128)S(1)} %get-tuple-element.138.gprev_ref, ...), custom_call_target="tpu_custom_call" | custom-call | tf_op jit(solution)/shard_map/rows5/pallas_call | solution.py:391
  992.9 86.5 %cols6.1 = (f32[32,128]{1,0:T(8,128)S(1)}, f32[8,128]{1,0:T(8,128)S(1)}, f32[16,128]{1,0:T(8,128)S(1)}, f32[32,8,128]{2,1,0:T(8,128)S(1)}) custom-call(f32[32,128]{1,0:T(8,128)S(1)} %multiply_add_fusion.3.refs_0_, f32[32,128]{1,0:T(8,128)S(1)} %collective-permute-done.12.refs_1_, f32[32,128]{1,0:T(8,128)S(1)} %bitcast.13, ...), custom_call_target="tpu_custom_call" | custom-call | tf_op jit(solution)/shard_map/cols6/pallas_call | solution.py:391
  1091.7 54.3 %rows6.1 = (f32[8,128]{1,0:T(8,128)S(1)}, f32[8,128]{1,0:T(8,128)S(1)}, f32[16,128]{1,0:T(8,128)S(1)}, f32[32,128]{1,0:T(8,128)S(1)}) custom-call(f32[32,8,128]{2,1,0:T(8,128)S(1)} %all_to_all.67.recv_ref, f32[8,128]{1,0:T(8,128)S(1)} %get-tuple-element.99.cm_ref, f32[8,128]{1,0:T(8,128)S(1)} %get-tuple-element.146.gprev_ref, ...), custom_call_target="tpu_custom_call" | custom-call | tf_op jit(solution)/shard_map/rows6/pallas_call | solution.py:391
  1152.4 86.5 %cols7.1 = (f32[32,128]{1,0:T(8,128)S(1)}, f32[8,128]{1,0:T(8,128)S(1)}, f32[16,128]{1,0:T(8,128)S(1)}, f32[32,8,128]{2,1,0:T(8,128)S(1)}) custom-call(f32[32,128]{1,0:T(8,128)S(1)} %multiply_add_fusion.2.refs_0_, f32[32,128]{1,0:T(8,128)S(1)} %collective-permute-done.14.refs_1_, f32[32,128]{1,0:T(8,128)S(1)} %bitcast.14, ...), custom_call_target="tpu_custom_call" | custom-call | tf_op jit(solution)/shard_map/cols7/pallas_call | solution.py:391
  1238.9 12.6 all_to_all.68.recv_ref
  1251.5 54.3 %rows7.1 = (f32[8,128]{1,0:T(8,128)S(1)}, f32[8,128]{1,0:T(8,128)S(1)}, f32[16,128]{1,0:T(8,128)S(1)}, f32[32,128]{1,0:T(8,128)S(1)}) custom-call(f32[32,8,128]{2,1,0:T(8,128)S(1)} %all_to_all.68.recv_ref, f32[8,128]{1,0:T(8,128)S(1)} %get-tuple-element.99.cm_ref, f32[8,128]{1,0:T(8,128)S(1)} %get-tuple-element.154.gprev_ref, ...), custom_call_target="tpu_custom_call" | custom-call | tf_op jit(solution)/shard_map/rows7/pallas_call | solution.py:391
  1312.0 86.5 %cols8.1 = (f32[32,128]{1,0:T(8,128)S(1)}, f32[8,128]{1,0:T(8,128)S(1)}, f32[16,128]{1,0:T(8,128)S(1)}, f32[32,8,128]{2,1,0:T(8,128)S(1)}) custom-call(f32[32,128]{1,0:T(8,128)S(1)} %multiply_add_fusion.1.refs_0_, f32[32,128]{1,0:T(8,128)S(1)} %collective-permute-done.16.refs_1_, f32[32,128]{1,0:T(8,128)S(1)} %bitcast.15, ...), custom_call_target="tpu_custom_call" | custom-call | tf_op jit(solution)/shard_map/cols8/pallas_call | solution.py:391
  1410.8 54.1 %rows8.1 = (f32[8,128]{1,0:T(8,128)S(1)}, f32[8,128]{1,0:T(8,128)S(1)}, f32[16,128]{1,0:T(8,128)S(1)}, f32[32,128]{1,0:T(8,128)S(1)}) custom-call(f32[32,8,128]{2,1,0:T(8,128)S(1)} %all_to_all.69.recv_ref, f32[8,128]{1,0:T(8,128)S(1)} %get-tuple-element.99.cm_ref, f32[8,128]{1,0:T(8,128)S(1)} %get-tuple-element.162.gprev_ref, ...), custom_call_target="tpu_custom_call" | custom-call | tf_op jit(solution)/shard_map/rows8/pallas_call | solution.py:391
  1471.7 87.1 %cols9.1 = (f32[32,128]{1,0:T(8,128)}, f32[8,128]{1,0:T(8,128)S(1)}, f32[16,128]{1,0:T(8,128)}, f32[32,16,128]{2,1,0:T(8,128)S(1)}) custom-call(f32[32,128]{1,0:T(8,128)S(1)} %multiply_add_fusion.refs_0_, f32[32,128]{1,0:T(8,128)S(1)} %collective-permute-done.18.refs_1_, f32[32,128]{1,0:T(8,128)S(1)} %bitcast.16, f32[32,128]{1,0:T(8,128)S(1)} %get-tuple-element.166.refs_3_, ...), custom_call_target="tpu_custom_call" | custom-call | tf_op jit(solution)/shard_map/cols9/pallas_call | solution.py:391
  1558.8 13.5 all_to_all.70.recv_ref
  (77 shorter events, 156.8 us)
Async XLA Ops:
  2.5 19.4 %collective-permute-start = (f32[520,128]{1,0:T(8,128)S(1)}, f32[520,128]{1,0:T(8,128)S(1)}, u32[]{:S(2)}, u32[]{:S(2)}) collective-permute-start(f32[520,128]{1,0:T(8,128)S(1)} %maximum_maximum_fusion), channel_id=1, source_target_pairs={{0,4},{1,5},{2,6},{3,7},{4,0},{5,1},{6,2},{7,3},{8,12},{9,13},{10,... | collective-permute-start | bytes 798728 | tf_op jit(solution)/shard_map/ppermute | solution.py:408
  6.3 1.2 copy-start
  7.5 0.9 copy-start.1
  8.4 0.7 copy-start.4
  23.8 0.9 copy-start.2
  24.7 0.7 copy-start.3
  187.6 3.5 collective-permute-start.1
  191.1 2.7 collective-permute-start.2
  347.5 4.0 collective-permute-start.3
  351.5 2.7 collective-permute-start.4
  507.3 3.7 collective-permute-start.5
  511.0 2.7 collective-permute-start.6
  666.9 4.0 collective-permute-start.7
  670.9 2.7 collective-permute-start.8
  826.7 3.7 collective-permute-start.9
  830.4 2.7 collective-permute-start.10
  986.2 4.0 collective-permute-start.11
  990.2 2.7 collective-permute-start.12
  1146.0 3.7 collective-permute-start.13
  1149.7 2.7 collective-permute-start.14
  1305.7 3.6 collective-permute-start.15
  1309.3 2.7 collective-permute-start.16
  1465.0 4.0 collective-permute-start.17
  1469.0 2.7 collective-permute-start.18

commit v7 on v6

--- a/solution.py
+++ b/solution.py
@@ -87,7 +87,7 @@
     return jnp.sum(picked, axis=0, keepdims=True)
 
 
-def init_kernel(kappa, x_ref, y_ref, cm_ref, k_ref, mr_ref, xs_ref, out_ref, cs_ref, l_ref):
+def init_kernel(kappa, x_ref, y_ref, cm_ref, k_ref, mr_ref, xs_ref, out_ref, own_ref, pack_ref, cs_ref, l_ref):
     cols = y_ref.shape[0]
     rows = x_ref.shape[0]
     wide = 1024
@@ -134,19 +134,23 @@
     lax.fori_loop(0, rows // wide, chunk, 0)
     mass = jnp.broadcast_to(jnp.sum(cm_ref[...], axis=0, keepdims=True), (8, LANES))
     spread(out_ref, l_ref[...], mass)
+    own_ref[...] = y_ref[...]
+    pack_ref[0:cols, :] = y_ref[...].astype(f32)
+    pack_ref[cols:, :] = jnp.zeros((pack_ref.shape[0] - cols, LANES), f32)
+    pack_ref[cols : cols + cm_ref.shape[0], :] = cm_ref[...]
 
 
 def widen_kernel(
-    kappa, recv_ref, x_ref, other_ref, cm_ref, xs_ref, k_ref, mr_ref, y_ref, cmb_ref, cs_ref, base_ref
+    kappa, col_lines, recv_ref, x_ref, other_ref, pack_ref, xs_ref, k_ref, mr_ref, y_ref, cmb_ref, cs_ref, base_ref
 ):
     cols, rows = k_ref.shape
-    lines, col_lines = rows // LANES, cm_ref.shape[0]
+    lines = rows // LANES
     lse = joined([recv_ref[d, 0:lines, :] for d in range(recv_ref.shape[0])])
     mr_ref[...] = lse
     base_ref[...] = lse + xs_ref[...]
     y_ref[...] = other_ref[0:cols, :].astype(jnp.bfloat16)
     cs_ref[...] = jnp.broadcast_to(scaled_norms(other_ref[0:cols, :], kappa), (cols, LANES))
-    cmb_ref[0:col_lines, :] = cm_ref[...]
+    cmb_ref[0:col_lines, :] = pack_ref[cols : cols + col_lines, :]
     cmb_ref[col_lines : 2 * col_lines, :] = other_ref[cols : cols + col_lines, :]
     wide = 1024
     tiles = wide // LANES
@@ -260,7 +264,7 @@
             high = [part - shift for part in high]
         errs = noted(errs, index, jnp.abs(jnp.exp2(la - shift + (f_old - f_new)) - share))
         newest = [largest(part) for part in u]
-    together = 8
+    together = 16 if cols % 128 == 0 else 8
     for half, matrix in enumerate((k_ref, k2_ref)):
         weights = jnp.exp2(u[half] - high[half])
         us = [jnp.broadcast_to(weights[l : l + 1, :], (8, LANES)) for l in range(lines)]
@@ -423,16 +427,22 @@
     rm = row_mass.reshape(row_lines, LANES)
     cm = col_mass.reshape(col_lines, LANES)
     tile = (8, LANES)
-    padding = jnp.zeros((-col_lines % 8, LANES), f32)
-    other = swapped(jnp.concatenate([col_embed.astype(f32), cm, padding]), by_col // 2)
     mib = 1 << 20
-    k, mr, xs, out = call(
+    shapes = [
+        ((cols, rows), f32), ((row_lines, LANES), f32), ((row_lines, LANES), f32),
+        ((by_col, row_lines + 8, LANES), f32), (col_embed.shape, col_embed.dtype),
+        ((cols + col_lines + -col_lines % 8, LANES), f32),
+    ]
+    k, mr, xs, out, col_embed, pack = pl.pallas_call(
         functools.partial(init_kernel, kappa),
-        (row_embed, col_embed, cm),
-        [(cols, rows), (row_lines, LANES), (row_lines, LANES), (by_col, row_lines + 8, LANES)],
-        [(cols, LANES), (row_lines, LANES)],
-        24 * mib, "init",
-    )
+        in_specs=[on_chip() for _ in range(3)],
+        out_specs=[on_chip() for _ in shapes],
+        out_shape=[jax.ShapeDtypeStruct(*shape) for shape in shapes],
+        scratch_shapes=[pltpu.VMEM((cols, LANES), f32), pltpu.VMEM((row_lines, LANES), f32)],
+        compiler_params=pltpu.CompilerParams(vmem_limit_bytes=24 * mib),
+        name="init",
+    )(row_embed, col_embed, cm)
+    other = swapped(pack, by_col // 2)
     f_pot = jnp.zeros((row_lines, LANES), f32)
     g_pot = jnp.zeros((2 * col_lines, LANES), f32)
     sc = jnp.zeros(tile, f32)
@@ -445,7 +455,7 @@
         if index == 0:
             got = (exchange(out, COLS_OVER),)
             k2, mr2, y2, cmb = pl.pallas_call(
-                functools.partial(widen_kernel, kappa),
+                functools.partial(widen_kernel, kappa, col_lines),
                 in_specs=[on_chip() for _ in range(5)],
                 out_specs=[on_chip() for _ in range(4)],
                 out_shape=[
@@ -457,7 +467,7 @@
                 scratch_shapes=[vmem((cols, LANES), f32), vmem((row_lines, LANES), f32)],
                 compiler_params=pltpu.CompilerParams(vmem_limit_bytes=24 * mib),
                 name="widen",
-            )(got[0], row_embed, other, cm, xs)
+            )(got[0], row_embed, other, pack, xs)
         else:
             got = paired(out)
         more = 8 if index == 0 or last else 0

time: 1590 us -> 1580 us (level)
    pallas_call x21 -> x20, Pallas kernels: 1360 us -> 1350 us  [call(): pl.pallas_call(kernel, in_specs=[on_chip() for _ in args], out_specs=[on_...]
where the time goes in v7:
time: 1580 us
  Pallas kernels  1360 us (86%)
  blocking collectives  156 us (10%)
  starting transfers between devices  37.6 us (2%)
  waiting for transfers between devices  24.9 us (2%)
    pallas_call x20, Pallas kernels, call(): pl.pallas_call(kernel, in_specs=[on_chip() for _ in args], out_specs=[on_...  1350 us
    all_to_all x12, blocking collectives, exchange(): return lax.all_to_all(x, axis, split_axis=0, concat_axis=0, tiled=True)  156 us
    ppermute x19, starting transfers between devices, swapped(): return lax.ppermute(x, COLS_OVER, [(i, i ^ by) for i in range(count)])  37.6 us
  transfers between devices with their start and end apart: 19, of which 18 were waited for; matrix products, arithmetic and copies ran while one was open for 0% of the time, Pallas kernels for 0%

profile of v7, /device:TPU:1, one launch (start us, length us, event | category | flops | bytes accessed | tf_op | source)
XLA Modules:
  0.0 1582.8 jit_solution(16993707091257303703)
XLA Ops:
  22.7 86.4 %cols0.1 = (f32[32,128]{1,0:T(8,128)S(1)}, f32[8,128]{1,0:T(8,128)S(1)}, f32[16,128]{1,0:T(8,128)S(1)}, f32[32,16,128]{2,1,0:T(8,128)S(1)}) custom-call(f32[8,40,128]{2,1,0:T(8,128)S(1)} %all_to_all.60.recv_ref.refs_0_, f32[32,128]{1,0:T(8,128)S(1)} %bitcast.7, f32[32,128]{1,0:T(8,128)S(1)} %broadcast_in_dim.3.refs_2_, ...), custom_call_target="tpu_custom_call" | custom-call | tf_op jit(solution)/shard_map/cols0/pallas_call | solution.py:395
  109.1 21.2 %all_to_all.61.recv_ref = f32[32,16,128]{2,1,0:T(8,128)S(1)} all-to-all(f32[32,16,128]{2,1,0:T(8,128)S(1)} %get-tuple-element.102), channel_id=1, replica_groups=mesh['gx'=8,'gz'=4,'gy'=8] {'gx','gz'}, dimensions={0} | all-to-all | bytes 524288 | tf_op jit(solution)/shard_map/all_to_all | solution.py:407
  130.3 54.5 %rows0.1 = (f32[8,128]{1,0:T(8,128)S(1)}, f32[8,128]{1,0:T(8,128)S(1)}, f32[16,128]{1,0:T(8,128)S(1)}, f32[32,128]{1,0:T(8,128)S(1)}) custom-call(f32[32,16,128]{2,1,0:T(8,128)S(1)} %all_to_all.61.recv_ref, f32[8,128]{1,0:T(8,128)S(1)} %get-tuple-element.103.cm_ref, f32[8,128]{1,0:T(8,128)S(1)} %broadcast_7_refs_6__gprev_ref.2.refs_6_.gprev_ref, ...), custom_call_target="tpu_custom_call" | custom-call | tf_op jit(solution)/shard_map/rows0/pallas_call | solution.py:395
  191.0 86.4 %cols1.1 = (f32[32,128]{1,0:T(8,128)S(1)}, f32[8,128]{1,0:T(8,128)S(1)}, f32[16,128]{1,0:T(8,128)S(1)}, f32[32,8,128]{2,1,0:T(8,128)S(1)}) custom-call(f32[32,128]{1,0:T(8,128)S(1)} %multiply_add_fusion.8.refs_0_, f32[32,128]{1,0:T(8,128)S(1)} %collective-permute-done.2.refs_1_, f32[32,128]{1,0:T(8,128)S(1)} %bitcast.8, ...), custom_call_target="tpu_custom_call" | custom-call | tf_op jit(solution)/shard_map/cols1/pallas_call | solution.py:395
  277.4 13.0 all_to_all.62.recv_ref
  290.3 54.4 %rows1.1 = (f32[8,128]{1,0:T(8,128)S(1)}, f32[8,128]{1,0:T(8,128)S(1)}, f32[16,128]{1,0:T(8,128)S(1)}, f32[32,128]{1,0:T(8,128)S(1)}) custom-call(f32[32,8,128]{2,1,0:T(8,128)S(1)} %all_to_all.62.recv_ref, f32[8,128]{1,0:T(8,128)S(1)} %get-tuple-element.103.cm_ref, f32[8,128]{1,0:T(8,128)S(1)} %get-tuple-element.110.gprev_ref, ...), custom_call_target="tpu_custom_call" | custom-call | tf_op jit(solution)/shard_map/rows1/pallas_call | solution.py:395
  351.4 86.4 %cols2.1 = (f32[32,128]{1,0:T(8,128)S(1)}, f32[8,128]{1,0:T(8,128)S(1)}, f32[16,128]{1,0:T(8,128)S(1)}, f32[32,8,128]{2,1,0:T(8,128)S(1)}) custom-call(f32[32,128]{1,0:T(8,128)S(1)} %multiply_add_fusion.7.refs_0_, f32[32,128]{1,0:T(8,128)S(1)} %collective-permute-done.4.refs_1_, f32[32,128]{1,0:T(8,128)S(1)} %bitcast.9, ...), custom_call_target="tpu_custom_call" | custom-call | tf_op jit(solution)/shard_map/cols2/pallas_call | solution.py:395
  437.8 12.4 all_to_all.63.recv_ref
  450.1 54.4 %rows2.1 = (f32[8,128]{1,0:T(8,128)S(1)}, f32[8,128]{1,0:T(8,128)S(1)}, f32[16,128]{1,0:T(8,128)S(1)}, f32[32,128]{1,0:T(8,128)S(1)}) custom-call(f32[32,8,128]{2,1,0:T(8,128)S(1)} %all_to_all.63.recv_ref, f32[8,128]{1,0:T(8,128)S(1)} %get-tuple-element.103.cm_ref, f32[8,128]{1,0:T(8,128)S(1)} %get-tuple-element.118.gprev_ref, ...), custom_call_target="tpu_custom_call" | custom-call | tf_op jit(solution)/shard_map/rows2/pallas_call | solution.py:395
  511.1 86.4 %cols3.1 = (f32[32,128]{1,0:T(8,128)S(1)}, f32[8,128]{1,0:T(8,128)S(1)}, f32[16,128]{1,0:T(8,128)S(1)}, f32[32,8,128]{2,1,0:T(8,128)S(1)}) custom-call(f32[32,128]{1,0:T(8,128)S(1)} %multiply_add_fusion.6.refs_0_, f32[32,128]{1,0:T(8,128)S(1)} %collective-permute-done.6.refs_1_, f32[32,128]{1,0:T(8,128)S(1)} %bitcast.10, ...), custom_call_target="tpu_custom_call" | custom-call | tf_op jit(solution)/shard_map/cols3/pallas_call | solution.py:395
  609.8 54.3 %rows3.1 = (f32[8,128]{1,0:T(8,128)S(1)}, f32[8,128]{1,0:T(8,128)S(1)}, f32[16,128]{1,0:T(8,128)S(1)}, f32[32,128]{1,0:T(8,128)S(1)}) custom-call(f32[32,8,128]{2,1,0:T(8,128)S(1)} %all_to_all.64.recv_ref, f32[8,128]{1,0:T(8,128)S(1)} %get-tuple-element.103.cm_ref, f32[8,128]{1,0:T(8,128)S(1)} %get-tuple-element.126.gprev_ref, ...), custom_call_target="tpu_custom_call" | custom-call | tf_op jit(solution)/shard_map/rows3/pallas_call | solution.py:395
  670.8 86.4 %cols4.1 = (f32[32,128]{1,0:T(8,128)S(1)}, f32[8,128]{1,0:T(8,128)S(1)}, f32[16,128]{1,0:T(8,128)S(1)}, f32[32,8,128]{2,1,0:T(8,128)S(1)}) custom-call(f32[32,128]{1,0:T(8,128)S(1)} %multiply_add_fusion.5.refs_0_, f32[32,128]{1,0:T(8,128)S(1)} %collective-permute-done.8.refs_1_, f32[32,128]{1,0:T(8,128)S(1)} %bitcast.11, ...), custom_call_target="tpu_custom_call" | custom-call | tf_op jit(solution)/shard_map/cols4/pallas_call | solution.py:395
  769.6 54.4 %rows4.1 = (f32[8,128]{1,0:T(8,128)S(1)}, f32[8,128]{1,0:T(8,128)S(1)}, f32[16,128]{1,0:T(8,128)S(1)}, f32[32,128]{1,0:T(8,128)S(1)}) custom-call(f32[32,8,128]{2,1,0:T(8,128)S(1)} %all_to_all.65.recv_ref, f32[8,128]{1,0:T(8,128)S(1)} %get-tuple-element.103.cm_ref, f32[8,128]{1,0:T(8,128)S(1)} %get-tuple-element.134.gprev_ref, ...), custom_call_target="tpu_custom_call" | custom-call | tf_op jit(solution)/shard_map/rows4/pallas_call | solution.py:395
  830.4 86.4 %cols5.1 = (f32[32,128]{1,0:T(8,128)S(1)}, f32[8,128]{1,0:T(8,128)S(1)}, f32[16,128]{1,0:T(8,128)S(1)}, f32[32,8,128]{2,1,0:T(8,128)S(1)}) custom-call(f32[32,128]{1,0:T(8,128)S(1)} %multiply_add_fusion.4.refs_0_, f32[32,128]{1,0:T(8,128)S(1)} %collective-permute-done.10.refs_1_, f32[32,128]{1,0:T(8,128)S(1)} %bitcast.12, ...), custom_call_target="tpu_custom_call" | custom-call | tf_op jit(solution)/shard_map/cols5/pallas_call | solution.py:395
  929.1 54.4 %rows5.1 = (f32[8,128]{1,0:T(8,128)S(1)}, f32[8,128]{1,0:T(8,128)S(1)}, f32[16,128]{1,0:T(8,128)S(1)}, f32[32,128]{1,0:T(8,128)S(1)}) custom-call(f32[32,8,128]{2,1,0:T(8,128)S(1)} %all_to_all.66.recv_ref, f32[8,128]{1,0:T(8,128)S(1)} %get-tuple-element.103.cm_ref, f32[8,128]{1,0:T(8,128)S(1)} %get-tuple-element.142.gprev_ref, ...), custom_call_target="tpu_custom_call" | custom-call | tf_op jit(solution)/shard_map/rows5/pallas_call | solution.py:395
  990.2 86.4 %cols6.1 = (f32[32,128]{1,0:T(8,128)S(1)}, f32[8,128]{1,0:T(8,128)S(1)}, f32[16,128]{1,0:T(8,128)S(1)}, f32[32,8,128]{2,1,0:T(8,128)S(1)}) custom-call(f32[32,128]{1,0:T(8,128)S(1)} %multiply_add_fusion.3.refs_0_, f32[32,128]{1,0:T(8,128)S(1)} %collective-permute-done.12.refs_1_, f32[32,128]{1,0:T(8,128)S(1)} %bitcast.13, ...), custom_call_target="tpu_custom_call" | custom-call | tf_op jit(solution)/shard_map/cols6/pallas_call | solution.py:395
  1076.5 12.4 all_to_all.67.recv_ref
  1088.9 54.4 %rows6.1 = (f32[8,128]{1,0:T(8,128)S(1)}, f32[8,128]{1,0:T(8,128)S(1)}, f32[16,128]{1,0:T(8,128)S(1)}, f32[32,128]{1,0:T(8,128)S(1)}) custom-call(f32[32,8,128]{2,1,0:T(8,128)S(1)} %all_to_all.67.recv_ref, f32[8,128]{1,0:T(8,128)S(1)} %get-tuple-element.103.cm_ref, f32[8,128]{1,0:T(8,128)S(1)} %get-tuple-element.150.gprev_ref, ...), custom_call_target="tpu_custom_call" | custom-call | tf_op jit(solution)/shard_map/rows6/pallas_call | solution.py:395
  1149.9 86.4 %cols7.1 = (f32[32,128]{1,0:T(8,128)S(1)}, f32[8,128]{1,0:T(8,128)S(1)}, f32[16,128]{1,0:T(8,128)S(1)}, f32[32,8,128]{2,1,0:T(8,128)S(1)}) custom-call(f32[32,128]{1,0:T(8,128)S(1)} %multiply_add_fusion.2.refs_0_, f32[32,128]{1,0:T(8,128)S(1)} %collective-permute-done.14.refs_1_, f32[32,128]{1,0:T(8,128)S(1)} %bitcast.14, ...), custom_call_target="tpu_custom_call" | custom-call | tf_op jit(solution)/shard_map/cols7/pallas_call | solution.py:395
  1248.6 54.4 %rows7.1 = (f32[8,128]{1,0:T(8,128)S(1)}, f32[8,128]{1,0:T(8,128)S(1)}, f32[16,128]{1,0:T(8,128)S(1)}, f32[32,128]{1,0:T(8,128)S(1)}) custom-call(f32[32,8,128]{2,1,0:T(8,128)S(1)} %all_to_all.68.recv_ref, f32[8,128]{1,0:T(8,128)S(1)} %get-tuple-element.103.cm_ref, f32[8,128]{1,0:T(8,128)S(1)} %get-tuple-element.158.gprev_ref, ...), custom_call_target="tpu_custom_call" | custom-call | tf_op jit(solution)/shard_map/rows7/pallas_call | solution.py:395
  1309.7 86.4 %cols8.1 = (f32[32,128]{1,0:T(8,128)S(1)}, f32[8,128]{1,0:T(8,128)S(1)}, f32[16,128]{1,0:T(8,128)S(1)}, f32[32,8,128]{2,1,0:T(8,128)S(1)}) custom-call(f32[32,128]{1,0:T(8,128)S(1)} %multiply_add_fusion.1.refs_0_, f32[32,128]{1,0:T(8,128)S(1)} %collective-permute-done.16.refs_1_, f32[32,128]{1,0:T(8,128)S(1)} %bitcast.15, ...), custom_call_target="tpu_custom_call" | custom-call | tf_op jit(solution)/shard_map/cols8/pallas_call | solution.py:395
  1408.5 54.2 %rows8.1 = (f32[8,128]{1,0:T(8,128)S(1)}, f32[8,128]{1,0:T(8,128)S(1)}, f32[16,128]{1,0:T(8,128)S(1)}, f32[32,128]{1,0:T(8,128)S(1)}) custom-call(f32[32,8,128]{2,1,0:T(8,128)S(1)} %all_to_all.69.recv_ref, f32[8,128]{1,0:T(8,128)S(1)} %get-tuple-element.103.cm_ref, f32[8,128]{1,0:T(8,128)S(1)} %get-tuple-element.166.gprev_ref, ...), custom_call_target="tpu_custom_call" | custom-call | tf_op jit(solution)/shard_map/rows8/pallas_call | solution.py:395
  1469.1 87.0 %cols9.1 = (f32[32,128]{1,0:T(8,128)}, f32[8,128]{1,0:T(8,128)S(1)}, f32[16,128]{1,0:T(8,128)}, f32[32,16,128]{2,1,0:T(8,128)S(1)}) custom-call(f32[32,128]{1,0:T(8,128)S(1)} %multiply_add_fusion.refs_0_, f32[32,128]{1,0:T(8,128)S(1)} %collective-permute-done.18.refs_1_, f32[32,128]{1,0:T(8,128)S(1)} %bitcast.16, f32[32,128]{1,0:T(8,128)S(1)} %get-tuple-element.170.refs_3_, ...), custom_call_target="tpu_custom_call" | custom-call | tf_op jit(solution)/shard_map/cols9/pallas_call | solution.py:395
  1556.1 13.4 all_to_all.70.recv_ref
  (71 shorter events, 156.0 us)
Async XLA Ops:
  0.6 1.2 copy-start
  1.9 0.9 copy-start.2
  2.8 0.7 copy-start.3
  6.6 13.4 collective-permute-start
  22.0 0.7 copy-start.1
  184.8 3.5 collective-permute-start.1
  188.3 2.7 collective-permute-start.2
  344.7 4.0 collective-permute-start.3
  348.7 2.7 collective-permute-start.4
  504.5 3.7 collective-permute-start.5
  508.3 2.9 collective-permute-start.6
  664.1 4.0 collective-permute-start.7
  668.2 2.7 collective-permute-start.8
  824.0 3.7 collective-permute-start.9
  827.7 2.7 collective-permute-start.10
  983.5 4.0 collective-permute-start.11
  987.5 2.7 collective-permute-start.12
  1143.3 3.7 collective-permute-start.13
  1147.0 2.9 collective-permute-start.14
  1303.0 4.0 collective-permute-start.15
  1307.0 2.7 collective-permute-start.16
  1462.7 3.7 collective-permute-start.17
  1466.4 2.7 collective-permute-start.18
